TPU v7x, 32 devices: a whole 2x2x4 slice. The times are simulated.
32 devices in a mesh: dp: 16 (over z, y, core), cp: 2 (over x).
Axes of the slice: x: 2, y: 2, z: 4, core: 2. Of those that a mesh axis runs over, the one named last changes fastest.
Arguments:
- x_source: bfloat16 [16, 1024, 768], P(None, ('cp', 'dp')), may hold values from -6 to 6
- cotangent: bfloat16 [16, 1024, 768], P('dp', 'cp'), may hold values from -6 to 6
- lengths: int32 [16], replicated, may hold values from 1 to 1024, 10240 in all
- dealing: int32 [16], replicated, may hold values from 0 to 15, each once
- qkv_weight: float32 [768, 2304], P('cp', 'dp'), may hold values from -0.21875 to 0.21875
- proj_weight: float32 [768, 768], P('cp', 'dp'), may hold values from -2 to 2
- up_weight: float32 [768, 3072], P('cp', 'dp'), may hold values from -0.21875 to 0.21875
- down_weight: float32 [3072, 768], P('cp', 'dp'), may hold values from -0.109375 to 0.109375
- first_gain: float32 [768], P('dp'), may hold values from 0.1 to 1.9
- first_shift: float32 [768], P('dp'), may hold values from -1.75 to 1.75
- proj_bias: float32 [768], P('dp'), may hold values from -1.75 to 1.75
- second_gain: float32 [768], P('dp'), may hold values from 0.1 to 1.9
- second_shift: float32 [768], P('dp'), may hold values from -1.75 to 1.75
- up_bias: float32 [3072], P('dp'), may hold values from -3 to 3
- down_bias: float32 [768], P('dp'), may hold values from -1.75 to 1.75
Outputs:
- output: bfloat16 [16, 1024, 768], P('dp', 'cp')
- input_grad: bfloat16 [16, 1024, 768], P(None, ('cp', 'dp'))
- qkv_grad: float32 [768, 2304], P('cp', 'dp')
- proj_grad: float32 [768, 768], P('cp', 'dp')
- up_grad: float32 [768, 3072], P('cp', 'dp')
- down_grad: float32 [3072, 768], P('cp', 'dp')
- first_gain_grad: float32 [768], P('dp')
- first_shift_grad: float32 [768], P('dp')
- proj_bias_grad: float32 [768], P('dp')
- second_gain_grad: float32 [768], P('dp')
- second_shift_grad: float32 [768], P('dp')
- up_bias_grad: float32 [3072], P('dp')
- down_bias_grad: float32 [768], P('dp')
Inputs may be any that keep to these rules, and one draw needn't show every extreme that they name: The lengths sum to 10240 and the longest is exactly 1024. `dealing`: a permutation of the sequence numbers.
All inputs are finite; a program needn't handle non-finite values.
Results may differ from a plain program's by a relative error of at most 0.019.
Values may be sent and summed in bfloat16 or wider, within the bound.
A program may use at most 192 MiB of HBM per device.

v0:
```python
import math

import jax
import jax.numpy as jnp
from jax import lax
from jax.sharding import PartitionSpec as P

HEADS = 12
HEAD_DIM = 64


EPSILON = 1e-05
NEG_BIG = -1e30
TANH_SCALE = 0.7978845608028654
CUBIC_TERM = 0.044715


def layer_norm(values, scaling, offset):
    centered = values - jnp.mean(values, axis=-1, keepdims=True)
    spread = jnp.mean(centered * centered, axis=-1, keepdims=True)
    return centered * lax.rsqrt(spread + EPSILON) * scaling + offset


def gelu_tanh(values):
    return (
        0.5
        * values
        * (1.0 + jnp.tanh(TANH_SCALE * (values + CUBIC_TERM * values * values * values)))
    )


def grouped(array, block_seqs):
    return array.reshape(
        (array.shape[0] // block_seqs, block_seqs, array.shape[1], HEADS, array.shape[2] // HEADS)
    )


def grouped_stats(array, block_seqs):
    return array.reshape((array.shape[0] // block_seqs, block_seqs) + array.shape[1:])


def joined(array):
    return array.reshape(
        (array.shape[0] * array.shape[1], array.shape[2], array.shape[3] * array.shape[4])
    )


def masked_scores(queries, key_rows, query_start, score_scale):
    scores = (
        jnp.einsum("bqhd,bkhd->bhqk", queries, key_rows, preferred_element_type=jnp.float32)
        * score_scale
    )
    query_pos = query_start + jnp.arange(queries.shape[1])
    key_pos = jnp.arange(key_rows.shape[1])
    return jnp.where(key_pos[None, :] <= query_pos[:, None], scores, NEG_BIG)


def attend(inputs, query_start, score_scale):
    queries, key_rows, val_rows = inputs
    scores = masked_scores(queries, key_rows, query_start, score_scale)
    row_top = jnp.max(scores, axis=-1, keepdims=True)
    exponent = jnp.exp(scores - row_top)
    totals = jnp.sum(exponent, axis=-1, keepdims=True)
    weights = (exponent / totals).astype(jnp.bfloat16)
    attended = jnp.einsum("bhqk,bkhd->bqhd", weights, val_rows, preferred_element_type=jnp.float32)
    return (attended.astype(jnp.bfloat16), (row_top + jnp.log(totals))[..., 0])


def rows_back(inputs, query_start, score_scale):
    queries, key_rows, val_rows, grad_rows, log_total = inputs
    scores = masked_scores(queries, key_rows, query_start, score_scale)
    weights = jnp.exp(scores - log_total[..., None])
    grad_weights = jnp.einsum(
        "bqhd,bkhd->bhqk", grad_rows, val_rows, preferred_element_type=jnp.float32
    )
    delta_rows = jnp.sum(weights * grad_weights, axis=-1)
    grad_scores = (weights * (grad_weights - delta_rows[..., None])).astype(jnp.bfloat16)
    grad_query = (
        jnp.einsum("bhqk,bkhd->bqhd", grad_scores, key_rows, preferred_element_type=jnp.float32)
        * score_scale
    )
    grad_keys = (
        jnp.einsum("bhqk,bqhd->bkhd", grad_scores, queries, preferred_element_type=jnp.float32)
        * score_scale
    )
    grad_vals = jnp.einsum(
        "bhqk,bqhd->bkhd",
        weights.astype(jnp.bfloat16),
        grad_rows,
        preferred_element_type=jnp.float32,
    )
    return (grad_query, grad_keys, grad_vals)


def fetch_weights(
    qkv_weight,
    proj_weight,
    up_weight,
    down_weight,
    first_gain,
    first_shift,
    proj_bias,
    second_gain,
    second_shift,
    up_bias,
    down_bias,
):
    qkv_part, proj_part, up_part, down_part = (
        lax.all_gather(qkv_weight.astype(jnp.bfloat16), "cp", axis=0, tiled=True),
        lax.all_gather(proj_weight.astype(jnp.bfloat16), "cp", axis=0, tiled=True),
        lax.all_gather(up_weight.astype(jnp.bfloat16), "cp", axis=0, tiled=True),
        lax.all_gather(down_weight.astype(jnp.bfloat16), "cp", axis=0, tiled=True),
    )
    return (
        lax.all_gather(qkv_part, "dp", axis=1, tiled=True),
        lax.all_gather(proj_part, "dp", axis=1, tiled=True),
        lax.all_gather(up_part, "dp", axis=1, tiled=True),
        lax.all_gather(down_part, "dp", axis=1, tiled=True),
        lax.all_gather(first_gain.astype(jnp.bfloat16), "dp", axis=0, tiled=True),
        lax.all_gather(first_shift.astype(jnp.bfloat16), "dp", axis=0, tiled=True),
        lax.all_gather(proj_bias.astype(jnp.bfloat16), "dp", axis=0, tiled=True),
        lax.all_gather(second_gain.astype(jnp.bfloat16), "dp", axis=0, tiled=True),
        lax.all_gather(second_shift.astype(jnp.bfloat16), "dp", axis=0, tiled=True),
        lax.all_gather(up_bias.astype(jnp.bfloat16), "dp", axis=0, tiled=True),
        lax.all_gather(down_bias.astype(jnp.bfloat16), "dp", axis=0, tiled=True),
    )


def mat_rows(left, right):
    return jnp.einsum("sqd,de->sqe", left, right, preferred_element_type=jnp.float32)


def mat_back(left, right):
    return jnp.einsum("sqe,de->sqd", left, right, preferred_element_type=jnp.float32)


def mat_grad(left, right):
    return jnp.einsum("sqd,sqe->de", left, right, preferred_element_type=jnp.float32)


def local(
    x_source,
    cotangent,
    lengths,
    dealing,
    qkv_weight,
    proj_weight,
    up_weight,
    down_weight,
    first_gain,
    first_shift,
    proj_bias,
    second_gain,
    second_shift,
    up_bias,
    down_bias,
):
    groups = lax.axis_size("dp")
    seqs_all, piece_rows, features = x_source.shape
    seq_group = seqs_all // groups
    span_rows = groups * piece_rows
    score_scale = HEAD_DIM ** (-0.5)
    block_seqs = math.gcd(seq_group, max(1, 512 // span_rows))
    owners = jnp.argsort(dealing)
    send_order = owners.reshape(groups, seq_group).T.reshape(-1)
    outgoing = x_source[send_order].reshape(seq_group, span_rows, features)
    arrived = lax.all_to_all(outgoing, "dp", split_axis=1, concat_axis=1, tiled=True)
    first_slot = lax.axis_index("dp") * seq_group
    my_lengths = lax.dynamic_slice_in_dim(lengths[owners], first_slot, seq_group)
    query_start = lax.axis_index("cp") * span_rows
    positions = query_start + jnp.arange(span_rows)
    live_rows = positions[None, :] < my_lengths[:, None]
    fetched = fetch_weights(
        qkv_weight,
        proj_weight,
        up_weight,
        down_weight,
        first_gain,
        first_shift,
        proj_bias,
        second_gain,
        second_shift,
        up_bias,
        down_bias,
    )
    qkv_full, proj_full, up_full, down_full = (fetched[0], fetched[1], fetched[2], fetched[3])
    gain_one, shift_one, bias_proj, gain_two, shift_two, bias_up, bias_down = [
        vector.astype(jnp.float32) for vector in fetched[4:]
    ]
    inputs_f = arrived.astype(jnp.float32)
    norm_one, back_one = jax.vjp(layer_norm, inputs_f, gain_one, shift_one)
    act_one = norm_one.astype(jnp.bfloat16)
    mixed_rows = mat_rows(act_one, qkv_full).astype(jnp.bfloat16)
    queries = mixed_rows[..., :features]
    kv_local = mixed_rows[..., features:]
    kv_all = lax.all_gather(kv_local, "cp", axis=1, tiled=True)
    attended, log_total = lax.map(
        lambda inputs: attend(inputs, query_start, score_scale),
        (
            grouped(queries, block_seqs),
            grouped(kv_all[..., :features], block_seqs),
            grouped(kv_all[..., features:], block_seqs),
        ),
    )
    attended = joined(attended)
    log_total = log_total.reshape((seq_group,) + log_total.shape[2:])
    residual = inputs_f + mat_rows(attended, proj_full) + bias_proj
    norm_two, back_two = jax.vjp(layer_norm, residual, gain_two, shift_two)
    act_two = norm_two.astype(jnp.bfloat16)
    up_raw = mat_rows(act_two, up_full) + bias_up
    hidden, back_gelu = jax.vjp(gelu_tanh, up_raw)
    hid_low = hidden.astype(jnp.bfloat16)
    result = residual + mat_rows(hid_low, down_full) + bias_down
    output = jnp.where(live_rows[..., None], result, 0.0).astype(jnp.bfloat16)
    fetched = fetch_weights(
        qkv_weight,
        proj_weight,
        up_weight,
        down_weight,
        first_gain,
        first_shift,
        proj_bias,
        second_gain,
        second_shift,
        up_bias,
        down_bias,
    )
    qkv_full, proj_full, up_full, down_full = (fetched[0], fetched[1], fetched[2], fetched[3])
    gain_one, gain_two = (fetched[4].astype(jnp.float32), fetched[7].astype(jnp.float32))
    grad_out = jnp.where(live_rows[..., None], cotangent.astype(jnp.float32), 0.0)
    grad_low = grad_out.astype(jnp.bfloat16)
    grad_down = mat_grad(hid_low, grad_low)
    grad_bias_down = jnp.sum(grad_out, axis=(0, 1))
    grad_hidden = mat_back(grad_low, down_full)
    grad_up_raw = back_gelu(grad_hidden)[0].astype(jnp.bfloat16)
    grad_up = mat_grad(act_two, grad_up_raw)
    grad_bias_up = jnp.sum(grad_up_raw.astype(jnp.float32), axis=(0, 1))
    grad_act_two = mat_back(grad_up_raw, up_full)
    grad_resid, grad_gain_two, grad_shift_two = back_two(grad_act_two)
    grad_resid = grad_resid + grad_out
    grad_bias_proj = jnp.sum(grad_resid, axis=(0, 1))
    resid_low = grad_resid.astype(jnp.bfloat16)
    grad_proj = mat_grad(attended, resid_low)
    grad_attended = mat_back(resid_low, proj_full).astype(jnp.bfloat16)
    kv_back = lax.all_gather(kv_local, "cp", axis=1, tiled=True)
    key_rows = kv_back[..., :features]
    val_rows = kv_back[..., features:]
    grad_query, grad_keys, grad_vals = lax.map(
        lambda inputs: rows_back(inputs, query_start, score_scale),
        (
            grouped(queries, block_seqs),
            grouped(key_rows, block_seqs),
            grouped(val_rows, block_seqs),
            grouped(grad_attended, block_seqs),
            grouped_stats(log_total, block_seqs),
        ),
    )
    grad_keys, grad_vals = (
        lax.psum_scatter(
            joined(grad_keys).astype(jnp.bfloat16), "cp", scatter_dimension=1, tiled=True
        ).astype(jnp.float32),
        lax.psum_scatter(
            joined(grad_vals).astype(jnp.bfloat16), "cp", scatter_dimension=1, tiled=True
        ).astype(jnp.float32),
    )
    grad_mixed = jnp.concatenate([joined(grad_query), grad_keys, grad_vals], axis=-1).astype(
        jnp.bfloat16
    )
    grad_qkv = mat_grad(act_one, grad_mixed)
    grad_act_one = mat_back(grad_mixed, qkv_full)
    grad_input, grad_gain_one, grad_shift_one = back_one(grad_act_one)
    grad_input = (grad_input + grad_resid).astype(jnp.bfloat16)
    returned = lax.all_to_all(grad_input, "dp", split_axis=1, concat_axis=0, tiled=True)
    input_grad = returned[dealing]
    (
        grad_qkv,
        grad_proj,
        grad_up,
        grad_down,
        grad_gain_one,
        grad_shift_one,
        grad_bias_proj,
        grad_gain_two,
        grad_shift_two,
        grad_bias_up,
        grad_bias_down,
    ) = (
        lax.psum_scatter(
            grad_qkv.astype(jnp.bfloat16), "dp", scatter_dimension=1, tiled=True
        ).astype(jnp.float32),
        lax.psum_scatter(
            grad_proj.astype(jnp.bfloat16), "dp", scatter_dimension=1, tiled=True
        ).astype(jnp.float32),
        lax.psum_scatter(
            grad_up.astype(jnp.bfloat16), "dp", scatter_dimension=1, tiled=True
        ).astype(jnp.float32),
        lax.psum_scatter(
            grad_down.astype(jnp.bfloat16), "dp", scatter_dimension=1, tiled=True
        ).astype(jnp.float32),
        lax.psum_scatter(
            grad_gain_one.astype(jnp.bfloat16), "dp", scatter_dimension=0, tiled=True
        ).astype(jnp.float32),
        lax.psum_scatter(
            grad_shift_one.astype(jnp.bfloat16), "dp", scatter_dimension=0, tiled=True
        ).astype(jnp.float32),
        lax.psum_scatter(
            grad_bias_proj.astype(jnp.bfloat16), "dp", scatter_dimension=0, tiled=True
        ).astype(jnp.float32),
        lax.psum_scatter(
            grad_gain_two.astype(jnp.bfloat16), "dp", scatter_dimension=0, tiled=True
        ).astype(jnp.float32),
        lax.psum_scatter(
            grad_shift_two.astype(jnp.bfloat16), "dp", scatter_dimension=0, tiled=True
        ).astype(jnp.float32),
        lax.psum_scatter(
            grad_bias_up.astype(jnp.bfloat16), "dp", scatter_dimension=0, tiled=True
        ).astype(jnp.float32),
        lax.psum_scatter(
            grad_bias_down.astype(jnp.bfloat16), "dp", scatter_dimension=0, tiled=True
        ).astype(jnp.float32),
    )
    grad_qkv, grad_proj, grad_up, grad_down = (
        lax.psum_scatter(
            grad_qkv.astype(jnp.bfloat16), "cp", scatter_dimension=0, tiled=True
        ).astype(jnp.float32),
        lax.psum_scatter(
            grad_proj.astype(jnp.bfloat16), "cp", scatter_dimension=0, tiled=True
        ).astype(jnp.float32),
        lax.psum_scatter(
            grad_up.astype(jnp.bfloat16), "cp", scatter_dimension=0, tiled=True
        ).astype(jnp.float32),
        lax.psum_scatter(
            grad_down.astype(jnp.bfloat16), "cp", scatter_dimension=0, tiled=True
        ).astype(jnp.float32),
    )
    (
        grad_gain_one,
        grad_shift_one,
        grad_bias_proj,
        grad_gain_two,
        grad_shift_two,
        grad_bias_up,
        grad_bias_down,
    ) = lax.psum(
        (
            grad_gain_one,
            grad_shift_one,
            grad_bias_proj,
            grad_gain_two,
            grad_shift_two,
            grad_bias_up,
            grad_bias_down,
        ),
        "cp",
    )
    return (
        output,
        input_grad,
        grad_qkv,
        grad_proj,
        grad_up,
        grad_down,
        grad_gain_one,
        grad_shift_one,
        grad_bias_proj,
        grad_gain_two,
        grad_shift_two,
        grad_bias_up,
        grad_bias_down,
    )


def solution(mesh):
    in_specs = (
        P(None, ("cp", "dp"), None),
        P("dp", "cp", None),
        P(),
        P(),
        P("cp", "dp"),
        P("cp", "dp"),
        P("cp", "dp"),
        P("cp", "dp"),
        P("dp"),
        P("dp"),
        P("dp"),
        P("dp"),
        P("dp"),
        P("dp"),
        P("dp"),
    )
    out_specs = (
        P("dp", "cp", None),
        P(None, ("cp", "dp"), None),
        P("cp", "dp"),
        P("cp", "dp"),
        P("cp", "dp"),
        P("cp", "dp"),
        P("dp"),
        P("dp"),
        P("dp"),
        P("dp"),
        P("dp"),
        P("dp"),
        P("dp"),
    )
    return jax.shard_map(local, mesh=mesh, in_specs=in_specs, out_specs=out_specs, check_vma=False)
```

profile of v0, /device:TPU:0, one launch (start us, length us, event | category | flops | bytes accessed | tf_op | source)
XLA Modules:
  0.0 742.8 jit_solution(12308336290372131124)
XLA Ops:
  8.3 6.8 all_gather.59
  19.4 5.5 reduce.22
  25.9 6.2 all-to-all-start
  35.5 69.3 %all-reduce.16 = (bf16[768]{0:T(1024)(128)(2,1)S(1)}, bf16[768]{0:T(1024)(128)(2,1)S(1)}, bf16[768]{0:T(1024)(128)(2,1)S(1)}, bf16[768]{0:T(1024)(128)(2,1)S(1)}...) all-reduce(bf16[768]{0:T(1024)(128)(2,1)S(1)} %dynamic-update-slice, ...), channel_id=1, replica_groups=mesh['dp'=16,'cp'=2] {'dp'}, use_global_device_ids=true, to_apply=%add.1 | all-reduce | flops 6912 | bytes 27648
  113.3 5.1 all_gather.62
  118.6 9.8 %all_gather.67 = bf16[768,192]{0,1:T(8,128)(2,1)} all-gather(bf16[384,192]{0,1:T(8,128)(2,1)S(1)} %convert_element_type.266), channel_id=1, replica_groups=mesh['dp'=16,'cp'=2] {'cp'}, dimensions={0}, use_global_device_ids=true | all-gather | bytes 442368 | tf_op jit(solution)/shard_map/all_gather | solution.py:111
  128.5 9.1 %all_gather.70 = bf16[3072,48]{0,1:T(8,128)(2,1)} all-gather(bf16[1536,48]{0,1:T(8,128)(2,1)S(1)} %convert_element_type.270), channel_id=1, replica_groups=mesh['dp'=16,'cp'=2] {'cp'}, dimensions={0}, use_global_device_ids=true | all-gather | bytes 442368 | tf_op jit(solution)/shard_map/all_gather | solution.py:112
  141.1 19.5 %all-gather.8.cloned.1.call-done = bf16[1,1024,1536]{2,1,0:T(8,128)(2,1)} async-done(((bf16[1,512,1536]{2,1,0:T(8,128)(2,1)}), bf16[1,1024,1536]{2,1,0:T(8,128)(2,1)}) %all-gather.8.cloned.1.call-update) | async-done | bytes 3145744 | tf_op jit(solution)/shard_map/all_gather | solution.py:196
  169.3 12.1 %fusion.6 = (f32[12,512]{1,0:T(8,128)S(1)}, f32[12,512,1024]{2,1,0:T(8,128)}) fusion(pred[512,1024]{1,0:T(8,128)(4,1)S(1)} %iota_compare_fusion, bf16[512,12,64]{0,2,1:T(8,128)(2,1)} %bitcast.121, bf16[1024,12,64]{0,2,1:T(8,128)(2,1)S(1)} %bitcast.119), kind=kOutput, calls=%fused_computation.18 | convolution fusion | flops 824174592 | bytes 28073984 | tf_op jit(solution)/shard_map/while/body/eval_jaxpr/bqhd,bkhd->bhqk/dot_general | solution.py:50
  181.4 12.5 %fusion = f32[12,512]{1,0:T(8,128)S(1)} fusion(f32[12,512]{1,0:T(8,128)S(1)} %get-tuple-element.102, f32[12,512,1024]{2,1,0:T(8,128)} %get-tuple-element.103, pred[512,1024]{1,0:T(8,128)(4,1)S(1)} %iota_compare_fusion), kind=kLoop, calls=%fused_computation.9 | loop fusion | flops 25159680 | bytes 25739264 | tf_op jit(solution)/shard_map/while/body/eval_jaxpr/reduce_sum | solution.py:63
  197.0 8.5 %fusion.36 = bf16[12,64,512]{2,1,0:T(8,128)(2,1)} fusion(bf16[1024,12,64]{0,2,1:T(8,128)(2,1)S(1)} %bitcast.124, f32[12,512]{1,0:T(8,128)S(1)} %fusion, f32[12,512]{1,0:T(8,128)S(1)} %get-tuple-element.102, f32[12,512,1024]{2,1,0:T(8,128)S(1)} %copy-done.3, pred[512,1024]{1,0:T(8,128)(4,1)S(1)} %iota_compare_fusion), kind=kOutput, calls=%fused_computation.70 | convolution fusion | flops 837156864 | bytes 28098560 | tf_op jit(solution)/shard_map/while/body/eval_jaxpr/bhqk,bkhd->bqhd/dot_general | solution.py:65
  208.3 46.6 %all-gather.12.cloned.1.call-done = bf16[768,3072]{0,1:T(8,128)(2,1)} async-done(((bf16[768,192]{0,1:T(8,128)(2,1)}), bf16[768,3072]{0,1:T(8,128)(2,1)}) %all-gather.12.cloned.1.call-update) | async-done | bytes 4718608 | tf_op jit(solution)/shard_map/all_gather | solution.py:117
  254.9 7.0 fusion.64
  262.0 47.1 %all-gather.14.cloned.1.call-done = bf16[3072,768]{0,1:T(8,128)(2,1)} async-done(((bf16[3072,48]{0,1:T(8,128)(2,1)}), bf16[3072,768]{0,1:T(8,128)(2,1)}) %all-gather.14.cloned.1.call-update) | async-done | bytes 4718608 | tf_op jit(solution)/shard_map/all_gather | solution.py:118
  309.0 11.8 %fusion.71 = (bf16[3072]{0:T(1024)(128)(2,1)S(1)}, bf16[512,3072]{1,0:T(8,128)(2,1)S(1)}) fusion(bf16[3072,768]{0,1:T(8,128)(2,1)} %all-gather.14.cloned.1.call-done, bf16[1,512,768]{2,1,0:T(8,128)(2,1)} %param.16, pred[512]{0:T(512)(128)(4,1)S(1)} %broadcast_compare_fusion, f32[512,3072]{1,0:T(8,128)} %fusion.64, f32[3072]{0:T(1024)S(1)} %convert_element_type.268), kind=kOutput, calls=%fused_computation.119 | convolution fusion | flops 2457990144 | bytes 14961152 | tf_op jit(solution)/shard_map/sqe,de->sqd/dot_general | solution.py:134
  334.1 17.9 %multiply_reduce_fusion = (f32[12,512]{1,0:T(8,128)S(1)}, f32[12,512,1024]{2,1,0:T(8,128)}) fusion(f32[12,512]{1,0:T(8,128)S(1)} %log_add_fusion, f32[12,512,1024]{2,1,0:T(8,128)} %get-tuple-element.103, pred[512,1024]{1,0:T(8,128)(4,1)S(1)} %iota_compare_fusion, bf16[512,12,64]{0,2,1:T(8,128)(2,1)} %bitcast.132, bf16[1024,12,64]{0,2,1:T(8,128)(2,1)S(1)} %bitcast.125), kind=kOutput, calls=%fused_computation.4 | convolution fusion | flops 836757504 | bytes 53264384 | tf_op jit(solution)/shard_map/while/body/eval_jaxpr/bqhd,bkhd->bhqk/dot_general | solution.py:73
  352.0 13.1 %fusion.20 = bf16[12,64,1024]{2,1,0:T(8,128)(2,1)} fusion(bf16[512,12,64]{0,2,1:T(8,128)(2,1)} %bitcast.133, f32[12,512]{1,0:T(8,128)S(1)} %log_add_fusion, f32[12,512,1024]{2,1,0:T(8,128)} %get-tuple-element.103, pred[512,1024]{1,0:T(8,128)(4,1)S(1)} %iota_compare_fusion), kind=kOutput, calls=%fused_computation.45 | convolution fusion | flops 831258624 | bytes 28073984 | tf_op jit(solution)/shard_map/while/body/eval_jaxpr/bhqk,bqhd->bkhd/dot_general | solution.py:86
  365.2 17.1 %multiply_convert_fusion = bf16[12,512,1024]{2,1,0:T(8,128)(2,1)S(1)} fusion(f32[12,512,1024]{2,1,0:T(8,128)} %get-tuple-element.108, f32[12,512]{1,0:T(8,128)S(1)} %get-tuple-element.107, f32[12,512]{1,0:T(8,128)S(1)} %log_add_fusion, f32[12,512,1024]{2,1,0:T(8,128)} %get-tuple-element.103, pred[512,1024]{1,0:T(8,128)(4,1)S(1)} %iota_compare_fusion), kind=kLoop, calls=%fused_computation.3 | loop fusion | flops 37748736 | bytes 63488000 | tf_op jit(solution)/shard_map/while/body/eval_jaxpr/convert_element_type | solution.py:77
  392.9 6.8 convolution_convert_fusion.2
  400.9 8.1 %convolution_convert_fusion.1 = bf16[3072,768]{0,1:T(8,128)(2,1)} fusion(bf16[1,512,768]{2,1,0:T(8,128)(2,1)S(1)} %copy-done.19, pred[512]{0:T(512)(128)(4,1)S(1)} %broadcast_compare_fusion, f32[512,3072]{1,0:T(8,128)} %fusion.64, f32[3072]{0:T(1024)S(1)} %convert_element_type.268), kind=kOutput, calls=%fused_computation.27 | convolution fusion | flops 2435186688 | bytes 11809280 | tf_op jit(solution)/shard_map/sqd,sqe->de/dot_general | solution.py:138
  410.5 8.6 %multiply_convert_fusion.3 = bf16[12,64,512]{2,1,0:T(8,128)(2,1)S(1)} fusion(bf16[1024,12,64]{0,2,1:T(8,128)(2,1)S(1)} %bitcast.120, bf16[12,512,1024]{2,1,0:T(8,128)(2,1)} %copy-done.4), kind=kOutput, calls=%fused_computation.61 | convolution fusion | flops 806092800 | bytes 14942208 | tf_op jit(solution)/shard_map/while/body/eval_jaxpr/bhqk,bkhd->bqhd/dot_general | solution.py:79
  419.0 27.6 %reduce-scatter.17.cloned.1.call-done = bf16[1,512,768]{1,2,0:T(8,128)(2,1)} async-done(((bf16[1,1024,768]{1,2,0:T(8,128)(2,1)}), bf16[1,512,768]{1,2,0:T(8,128)(2,1)}) %reduce-scatter.17.cloned.1.call-update) | async-done | bytes 786448 | tf_op jit(solution)/shard_map/reduce_scatter | solution.py:259
  446.7 5.4 convolution_convert_fusion
  454.2 6.2 reduce-scatter.33.cloned.1.call-done
  467.7 72.0 %reduce-scatter.25.cloned.1.call-done = bf16[768,192]{0,1:T(8,128)(2,1)} async-done(((bf16[768,3072]{0,1:T(8,128)(2,1)}), bf16[768,192]{0,1:T(8,128)(2,1)}) %reduce-scatter.25.cloned.1.call-update) | async-done | bytes 294928 | tf_op jit(solution)/shard_map/reduce_scatter | solution.py:294
  544.0 58.9 %all-reduce.15 = (bf16[768]{0:T(1024)(128)(2,1)S(1)}, bf16[768]{0:T(1024)(128)(2,1)S(1)}, bf16[768]{0:T(1024)(128)(2,1)S(1)}, bf16[768]{0:T(1024)(128)(2,1)S(1)}...) all-reduce(bf16[768]{0:T(1024)(128)(2,1)S(1)} %dynamic-update-slice, ...), channel_id=1, replica_groups=mesh['dp'=16,'cp'=2] {'dp'}, use_global_device_ids=true, to_apply=%add.6 | all-reduce | flops 8448 | bytes 33792
  604.2 5.4 reduce.23
  619.5 9.1 %fusion.33 = bf16[1,512,768]{2,1,0:T(8,128)(2,1)} fusion(f32[1,512,768]{2,1,0:T(8,128)S(1)} %copy-done.12, bf16[3072,768]{0,1:T(8,128)(2,1)} %all-gather.14.cloned.1.call-done, f32[768]{0:T(1024)S(1)} %convert_element_type.272, pred[512]{0:T(512)(128)(4,1)S(1)} %broadcast_compare_fusion, f32[512,3072]{1,0:T(8,128)} %fusion.64, ...), kind=kOutput, calls=%fused_computation.59 | convolution fusion | flops 2433220608 | bytes 13385216 | tf_op jit(solution)/shard_map/sqd,de->sqe/dot_general | solution.py:130
  628.6 62.0 %reduce-scatter.21.cloned.1.call-done = bf16[768,144]{0,1:T(8,128)(2,1)} async-done(((bf16[768,2304]{0,1:T(8,128)(2,1)}), bf16[768,144]{0,1:T(8,128)(2,1)}) %reduce-scatter.21.cloned.1.call-update) | async-done | bytes 221200 | tf_op jit(solution)/shard_map/reduce_scatter | solution.py:288
  692.8 5.5 all-reduce.14
  706.6 12.5 %reduce-scatter.29.cloned.1.call-done = bf16[1536,48]{0,1:T(8,128)(2,1)} async-done(((bf16[3072,48]{0,1:T(8,128)(2,1)}), bf16[1536,48]{0,1:T(8,128)(2,1)}) %reduce-scatter.29.cloned.1.call-update) | async-done | bytes 147472 | tf_op jit(solution)/shard_map/reduce_scatter | solution.py:332
  720.7 13.7 %reduce-scatter.31.cloned.1.call-done = bf16[384,144]{1,0:T(8,128)(2,1)} async-done(((bf16[768,144]{1,0:T(8,128)(2,1)}), bf16[384,144]{1,0:T(8,128)(2,1)}) %reduce-scatter.31.cloned.1.call-update) | async-done | bytes 110608
  (229 shorter events, 98.4 us)
Async XLA Ops:
  7.2 99.1 %all-gather.6.cloned.1.call-start = ((), (), s32[]{:S(2)}) async-start(), calls=%async_computation.12 | async-start | bytes 3760128 | tf_op jit(solution)/shard_map/all_gather | solution.py:115
  19.3 14.8 %copy-start.40 = (f32[48]{0:T(128)S(1)}, f32[48]{0:T(128)}, u32[]{:S(2)}) copy-start(f32[48]{0:T(128)} %param.27) | copy-start | bytes 580
  19.3 14.9 %copy-start.35 = (f32[192]{0:T(256)S(1)}, f32[192]{0:T(256)}, u32[]{:S(2)}) copy-start(f32[192]{0:T(256)} %param.28) | copy-start | bytes 2308
  25.9 78.9 %all-to-all-start = ((bf16[16,2,12288]{2,1,0:T(2,128)(2,1)}), bf16[16,2,12288]{2,1,0:T(2,128)(2,1)S(1)}, u32[]{:S(2)}, u32[]{:S(2)}) async-start(bf16[16,2,12288]{2,1,0:T(2,128)(2,1)} %reshape.514), calls=%async_computation | async-start | bytes 1572864 | tf_op jit(solution)/shard_map/all_to_all | solution.py:167
  32.1 128.5 %all-gather.8.cloned.1.call-start = ((), (), s32[]{:S(2)}) async-start(), calls=%async_computation.13 | async-start | bytes 4718592 | tf_op jit(solution)/shard_map/all_gather | solution.py:196
  111.9 16.5 %copy-start.21 = (f32[1536,48]{0,1:T(8,128)S(1)}, f32[1536,48]{0,1:T(8,128)}, u32[]{:S(2)}) copy-start(f32[1536,48]{0,1:T(8,128)} %param.22) | copy-start | bytes 884740
  113.2 24.4 %copy-start.2 = (s32[16]{0:T(128)S(1)}, s32[16]{0:T(128)}, u32[]{:S(2)}) copy-start(s32[16]{0:T(128)} %param.17) | copy-start | bytes 196
  113.2 92.3 %all-gather.10.cloned.1.call-start = ((), (), s32[]{:S(2)}) async-start(), calls=%async_computation.14 | async-start | bytes 1253376 | tf_op jit(solution)/shard_map/all_gather | solution.py:116
  118.5 136.5 %all-gather.12.cloned.1.call-start = ((), (), s32[]{:S(2)}) async-start(), calls=%async_computation.15 | async-start | bytes 5013504 | tf_op jit(solution)/shard_map/all_gather | solution.py:117
  118.6 21.4 %slice-start = ((bf16[1,512,2304]{2,1,0:T(8,128)(2,1)}), bf16[1,512,768]{2,1,0:T(8,128)(2,1)S(1)}, s32[]{:S(2)}) async-start(bf16[1,512,2304]{2,1,0:T(8,128)(2,1)} %copy-done.16), calls=%async_computation.27 | async-start | bytes 1572864 | tf_op jit(solution)/shard_map/slice | solution.py:194
  128.4 180.6 %all-gather.14.cloned.1.call-start = ((), (), s32[]{:S(2)}) async-start(), calls=%async_computation.16 | async-start | bytes 5013504 | tf_op jit(solution)/shard_map/all_gather | solution.py:118
  137.6 253.3 %reduce-scatter.23.cloned.1.call-start = ((), (), s32[]{:S(2)}) async-start(), calls=%async_computation.20 | async-start | bytes 1253376 | tf_op jit(solution)/shard_map/reduce_scatter | solution.py:291
  166.1 15.3 %copy-start.5 = (bf16[1,1024,768]{1,2,0:T(8,128)(2,1)}, bf16[1,1024,768]{1,2,0:T(8,128)(2,1)S(1)}, u32[]{:S(2)}) copy-start(bf16[1,1024,768]{1,2,0:T(8,128)(2,1)S(1)} %copy.50) | copy-start | bytes 4718596
  169.3 24.6 %copy-start.8 = (bf16[1,1024,768]{1,2,0:T(8,128)(2,1)S(1)}, bf16[1,1024,768]{1,2,0:T(8,128)(2,1)}, u32[]{:S(2)}) copy-start(bf16[1,1024,768]{1,2,0:T(8,128)(2,1)} %copy.48) | copy-start | bytes 4718596
  181.4 15.6 %copy-start.3 = (f32[12,512,1024]{2,1,0:T(8,128)S(1)}, f32[12,512,1024]{2,1,0:T(8,128)}, u32[]{:S(2)}) copy-start(f32[12,512,1024]{2,1,0:T(8,128)} %get-tuple-element.103) | copy-start | bytes 75497472
  208.0 115.8 %copy-start.10 = (f32[1,512,768]{2,1,0:T(8,128)}, f32[1,512,768]{2,1,0:T(8,128)S(1)}, u32[]{:S(2)}) copy-start(f32[1,512,768]{2,1,0:T(8,128)S(1)} %get-tuple-element.105) | copy-start | bytes 4718596
  334.1 85.0 %reduce-scatter.19.cloned.1.call-start = ((), (), s32[]{:S(2)}) async-start(), calls=%async_computation.18 | async-start | bytes 2359296 | tf_op jit(solution)/shard_map/reduce_scatter | solution.py:262
  365.1 81.5 %reduce-scatter.17.cloned.1.call-start = ((), (), s32[]{:S(2)}) async-start(), calls=%async_computation.17 | async-start | bytes 2359296 | tf_op jit(solution)/shard_map/reduce_scatter | solution.py:259
  365.2 17.1 %copy-start.7 = (bf16[1,512,768]{1,2,0:T(8,128)(2,1)S(1)}, bf16[1,512,768]{1,2,0:T(8,128)(2,1)}, u32[]{:S(2)}) copy-start(bf16[1,512,768]{1,2,0:T(8,128)(2,1)} %copy.49) | copy-start | bytes 2359300
  387.6 72.8 %reduce-scatter.33.cloned.1.call-start = ((), (), s32[]{:S(2)}) async-start(), calls=%async_computation.25 | async-start | bytes 294912
  392.6 147.1 %reduce-scatter.25.cloned.1.call-start = ((), (), s32[]{:S(2)}) async-start(), calls=%async_computation.21 | async-start | bytes 5013504 | tf_op jit(solution)/shard_map/reduce_scatter | solution.py:294
  399.8 219.5 %reduce-scatter.27.cloned.1.call-start = ((), (), s32[]{:S(2)}) async-start(), calls=%async_computation.22 | async-start | bytes 5013504 | tf_op jit(solution)/shard_map/reduce_scatter | solution.py:297
  409.0 37.6 %copy-start.24 = (f32[768]{0:T(1024)S(1)}, f32[768]{0:T(1024)}, u32[]{:S(2)}) copy-start(f32[768]{0:T(1024)} %copy-done.23) | copy-start | bytes 9220
  409.0 37.6 %copy-start.26 = (f32[512]{0:T(512)S(1)}, f32[512]{0:T(512)}, u32[]{:S(2)}) copy-start(f32[512]{0:T(512)} %copy-done.25) | copy-start | bytes 6148
  409.1 37.6 %copy-start.28 = (f32[512]{0:T(512)S(1)}, f32[512]{0:T(512)}, u32[]{:S(2)}) copy-start(f32[512]{0:T(512)} %copy-done.27) | copy-start | bytes 6148
  409.1 37.6 %copy-start.32 = (f32[768]{0:T(1024)S(1)}, f32[768]{0:T(1024)}, u32[]{:S(2)}) copy-start(f32[768]{0:T(1024)} %copy-done.31) | copy-start | bytes 9220
  409.1 281.5 %reduce-scatter.21.cloned.1.call-start = ((), (), s32[]{:S(2)}) async-start(), calls=%async_computation.19 | async-start | bytes 3760128 | tf_op jit(solution)/shard_map/reduce_scatter | solution.py:288
  452.0 252.7 %reduce-scatter.35.cloned.1.call-start = ((), (), s32[]{:S(2)}) async-start(), calls=%async_computation.26 | async-start | bytes 589824
  610.7 87.5 %all-to-all-start.1 = ((bf16[16,2,12288]{2,1,0:T(2,128)(2,1)}), bf16[16,2,12288]{2,1,0:T(2,128)(2,1)S(1)}, u32[]{:S(2)}, u32[]{:S(2)}) async-start(bf16[16,2,12288]{2,1,0:T(2,128)(2,1)} %reshape.516), calls=%async_computation.3 | async-start | bytes 1572864 | tf_op jit(solution)/shard_map/all_to_all | solution.py:273
  614.3 104.7 %reduce-scatter.29.cloned.1.call-start = ((), (), s32[]{:S(2)}) async-start(), calls=%async_computation.23 | async-start | bytes 442368 | tf_op jit(solution)/shard_map/reduce_scatter | solution.py:332
  619.3 115.1 %reduce-scatter.31.cloned.1.call-start = ((), (), s32[]{:S(2)}) async-start(), calls=%async_computation.24 | async-start | bytes 589824
  699.0 37.1 %copy-start.1 = (bf16[16,32,768]{2,1,0:T(8,128)(2,1)S(1)}, bf16[16,32,768]{2,1,0:T(8,128)(2,1)}, u32[]{:S(2)}) copy-start(bf16[16,32,768]{2,1,0:T(8,128)(2,1)} %param.15) | copy-start | bytes 2359300
  (31 other events, 172.4 us)
Sparse Core Ops, SparseCore 0:
  15.2 55.2 all-gather.5
  113.4 47.2 all-gather.7
  162.9 37.4 all-gather.9
  202.6 52.3 all-gather.11
  257.1 51.9 all-gather.13
  334.2 56.6 reduce-scatter.22
  393.1 25.0 reduce-scatter.18
  420.6 26.0 reduce-scatter.16
  449.4 10.9 reduce-scatter.32
  464.1 75.5 reduce-scatter.24
  544.1 75.0 reduce-scatter.26
  623.0 67.5 reduce-scatter.20
  692.8 11.9 reduce-scatter.34
  706.9 12.0 reduce-scatter.28
  721.2 13.1 reduce-scatter.30
where the time goes:
time: 751 us; the launch traced here: 743 us
  waiting for transfers between devices  320 us (43%)
  blocking collectives  164 us (22%)
  matrix products  132 us (18%)
  other arithmetic  53.6 us (7%)
  local copies, waits for them, and re-layouts  44 us (6%)
  between operations  17.6 us (2%)
  starting transfers between devices  11.2 us (1%)
    unnamed x2, blocking collectives  128 us
    reduce_scatter x1, waiting for transfers between devices, local(): lax.psum_scatter(grad_up.astype(jnp.bfloat16), 'dp', scatter_dimension=1,...  72 us
    reduce_scatter x1, waiting for transfers between devices, local(): lax.psum_scatter(grad_qkv.astype(jnp.bfloat16), 'dp', scatter_dimension=1...  62 us
    all_gather x1, waiting for transfers between devices, fetch_weights(): lax.all_gather(down_part, 'dp', axis=1, tiled=True)  47.1 us
    all_gather x1, waiting for transfers between devices, fetch_weights(): lax.all_gather(up_part, 'dp', axis=1, tiled=True)  46.6 us
    reduce_scatter x1, waiting for transfers between devices, local(): lax.psum_scatter(joined(grad_keys).astype(jnp.bfloat16), 'cp', scatter_di...  27.6 us
    unnamed x117, local copies, waits for them, and re-layouts  24.7 us
    unnamed x18, waiting for transfers between devices  24.3 us
  transfers between devices with their start and end apart: 17, of which 12 were waited for; matrix products, arithmetic and copies ran while one was open for 25% of the time, Pallas kernels for 0%

commit v1 on v0

--- a/solution.py
+++ b/solution.py
@@ -1,8 +1,11 @@
+import functools
 import math
 
 import jax
 import jax.numpy as jnp
 from jax import lax
+from jax.experimental import pallas as pl
+from jax.experimental.pallas import tpu as pltpu
 from jax.sharding import PartitionSpec as P
 
 HEADS = 12
@@ -13,6 +16,1134 @@
 NEG_BIG = -1e30
 TANH_SCALE = 0.7978845608028654
 CUBIC_TERM = 0.044715
+MESH_IDS = pl.DeviceIdType.MESH
+BF = jnp.bfloat16
+F32 = jnp.float32
+
+Z, Y, C, X = 4, 2, 2, 2
+
+
+def mult(value, n):
+    return value if isinstance(value, int) else pl.multiple_of(value, n)
+
+
+def coords():
+    d = lax.axis_index("dp")
+    x = lax.axis_index("cp")
+    return d // (Y * C), (d // C) % Y, d % C, x, d
+
+
+def dev(z, y, c, x):
+    return {"dp": (z * Y + y) * C + c, "cp": x}
+
+
+def rcopy(src, dst, ssem, rsem, where):
+    return pltpu.make_async_remote_copy(
+        src_ref=src, dst_ref=dst, send_sem=ssem, recv_sem=rsem, device_id=where, device_id_type=MESH_IDS
+    )
+
+
+def wait_bytes(ref, sem):
+    pltpu.make_async_copy(ref, ref, sem).wait()
+
+
+def enter(everyone):
+    d = lax.axis_index("dp")
+    x = lax.axis_index("cp")
+    barrier = pltpu.get_barrier_semaphore()
+
+    def greet(k, carry):
+        kd = k // X
+        kx = k % X
+
+        @pl.when(jnp.logical_or(kd != d, kx != x))
+        def _():
+            pl.semaphore_signal(barrier, inc=1, device_id={"dp": kd, "cp": kx}, device_id_type=MESH_IDS)
+
+        return carry
+
+    lax.fori_loop(0, everyone, greet, 0)
+    pl.semaphore_wait(barrier, everyone - 1)
+
+
+def dot_nn(a, b):
+    return lax.dot_general(a, b, (((1,), (0,)), ((), ())), preferred_element_type=F32)
+
+
+def dot_nt(a, b):
+    return lax.dot_general(a, b, (((1,), (1,)), ((), ())), preferred_element_type=F32)
+
+
+def dot_tn(a, b):
+    return lax.dot_general(a, b, (((0,), (0,)), ((), ())), preferred_element_type=F32)
+
+
+def norm_parts(v):
+    mean = jnp.mean(v, axis=-1, keepdims=True)
+    cen = v - mean
+    var = jnp.mean(cen * cen, axis=-1, keepdims=True)
+    rstd = lax.rsqrt(var + EPSILON)
+    return cen * rstd, rstd
+
+
+def live_length(len_ref, deal_ref, slot):
+    total = jnp.int32(0)
+    for s in range(len_ref.shape[0]):
+        total = total + jnp.where(deal_ref[s] == slot, len_ref[s], 0)
+    return total
+
+
+class Piece:
+    def __init__(self, full, shard, R, r0, rn, step, c0, cn):
+        self.full, self.shard = full, shard
+        self.R, self.r0, self.rn, self.step, self.c0, self.cn = R, r0, rn, step, c0, cn
+
+    def at(self, z, y, c, x):
+        d = (z * Y + y) * C + c
+        return self.full.at[
+            pl.ds(mult(d * self.R + self.r0, 16), self.rn), pl.ds(mult(x * self.step + self.c0, 128), self.cn)
+        ]
+
+    def own(self):
+        return self.shard.at[pl.ds(self.r0, self.rn), pl.ds(self.c0, self.cn)]
+
+
+class Gather:
+    LOC, ZS, ZR, S2, R2, S3, R3, S4, R4 = range(9)
+
+    def __init__(self, piece, sems, k, dummy, where):
+        self.p, self.sems, self.k, self.dummy = piece, sems, k, dummy
+        z, y, c, x, _ = where
+        self.z, self.y, self.c, self.x = z, y, c, x
+        self.y2, self.x2 = (y + 1 - c) % 2, (x + c) % 2
+        self.y3, self.x3 = (y + c) % 2, (x + 1 - c) % 2
+
+    def sem(self, which):
+        return self.sems.at[self.k, which]
+
+    def wait(self, count, which):
+        p = self.p
+        wait_bytes(self.dummy.at[pl.ds(0, count * p.rn), pl.ds(0, p.cn)], self.sem(which))
+
+    def start(self):
+        p, z, y, c, x = self.p, self.z, self.y, self.c, self.x
+        pltpu.make_async_copy(p.own(), p.at(z, y, c, x), self.sem(self.LOC)).start()
+        for dz in range(1, Z):
+            z2 = (z + dz) % Z
+            rcopy(p.own(), p.at(z, y, c, x), self.sem(self.ZS), self.sem(self.ZR), dev(z2, y, c, x)).start()
+
+    def tick2(self):
+        p, z, y, c, x = self.p, self.z, self.y, self.c, self.x
+        self.wait(1, self.LOC)
+        self.wait(Z - 1, self.ZR)
+        for zz in range(Z):
+            q = p.at(zz, y, c, x)
+            rcopy(q, q, self.sem(self.S2), self.sem(self.R2), dev(z, self.y2, c, self.x2)).start()
+        for zz in range(Z):
+            q = p.at(zz, y, c, x)
+            rcopy(q, q, self.sem(self.S3), self.sem(self.R3), dev(z, self.y3, c, self.x3)).start()
+            rcopy(q, q, self.sem(self.S4), self.sem(self.R4), dev(z, y, 1 - c, x)).start()
+
+    def tick3(self):
+        p, z, y, c, x = self.p, self.z, self.y, self.c, self.x
+        self.wait(Z, self.R2)
+        for zz in range(Z):
+            q = p.at(zz, self.y2, c, self.x2)
+            rcopy(q, q, self.sem(self.S3), self.sem(self.R3), dev(z, self.y3, c, self.x3)).start()
+            rcopy(q, q, self.sem(self.S4), self.sem(self.R4), dev(z, y, 1 - c, x)).start()
+
+    def tick4(self):
+        p, z, y, c, x = self.p, self.z, self.y, self.c, self.x
+        self.wait(2 * Z, self.R3)
+        for zz in range(Z):
+            for which in range(2):
+                yy = which * (1 - c) + (1 - y) * c
+                xx = (1 - x) * (1 - c) + which * c
+                q = p.at(zz, yy, c, xx)
+                rcopy(q, q, self.sem(self.S4), self.sem(self.R4), dev(z, y, 1 - c, x)).start()
+
+    def tick5(self):
+        self.wait(4 * Z, self.R4)
+
+    def drain(self):
+        self.wait(Z - 1, self.ZS)
+        self.wait(Z, self.S2)
+        self.wait(2 * Z, self.S3)
+        self.wait(4 * Z, self.S4)
+
+
+class Vectors:
+    LOC, ZS, ZR, S2, R2, S4, R4 = range(7)
+
+    def __init__(self, full, shard, sems, where):
+        self.full, self.shard, self.sems, self.where = full, shard, sems, where
+
+    def at(self, z, y, c):
+        return self.full.at[(z * Y + y) * C + c]
+
+    def start(self):
+        z, y, c, x, _ = self.where
+        pltpu.make_async_copy(self.shard, self.at(z, y, c), self.sems.at[self.LOC]).start()
+        for dz in range(1, Z):
+            z2 = (z + dz) % Z
+            rcopy(self.shard, self.at(z, y, c), self.sems.at[self.ZS], self.sems.at[self.ZR], dev(z2, y, c, x)).start()
+
+    def wait(self, count, which):
+        wait_bytes(self.full.at[pl.ds(0, count)], self.sems.at[which])
+
+    def tick2(self):
+        z, y, c, x, _ = self.where
+        self.wait(1, self.LOC)
+        self.wait(Z - 1, self.ZR)
+        for zz in range(Z):
+            q = self.at(zz, y, c)
+            rcopy(q, q, self.sems.at[self.S2], self.sems.at[self.R2], dev(z, 1 - y, c, x)).start()
+            rcopy(q, q, self.sems.at[self.S4], self.sems.at[self.R4], dev(z, y, 1 - c, x)).start()
+
+    def tick3(self):
+        z, y, c, x, _ = self.where
+        self.wait(Z, self.R2)
+        for zz in range(Z):
+            q = self.at(zz, 1 - y, c)
+            rcopy(q, q, self.sems.at[self.S4], self.sems.at[self.R4], dev(z, y, 1 - c, x)).start()
+
+    def tick4(self):
+        self.wait(2 * Z, self.R4)
+
+    def drain(self):
+        self.wait(Z - 1, self.ZS)
+        self.wait(Z, self.S2)
+        self.wait(2 * Z, self.S4)
+
+
+G1, C1, BP, G2, C2, BD, BU = range(7)
+
+
+def gather_chunks(wq, wp, wu, wd, sq, sp, su, sd):
+    rq, rp, ru, rd = sq.shape[0], sp.shape[0], su.shape[0], sd.shape[0]
+    half, wide = sq.shape[1], sd.shape[1]
+    out = []
+    for k in range(3):
+        out.append(Piece(wq, sq, rq, k * (rq // 3), rq // 3, half, 0, half))
+    out.append(Piece(wp, sp, rp, 0, rp, half, 0, half))
+    for k in range(4):
+        out.append(Piece(wu, su, ru, k * (ru // 4), ru // 4, half, 0, half))
+    for k in range(4):
+        out.append(Piece(wd, sd, rd, 0, rd, wide, k * (wide // 4), wide // 4))
+    return out
+
+
+N_GATHER = 12
+
+
+def forward_kernel(
+    len_ref, deal_ref, xg, cot, sq, sp, su, sd, sv,
+    wq_o, wp_o, wu_o, wd_o, xr_o, gw_o, qs_o, ka_o, va_o, at_o, lse_o, r_o, a2_o, hd_o, gp_o, vec_o, out_o,
+    wq, wp, wu, wd, xr, a1, qs, ka, va, at, lse, r, a2, hd, gp, vg, vec, bu3, sc0, sc1, outw,
+    gsem, vsem, msem, osem,
+):
+    where = coords()
+    z, y, c, x, d = where
+    width = xr.shape[1]
+    rows = xr.shape[0]
+    qrows = rows // 2
+    small = xg.shape[1]
+    pairs = width // 128
+    tile = 256
+
+    enter(Z * Y * C * X)
+
+    vectors = Vectors(vg, sv, vsem, where)
+    vectors.start()
+    per_quarter = qrows // small
+    place = mult(x * qrows + (d % per_quarter) * small, 16)
+    core_to = (x + d // per_quarter) % 2
+    dst = xr.at[pl.ds(place, small)]
+
+    def deal_out(t, carry):
+        td = (t // 2) * 2 + core_to
+        tx = t % 2
+        mine = jnp.logical_and(td == d, tx == x)
+
+        @pl.when(mine)
+        def _():
+            pltpu.make_async_copy(xg.at[t], dst, msem.at[1]).start()
+
+        @pl.when(jnp.logical_not(mine))
+        def _():
+            rcopy(xg.at[t], dst, msem.at[0], msem.at[1], {"dp": td, "cp": tx}).start()
+
+        return carry
+
+    lax.fori_loop(0, xg.shape[0], deal_out, 0)
+    chunks = [
+        Gather(p, gsem, k, wu, where) for k, p in enumerate(gather_chunks(wq, wp, wu, wd, sq, sp, su, sd))
+    ]
+    for ch in chunks:
+        ch.start()
+
+    vectors.tick2()
+    vectors.tick3()
+
+    order = []
+    for s in range(len(chunks) + 2):
+        for back, name in ((0, "tick2"), (1, "tick3"), (2, "tick4")):
+            if 0 <= s - back < len(chunks):
+                order.append((s - back, name))
+    pending = [getattr(chunks[k], name) for k, name in order]
+
+    def run(n):
+        for _ in range(n):
+            if pending:
+                pending.pop(0)()
+
+    vectors.tick4()
+
+    def add_table(k, acc):
+        return acc + vg[k].astype(F32)
+
+    vec[...] = lax.fori_loop(1, Z * Y * C, add_table, vg[0].astype(F32))
+    for k in range(bu3.shape[0]):
+        per = width // tile
+        bu3[k] = vec[BU + k // per:BU + k // per + 1, (k % per) * tile:(k % per + 1) * tile]
+
+    wait_bytes(xr, msem.at[1])
+    lrows = 128
+
+    def first_norm(k, carry):
+        at_rows = pl.ds(mult(k * lrows, lrows), lrows)
+        n1, _ = norm_parts(xr[at_rows, :].astype(F32))
+        a1[at_rows, :] = (n1 * vec[G1:G1 + 1, :] + vec[C1:C1 + 1, :]).astype(BF)
+        return carry
+
+    lax.fori_loop(0, rows // lrows, first_norm, 0)
+
+    run(13)
+    for k in range(3):
+        chunks[k].tick5()
+    keep = [pltpu.make_async_copy(wq, wq_o, osem.at[0])]
+    keep[-1].start()
+
+    def cot_copy(b):
+        return (x + b) % 2, cot.at[pl.ds(b * qrows, qrows)], gw_o.at[pl.ds(mult(x * qrows, qrows), qrows)]
+
+    for b in range(2):
+        core_b, src_b, dst_b = cot_copy(b)
+        same = jnp.logical_and(core_b == c, c == x)
+
+        @pl.when(same)
+        def _(src_b=src_b, dst_b=dst_b):
+            pltpu.make_async_copy(src_b, dst_b, msem.at[3]).start()
+
+        @pl.when(jnp.logical_not(same))
+        def _(src_b=src_b, dst_b=dst_b, core_b=core_b):
+            rcopy(src_b, dst_b, msem.at[2], msem.at[3], dev(z, y, core_b, c)).start()
+
+    quarters = (c, 3 - c)
+
+    def q_at(i):
+        return pl.ds(mult(quarters[i] * qrows, qrows), qrows)
+
+    steps = width // tile
+    for part in range(3):
+        def project(n, carry, part=part):
+            lanes = pl.ds(mult(n * tile, tile), tile)
+            res = dot_nt(a1[...], wq[pl.ds(mult(part * width + n * tile, tile), tile), :]).astype(BF)
+            if part == 0:
+                qs[:, lanes] = res * jnp.asarray(HEAD_DIM ** -0.5, BF)
+            else:
+                to = ka if part == 1 else va
+                for i in range(2):
+                    to[q_at(i), lanes] = res[i * qrows:(i + 1) * qrows]
+            return carry
+
+        lax.fori_loop(0, steps, project, 0)
+        if part > 0:
+            to = ka if part == 1 else va
+            for i in range(2):
+                rcopy(to.at[q_at(i)], to.at[q_at(i)], msem.at[4 + 2 * (part - 1)], msem.at[5 + 2 * (part - 1)], dev(z, y, 1 - c, x)).start()
+        run(1)
+    wait_bytes(ka.at[pl.ds(0, rows)], msem.at[5])
+    wait_bytes(va.at[pl.ds(0, rows)], msem.at[7])
+    for src, out, s in ((qs, qs_o, 1), (ka, ka_o, 2), (va, va_o, 3), (xr, xr_o, 4), (vec, vec_o, 5)):
+        keep.append(pltpu.make_async_copy(src, out, osem.at[s]))
+        keep[-1].start()
+
+    lane = lax.broadcasted_iota(jnp.int32, (qrows, 128), 1)
+    kpos = lax.broadcasted_iota(jnp.int32, (qrows, qrows), 0)
+    qpos = lax.broadcasted_iota(jnp.int32, (qrows, qrows), 1)
+    groups = qrows // 8
+
+    def pair_body(p, carry):
+        lanes = pl.ds(mult(p * 128, 128), 128)
+        for i in range(2):
+            quarter = quarters[i]
+            qp = qs[i * qrows:(i + 1) * qrows, lanes]
+            zero = jnp.zeros_like(qp)
+            qh = (jnp.where(lane < HEAD_DIM, qp, zero), jnp.where(lane >= HEAD_DIM, qp, zero))
+
+            def scores(j, tops):
+                at_keys = pl.ds(mult(j * qrows, qrows), qrows)
+                kj = ka[at_keys, lanes]
+                keep_it = jnp.logical_or(kpos <= qpos, j < quarter)
+                new = []
+                for h, sc in enumerate((sc0, sc1)):
+                    s = jnp.where(keep_it, dot_nt(kj, qh[h]), NEG_BIG)
+                    sc[at_keys, :] = s
+                    new.append(jnp.maximum(tops[h], jnp.max(s.reshape(groups, 8, qrows), axis=0)))
+                return tuple(new)
+
+            low = jnp.full((8, qrows), NEG_BIG, F32)
+            tops = lax.fori_loop(0, quarter + 1, scores, (low, low))
+            tops = tuple(jnp.max(t, axis=0, keepdims=True) for t in tops)
+
+            def values(j, state):
+                at_keys = pl.ds(mult(j * qrows, qrows), qrows)
+                vt = va[at_keys, lanes].T
+                new = []
+                for h, sc in enumerate((sc0, sc1)):
+                    total, acc = state[h]
+                    e = jnp.exp(sc[at_keys, :] - tops[h])
+                    total = total + jnp.sum(e.reshape(groups, 8, qrows), axis=0)
+                    acc = acc + dot_nn(vt[h * HEAD_DIM:(h + 1) * HEAD_DIM], e.astype(BF))
+                    new.append((total, acc))
+                return tuple(new)
+
+            blank = (jnp.zeros((8, qrows), F32), jnp.zeros((HEAD_DIM, qrows), F32))
+            state = lax.fori_loop(0, quarter + 1, values, (blank, blank))
+            parts = []
+            for h in range(2):
+                total = jnp.sum(state[h][0], axis=0, keepdims=True)
+                parts.append(state[h][1] / total)
+                lse[p, i * 2 + h:i * 2 + h + 1, :] = tops[h] + jnp.log(total)
+            at[i * qrows:(i + 1) * qrows, lanes] = jnp.concatenate(parts, axis=0).T.astype(BF)
+        return carry
+
+    per = 2
+    for k in range(0, pairs, per):
+        lax.fori_loop(k, k + per, pair_body, 0)
+        run(5)
+
+    chunks[3].tick5()
+    for src, out, s in ((wp, wp_o, 6), (at, at_o, 7), (lse, lse_o, 8)):
+        keep.append(pltpu.make_async_copy(src, out, osem.at[s]))
+        keep[-1].start()
+
+    def attend_out(n, carry):
+        lanes = pl.ds(mult(n * tile, tile), tile)
+        res = dot_nt(at[...], wp[pl.ds(mult(n * tile, tile), tile), :])
+        r[:, lanes] = xr[:, lanes].astype(F32) + res + vec[BP:BP + 1, lanes]
+        return carry
+
+    lax.fori_loop(0, steps, attend_out, 0)
+
+    def second_norm(k, carry):
+        at_rows = pl.ds(mult(k * lrows, lrows), lrows)
+        n2, _ = norm_parts(r[at_rows, :])
+        a2[at_rows, :] = (n2 * vec[G2:G2 + 1, :] + vec[C2:C2 + 1, :]).astype(BF)
+        return carry
+
+    lax.fori_loop(0, rows // lrows, second_norm, 0)
+    run(2)
+    for k in range(4, 8):
+        chunks[k].tick5()
+    for src, out, s in ((wu, wu_o, 9), (r, r_o, 10), (a2, a2_o, 11)):
+        keep.append(pltpu.make_async_copy(src, out, osem.at[s]))
+        keep[-1].start()
+
+    def up(n, carry):
+        lanes = pl.ds(mult(n * tile, tile), tile)
+        u = dot_nt(a2[...], wu[lanes, :]) + bu3[n]
+        sq_u = u * u
+        t = jnp.tanh(TANH_SCALE * (u + CUBIC_TERM * sq_u * u))
+        half_up = 0.5 * (1.0 + t)
+        hd[:, lanes] = (u * half_up).astype(BF)
+        slope = TANH_SCALE * (1.0 + 3.0 * CUBIC_TERM * sq_u)
+        gp[:, lanes] = (half_up + 0.5 * u * (1.0 - t * t) * slope).astype(BF)
+        return carry
+
+    blocks = hd.shape[1] // tile
+    for k in range(0, blocks, 4):
+        lax.fori_loop(k, k + 4, up, 0)
+        run(2)
+    for src, out, s in ((hd, hd_o, 12), (gp, gp_o, 13)):
+        keep.append(pltpu.make_async_copy(src, out, osem.at[s]))
+        keep[-1].start()
+    run(len(pending))
+    for k in range(8, len(chunks)):
+        chunks[k].tick5()
+    keep.append(pltpu.make_async_copy(wd, wd_o, osem.at[14]))
+    keep[-1].start()
+    my_len = live_length(len_ref, deal_ref, (z * Y + y) * C + x)
+    rowpos = lax.broadcasted_iota(jnp.int32, (qrows, 1), 0)
+
+    def down(n, carry):
+        lanes = pl.ds(mult(n * tile, tile), tile)
+        res = dot_nt(hd[...], wd[pl.ds(mult(n * tile, tile), tile), :])
+        res = r[:, lanes] + res + vec[BD:BD + 1, lanes]
+        for i in range(2):
+            live = quarters[i] * qrows + rowpos < my_len
+            outw[i * qrows:(i + 1) * qrows, lanes] = jnp.where(live, res[i * qrows:(i + 1) * qrows], 0.0).astype(BF)
+        return carry
+
+    lax.fori_loop(0, steps, down, 0)
+    keep.append(pltpu.make_async_copy(outw, out_o, osem.at[15]))
+    keep[-1].start()
+
+    for ch in chunks:
+        ch.drain()
+    vectors.drain()
+
+    @pl.when(core_to == c)
+    def _():
+        wait_bytes(xr.at[pl.ds(0, rows - small)], msem.at[0])
+
+    @pl.when(core_to != c)
+    def _():
+        wait_bytes(xr, msem.at[0])
+
+    @pl.when(c == x)
+    def _():
+        wait_bytes(xr.at[pl.ds(0, qrows)], msem.at[2])
+
+    @pl.when(c != x)
+    def _():
+        wait_bytes(xr, msem.at[2])
+
+    wait_bytes(xr, msem.at[3])
+    wait_bytes(ka.at[pl.ds(0, rows)], msem.at[4])
+    wait_bytes(va.at[pl.ds(0, rows)], msem.at[6])
+    for cp in keep:
+        cp.wait()
+
+
+def forward(lengths, dealing, xg, cot, sq, sp, su, sd, sv):
+    width = xg.shape[2]
+    rows = cot.shape[0]
+    ff = su.shape[0] * Z * Y * C
+    keys = rows * 2
+    pairs = width // 128
+
+    def arr(shape, dtype=BF):
+        return jax.ShapeDtypeStruct(shape, dtype)
+
+    outs = [
+        arr((3 * width, width)), arr((width, width)), arr((ff, width)), arr((width, ff)),
+        arr((rows, width)), arr((rows, width)), arr((rows, width)), arr((keys, width)), arr((keys, width)),
+        arr((rows, width)), arr((pairs, 8, rows // 2), F32), arr((rows, width), F32), arr((rows, width)),
+        arr((rows, ff)), arr((rows, ff)), arr((16, width), F32), arr((rows, width)),
+    ]
+    vm = pltpu.VMEM
+    scratch = [
+        vm((3 * width, width), BF), vm((width, width), BF), vm((ff, width), BF), vm((width, ff), BF),
+        vm((rows, width), BF), vm((rows, width), BF), vm((rows, width), BF), vm((keys, width), BF),
+        vm((keys, width), BF), vm((rows, width), BF), vm((pairs, 8, rows // 2), F32), vm((rows, width), F32),
+        vm((rows, width), BF), vm((rows, ff), BF), vm((rows, ff), BF), vm((Z * Y * C, 16, width), BF),
+        vm((16, width), F32), vm((ff // 256, 1, 256), F32), vm((keys, rows // 2), F32), vm((keys, rows // 2), F32),
+        vm((rows, width), BF),
+        pltpu.SemaphoreType.DMA((N_GATHER, 9)), pltpu.SemaphoreType.DMA((7,)), pltpu.SemaphoreType.DMA((8,)),
+        pltpu.SemaphoreType.DMA((16,)),
+    ]
+    anyspec = pl.BlockSpec(memory_space=pl.ANY)
+    smem = pl.BlockSpec(memory_space=pltpu.SMEM)
+    return pl.pallas_call(
+        forward_kernel,
+        out_shape=outs,
+        in_specs=[smem, smem] + [anyspec] * 7,
+        out_specs=[anyspec] * len(outs),
+        scratch_shapes=scratch,
+        compiler_params=pltpu.CompilerParams(
+            collective_id=0, has_side_effects=True, vmem_limit_bytes=60 * 1024 * 1024
+        ),
+        name="forward",
+    )(lengths, dealing, xg, cot, sq, sp, su, sd, sv)
+
+
+class Reduce:
+    S1, R1, S2, R2, S3, R3, S4, R4 = range(8)
+
+    def __init__(self, grad, R, step, c0, C, zlist, bufs, out, out_c0, sems, k, where):
+        self.grad, self.R, self.step, self.c0, self.cn, self.zlist = grad, R, step, c0, C, zlist
+        self.r1, self.r2, self.r3, self.r4 = bufs
+        self.out, self.out_c0, self.sems, self.k = out, out_c0, sems, k
+        self.z, self.y, self.c, self.x, _ = where
+        c, y, x = self.c, self.y, self.x
+        self.y2, self.x2 = (y + c) % 2, (x + 1 - c) % 2
+        self.y3, self.x3 = (y + 1 - c) % 2, (x + c) % 2
+
+    def sem(self, which):
+        return self.sems.at[self.k, which]
+
+    def rows(self, z, y, c):
+        return pl.ds(mult(((z * Y + y) * C + c) * self.R, 16), self.R)
+
+    def cols(self, x):
+        return pl.ds(mult(x * self.step + self.c0, 128), self.cn)
+
+    def at(self, z, y, c, x):
+        return self.grad.at[self.rows(z, y, c), self.cols(x)]
+
+    def add(self, rows, cols, got):
+        self.grad[rows, cols] = (self.grad[rows, cols].astype(F32) + got.astype(F32)).astype(BF)
+
+    def zidx(self, zi):
+        return self.zlist[0] if len(self.zlist) == 1 else zi
+
+    def start(self):
+        z, y, c, x = self.z, self.y, self.c, self.x
+        to = dev(z, y, 1 - c, x)
+        for zi, zz in enumerate(self.zlist):
+            for yy in range(Y):
+                for xx in range(X):
+                    rcopy(
+                        self.at(zz, yy, 1 - c, xx), self.r1.at[zi * Y + yy, xx],
+                        self.sem(self.S1), self.sem(self.R1), to,
+                    ).start()
+
+    def tick2(self):
+        z, y, c, x = self.z, self.y, self.c, self.x
+        wait_bytes(self.r1, self.sem(self.R1))
+
+        def body(e, carry):
+            rows = self.rows(self.zidx(e // Y), e % Y, c)
+            for xx in range(X):
+                self.add(rows, self.cols(xx), self.r1[e, xx])
+            return carry
+
+        lax.fori_loop(0, len(self.zlist) * Y, body, 0)
+        to = dev(z, self.y2, c, self.x2)
+        for zi, zz in enumerate(self.zlist):
+            for w in range(2):
+                yy = w * (1 - c) + (1 - y) * c
+                xx = (1 - x) * (1 - c) + w * c
+                rcopy(self.at(zz, yy, c, xx), self.r2.at[zi * 2 + w], self.sem(self.S2), self.sem(self.R2), to).start()
+
+    def tick3(self):
+        z, y, c, x = self.z, self.y, self.c, self.x
+        wait_bytes(self.r2, self.sem(self.R2))
+
+        def body(e, carry):
+            w = e % 2
+            yy = w * (1 - c) + y * c
+            xx = x * (1 - c) + w * c
+            self.add(self.rows(self.zidx(e // 2), yy, c), self.cols(xx), self.r2[e])
+            return carry
+
+        lax.fori_loop(0, len(self.zlist) * 2, body, 0)
+        to = dev(z, self.y3, c, self.x3)
+        for zi, zz in enumerate(self.zlist):
+            rcopy(self.at(zz, self.y3, c, self.x3), self.r3.at[zi], self.sem(self.S3), self.sem(self.R3), to).start()
+
+    def tick4(self):
+        z, y, c, x = self.z, self.y, self.c, self.x
+        wait_bytes(self.r3, self.sem(self.R3))
+
+        def body(zi, carry):
+            self.add(self.rows(self.zidx(zi), y, c), self.cols(x), self.r3[zi])
+            return carry
+
+        lax.fori_loop(0, len(self.zlist), body, 0)
+        for zz in self.zlist:
+            @pl.when(z != zz)
+            def _(zz=zz):
+                rcopy(
+                    self.at(zz, y, c, x), self.r4.at[z], self.sem(self.S4), self.sem(self.R4), dev(zz, y, c, x)
+                ).start()
+
+    def tick5(self):
+        z, y, c, x = self.z, self.y, self.c, self.x
+
+        def last():
+            wait_bytes(self.r4.at[pl.ds(0, Z - 1)], self.sem(self.R4))
+            total = self.grad[self.rows(z, y, c), self.cols(x)].astype(F32)
+            for dz in range(1, Z):
+                total = total + self.r4[(z + dz) % Z].astype(F32)
+            self.out[:, self.out_c0:self.out_c0 + self.cn] = total
+
+        if len(self.zlist) == Z:
+            last()
+        else:
+            pl.when(z == self.zlist[0])(last)
+
+    def drain(self):
+        wait_bytes(self.r1, self.sem(self.S1))
+        wait_bytes(self.r2, self.sem(self.S2))
+        wait_bytes(self.r3, self.sem(self.S3))
+        if len(self.zlist) == Z:
+            wait_bytes(self.r4.at[pl.ds(0, Z - 1)], self.sem(self.S4))
+        else:
+            @pl.when(self.z != self.zlist[0])
+            def _():
+                wait_bytes(self.r4.at[0], self.sem(self.S4))
+
+
+def reduce_shapes(width, ff):
+    n = Z * Y * C
+    every = list(range(Z))
+    half = width // X
+    wide = ff // X
+    shapes = [("d", width // n, wide, k * (wide // 2), wide // 2, every, k * (wide // 2)) for k in range(2)]
+    shapes += [("u", ff // n, half, 0, half, [k], 0) for k in range(Z)]
+    shapes += [("p", width // n, half, 0, half, every, 0)]
+    shapes += [("q", 3 * width // n, half, 0, half, [k], 0) for k in range(Z)]
+    return shapes
+
+
+def backward_kernel(*refs):
+    names = (
+        "len_ref", "deal_ref", "wq_i", "wp_i", "wu_i", "wd_i", "xr_i", "gw_i", "qs_i", "ka_i", "va_i", "at_i",
+        "lse_i", "r_i", "a2_i", "hd_i", "gp_i", "vec_i", "out_i", "og_q", "og_p", "og_u", "og_d", "osum", "ret",
+        "out_n", "wq", "wp", "xr", "g", "qs", "ka", "va", "at", "lse", "r", "a2", "vec", "gt", "d2", "dr", "drl",
+        "do", "gq", "gp_", "gu", "gd", "wd_t", "wu_t", "hd_t", "gp_t", "dka", "dva", "own_v", "sv", "rk", "rv", "dm",
+        "vs", "vr", "bub", "lsem", "tsem", "rsem", "msem", "vsem",
+    )
+    env = dict(zip(names, refs[: len(names)]))
+    env.update(a1=env["a2"], own_k=env["d2"], sk=env["drl"], dx=env["do"])
+    bufs = refs[len(names):]
+    e = type("Refs", (), env)
+    where = coords()
+    z, y, c, x, d = where
+    rows, width = e.g.shape
+    ff = e.hd_i.shape[1]
+    qrows = rows // 2
+    pairs = width // 128
+    tile = 256
+    lrows = 128
+    steps = width // tile
+    quarters = (c, 3 - c)
+    theirs = (1 - c, 2 + c)
+
+    def at_quarter(k):
+        return pl.ds(mult(k * qrows, qrows), qrows)
+
+    enter(Z * Y * C * X)
+
+    loads = {}
+    for k, (src, dst) in enumerate(
+        (
+            ("gw_i", "g"), ("a2_i", "a2"), ("r_i", "r"), ("vec_i", "vec"), ("wp_i", "wp"), ("at_i", "at"),
+            ("qs_i", "qs"), ("ka_i", "ka"), ("va_i", "va"), ("lse_i", "lse"), ("xr_i", "xr"), ("wq_i", "wq"),
+        )
+    ):
+        loads[dst] = pltpu.make_async_copy(env[src], env[dst], e.lsem.at[k])
+
+    def tile_of(idx):
+        block = idx // 3
+        return (block % 2) * 2 * 3 + (block // 2) * 3 + idx % 3
+
+    def tile_copies(idx):
+        n = tile_of(idx)
+        slot = idx % 2
+        cut = pl.ds(mult(n * tile, tile), tile)
+        return (
+            pltpu.make_async_copy(e.wd_i.at[:, cut], e.wd_t.at[slot], e.tsem.at[0, slot]),
+            pltpu.make_async_copy(e.gp_i.at[:, cut], e.gp_t.at[slot], e.tsem.at[1, slot]),
+            pltpu.make_async_copy(e.hd_i.at[:, cut], e.hd_t.at[slot], e.tsem.at[2, slot]),
+            pltpu.make_async_copy(e.wu_i.at[cut, :], e.wu_t.at[slot], e.tsem.at[3, slot]),
+        )
+
+    loads["g"].start()
+    for cp in tile_copies(0):
+        cp.start()
+    loads["a2"].start()
+    for name in ("r", "vec", "wp", "at", "qs", "ka", "va", "lse", "xr", "wq"):
+        loads[name].start()
+
+    for i in range(2):
+        same = jnp.logical_and(x == c, x == i)
+        src = e.out_i.at[pl.ds(i * qrows, qrows)]
+        dst = e.out_n.at[pl.ds(mult(((i + c) % 2) * qrows, qrows), qrows)]
+
+        @pl.when(same)
+        def _(src=src, dst=dst):
+            pltpu.make_async_copy(src, dst, e.msem.at[1]).start()
+
+        @pl.when(jnp.logical_not(same))
+        def _(src=src, dst=dst, i=i):
+            rcopy(src, dst, e.msem.at[0], e.msem.at[1], dev(z, y, x, i)).start()
+
+    grads = {"q": (e.gq, e.og_q), "p": (e.gp_, e.og_p), "u": (e.gu, e.og_u), "d": (e.gd, e.og_d)}
+    chunks = []
+    for k, (name, R, step, c0, cn, zlist, oc) in enumerate(reduce_shapes(width, ff)):
+        grad, out = grads[name]
+        chunks.append(Reduce(grad, R, step, c0, cn, zlist, bufs[4 * k:4 * k + 4], out, oc, e.rsem, k, where))
+    dA, dB, u0, u1, u2, u3, pj, q0, q1, q2, q3 = chunks
+
+    my_len = live_length(e.len_ref, e.deal_ref, (z * Y + y) * C + x)
+    rowpos = lax.broadcasted_iota(jnp.int32, (lrows, 1), 0)
+    loads["g"].wait()
+    blank = jnp.zeros((1, width), F32)
+    total_bd = blank
+    for k in range(rows // lrows):
+        base = quarters[k * lrows // qrows] * qrows + (k * lrows) % qrows
+        live = base + rowpos < my_len
+        part = jnp.where(live, e.g[k * lrows:(k + 1) * lrows, :], jnp.zeros((), BF))
+        e.g[k * lrows:(k + 1) * lrows, :] = part
+        e.gt[:, k * lrows:(k + 1) * lrows] = part.T
+        total_bd = total_bd + jnp.sum(part.astype(F32), axis=0, keepdims=True)
+    e.d2[...] = jnp.zeros_like(e.d2)
+    loads["a2"].wait()
+
+    ff_tiles = ff // tile
+    plan = {
+        2: [u0.start], 3: [u0.tick2], 5: [u2.start, dA.start, u0.tick3], 7: [u0.tick4, u2.tick2],
+        8: [u1.start, dA.tick2], 9: [u2.tick3], 10: [dA.tick3], 11: [u3.start, dB.start, u2.tick4],
+    }
+
+    def ffn(idx, carry):
+        slot = idx % 2
+        n = tile_of(idx)
+        cut = pl.ds(mult(n * tile, tile), tile)
+
+        @pl.when(idx + 1 < ff_tiles)
+        def _():
+            for cp in tile_copies(idx + 1):
+                cp.start()
+
+        for cp in tile_copies(idx):
+            cp.wait()
+        du = (e.gp_t[slot].astype(F32) * dot_nn(e.g[...], e.wd_t[slot])).astype(BF)
+        e.bub[n] = jnp.sum(du.astype(F32), axis=0, keepdims=True)
+        e.gd[:, cut] = dot_nn(e.gt[...], e.hd_t[slot]).astype(BF)
+        e.gu[cut, :] = dot_tn(du, e.a2[...]).astype(BF)
+        e.d2[...] += dot_nn(du, e.wu_t[slot])
+        for at_idx, acts in plan.items():
+            @pl.when(idx == at_idx)
+            def _(acts=acts):
+                for act in acts:
+                    act()
+        return carry
+
+    lax.fori_loop(0, ff_tiles, ffn, 0)
+
+    loads["r"].wait()
+    loads["vec"].wait()
+
+    def norm_two(k, sums):
+        at_rows = pl.ds(mult(k * lrows, lrows), lrows)
+        n2, rstd = norm_parts(e.r[at_rows, :])
+        da = e.d2[at_rows, :]
+        ee = da * e.vec[G2:G2 + 1, :]
+        gg = e.g[at_rows, :].astype(F32)
+        m1 = jnp.mean(ee, axis=-1, keepdims=True)
+        m2 = jnp.mean(ee * n2, axis=-1, keepdims=True)
+        dr = gg + (ee - m1 - n2 * m2) * rstd
+        e.dr[at_rows, :] = dr
+        e.drl[at_rows, :] = dr.astype(BF)
+        return (
+            sums[0] + jnp.sum(da * n2, axis=0, keepdims=True),
+            sums[1] + jnp.sum(da, axis=0, keepdims=True),
+            sums[2] + jnp.sum(dr, axis=0, keepdims=True),
+        )
+
+    sum_g2, sum_c2, sum_bp = lax.fori_loop(0, rows // lrows, norm_two, (blank, blank, blank))
+    u1.tick2()
+    dA.tick4()
+
+    loads["wp"].wait()
+    loads["at"].wait()
+
+    def proj_back(n, carry):
+        cut = pl.ds(mult(n * tile, tile), tile)
+        e.do[:, cut] = dot_nn(e.drl[...], e.wp[:, cut]).astype(BF)
+        e.gp_[cut, :] = dot_tn(e.drl[:, cut], e.at[...]).astype(BF)
+        return carry
+
+    lax.fori_loop(0, steps, proj_back, 0)
+    pj.start()
+    u1.tick3()
+    u3.tick2()
+
+    for name in ("qs", "ka", "va", "lse"):
+        loads[name].wait()
+    lane = lax.broadcasted_iota(jnp.int32, (qrows, 128), 1)
+    kpos = lax.broadcasted_iota(jnp.int32, (qrows, qrows), 0)
+    qpos = lax.broadcasted_iota(jnp.int32, (qrows, qrows), 1)
+
+    def split(v):
+        zero = jnp.zeros_like(v)
+        return jnp.where(lane < HEAD_DIM, v, zero), jnp.where(lane >= HEAD_DIM, v, zero)
+
+    def pair_body(p, carry):
+        lanes = pl.ds(mult(p * 128, 128), 128)
+        e.dka[...] = jnp.zeros_like(e.dka)
+        e.dva[...] = jnp.zeros_like(e.dva)
+        for i in range(2):
+            quarter = quarters[i]
+            own = slice(i * qrows, (i + 1) * qrows)
+            qp, dop = e.qs[own, lanes], e.do[own, lanes]
+            qh, doh = split(qp), split(dop)
+            qq, dd = jnp.concatenate(qh, axis=0), jnp.concatenate(doh, axis=0)
+            prod = (dop.astype(F32) * e.at[own, lanes].astype(F32)).T
+            delta = [jnp.sum(prod[h * HEAD_DIM:(h + 1) * HEAD_DIM], axis=0, keepdims=True) for h in range(2)]
+            logs = [e.lse[p, i * 2 + h:i * 2 + h + 1, :] for h in range(2)]
+
+            def keys(j, dq):
+                at_keys = pl.ds(mult(j * qrows, qrows), qrows)
+                kj, vj = e.ka[at_keys, lanes], e.va[at_keys, lanes]
+                kt = kj.T
+                keep_it = jnp.logical_or(kpos <= qpos, j < quarter)
+                probs, grads_s, new = [], [], []
+                for h in range(2):
+                    s = jnp.where(keep_it, dot_nt(kj, qh[h]), NEG_BIG)
+                    pt = jnp.exp(s - logs[h])
+                    ds = (pt * (dot_nt(vj, doh[h]) - delta[h])).astype(BF)
+                    probs.append(pt.astype(BF))
+                    grads_s.append(ds)
+                    new.append(dq[h] + dot_nn(kt[h * HEAD_DIM:(h + 1) * HEAD_DIM], ds))
+                e.dva[at_keys, :] += dot_nn(jnp.concatenate(probs, axis=1), dd)
+                e.dka[at_keys, :] += dot_nn(jnp.concatenate(grads_s, axis=1), qq)
+                return tuple(new)
+
+            none = jnp.zeros((HEAD_DIM, qrows), F32)
+            dq = lax.fori_loop(0, quarter + 1, keys, (none, none))
+            e.dm[own, lanes] = (jnp.concatenate(dq, axis=0).T * HEAD_DIM ** -0.5).astype(BF)
+        for i in range(2):
+            own = slice(i * qrows, (i + 1) * qrows)
+            e.own_k[own, lanes] = e.dka[at_quarter(quarters[i]), :]
+            e.own_v[own, lanes] = e.dva[at_quarter(quarters[i]), :]
+            e.sk[own, lanes] = e.dka[at_quarter(theirs[i]), :].astype(BF)
+            e.sv[own, lanes] = e.dva[at_quarter(theirs[i]), :].astype(BF)
+        return carry
+
+    between = [[dB.tick2, u1.tick4, u3.tick3, pj.tick2], [dB.tick3, u3.tick4, pj.tick3], [dB.tick4, pj.tick4]]
+    for k in range(3):
+        lax.fori_loop(2 * k, 2 * k + 2, pair_body, 0)
+        for act in between[k]:
+            act()
+        cut = slice(2 * k * 128, (2 * k + 2) * 128)
+        for src, dst, s in ((e.sk, e.rk, 2), (e.sv, e.rv, 4)):
+            rcopy(src.at[:, cut], dst.at[:, cut], e.msem.at[s], e.msem.at[s + 1], dev(z, y, 1 - c, x)).start()
+
+    loads["xr"].wait()
+
+    def norm_one(k, carry):
+        at_rows = pl.ds(mult(k * lrows, lrows), lrows)
+        n1, _ = norm_parts(e.xr[at_rows, :].astype(F32))
+        e.a1[at_rows, :] = (n1 * e.vec[G1:G1 + 1, :] + e.vec[C1:C1 + 1, :]).astype(BF)
+        return carry
+
+    lax.fori_loop(0, rows // lrows, norm_one, 0)
+
+    def qkv_grad(n, carry):
+        cut = pl.ds(mult(n * tile, tile), tile)
+        e.gq[cut, :] = dot_tn(e.dm[:, cut], e.a1[...]).astype(BF)
+        return carry
+
+    lax.fori_loop(0, 3, qkv_grad, 0)
+    q0.start()
+    wait_bytes(e.rk, e.msem.at[3])
+    wait_bytes(e.rv, e.msem.at[5])
+    for part, (mine, got) in enumerate(((e.own_k, e.rk), (e.own_v, e.rv))):
+        def merge(k, carry, part=part, mine=mine, got=got):
+            at_rows = pl.ds(mult(k * lrows, lrows), lrows)
+            e.dm[at_rows, (part + 1) * width:(part + 2) * width] = (
+                mine[at_rows, :] + got[at_rows, :].astype(F32)
+            ).astype(BF)
+            return carry
+
+        lax.fori_loop(0, rows // lrows, merge, 0)
+    lax.fori_loop(3, 5, qkv_grad, 0)
+    q1.start()
+    q0.tick2()
+    lax.fori_loop(5, 7, qkv_grad, 0)
+    q2.start()
+    q1.tick2()
+    lax.fori_loop(7, 9, qkv_grad, 0)
+    q3.start()
+    q0.tick3()
+    q2.tick2()
+
+    loads["wq"].wait()
+
+    def input_back(n, carry):
+        cut = pl.ds(mult(n * tile, tile), tile)
+        e.d2[:, cut] = dot_nn(e.dm[...], e.wq[:, cut])
+        return carry
+
+    lax.fori_loop(0, steps, input_back, 0)
+    q1.tick3()
+    q3.tick2()
+
+    def norm_one_back(k, sums):
+        at_rows = pl.ds(mult(k * lrows, lrows), lrows)
+        n1, rstd = norm_parts(e.xr[at_rows, :].astype(F32))
+        da = e.d2[at_rows, :]
+        ee = da * e.vec[G1:G1 + 1, :]
+        m1 = jnp.mean(ee, axis=-1, keepdims=True)
+        m2 = jnp.mean(ee * n1, axis=-1, keepdims=True)
+        e.dx[at_rows, :] = (e.dr[at_rows, :] + (ee - m1 - n1 * m2) * rstd).astype(BF)
+        return sums[0] + jnp.sum(da * n1, axis=0, keepdims=True), sums[1] + jnp.sum(da, axis=0, keepdims=True)
+
+    sum_g1, sum_c1 = lax.fori_loop(0, rows // lrows, norm_one_back, (blank, blank))
+
+    e.vs[0] = jnp.zeros_like(e.vs[0])
+    for row, value in ((G1, sum_g1), (C1, sum_c1), (BP, sum_bp), (G2, sum_g2), (C2, sum_c2), (BD, total_bd)):
+        e.vs[0, row:row + 1, :] = value
+    per = width // tile
+    for k in range(ff_tiles):
+        e.vs[0, BU + k // per:BU + k // per + 1, (k % per) * tile:(k % per + 1) * tile] = e.bub[k]
+    hops = (
+        dev(z, y, 1 - c, x), dev(z, y, c, 1 - x), dev(z, 1 - y, c, x),
+        dev(z + 1 - 2 * (z % 2), y, c, x), dev((z + 2) % 4, y, c, x),
+    )
+
+    def hop(k):
+        rcopy(e.vs.at[k], e.vr.at[k], e.vsem.at[0, k], e.vsem.at[1, k], hops[k]).start()
+
+    def land(k):
+        wait_bytes(e.vr.at[k], e.vsem.at[1, k])
+        e.vs[k + 1] = e.vs[k] + e.vr[k]
+
+    hop(0)
+
+    small = e.ret.shape[1]
+    per_quarter = qrows // small
+    slot = (z * Y + y) * C + x
+    for i in range(2):
+        def give_back(b, carry, i=i):
+            td = ((i + c) % 2) * per_quarter + b
+            src = e.dx.at[pl.ds(mult(i * qrows + b * small, small), small)]
+            mine = jnp.logical_and(td == d, x == i)
+
+            @pl.when(mine)
+            def _():
+                pltpu.make_async_copy(src, e.ret.at[slot], e.msem.at[7]).start()
+
+            @pl.when(jnp.logical_not(mine))
+            def _():
+                rcopy(src, e.ret.at[slot], e.msem.at[6], e.msem.at[7], {"dp": td, "cp": i}).start()
+
+            return carry
+
+        lax.fori_loop(0, per_quarter, give_back, 0)
+
+    q2.tick3()
+    land(0)
+    hop(1)
+    q0.tick4()
+    q3.tick3()
+    land(1)
+    hop(2)
+    q1.tick4()
+    q2.tick4()
+    for ch in (u0, u1, u2, u3, dA, dB, pj):
+        ch.tick5()
+    land(2)
+    hop(3)
+    q3.tick4()
+    land(3)
+    hop(4)
+    for ch in (q0, q1, q2, q3):
+        ch.tick5()
+    land(4)
+    e.osum[...] = e.vs[5]
+
+    for ch in chunks:
+        ch.drain()
+    for k in range(5):
+        wait_bytes(e.vr.at[k], e.vsem.at[0, k])
+    wait_bytes(e.rk, e.msem.at[2])
+    wait_bytes(e.rv, e.msem.at[4])
+
+    @pl.when((x + c) % 2 == d // per_quarter)
+    def _():
+        wait_bytes(e.dx.at[pl.ds(0, rows - small)], e.msem.at[6])
+
+    @pl.when((x + c) % 2 != d // per_quarter)
+    def _():
+        wait_bytes(e.dx, e.msem.at[6])
+
+    wait_bytes(e.dx, e.msem.at[7])
+
+    @pl.when(c == x)
+    def _():
+        wait_bytes(e.dx.at[pl.ds(0, qrows)], e.msem.at[0])
+
+    @pl.when(c != x)
+    def _():
+        wait_bytes(e.dx, e.msem.at[0])
+
+    wait_bytes(e.dx, e.msem.at[1])
+
+
+def backward(lengths, dealing, saved, shards):
+    wq, wp, wu, wd, xr, gw, qs, ka, va, at, lse, r, a2, hd, gp, vec, outw = saved
+    rows, width = xr.shape
+    ff = hd.shape[1]
+    n = Z * Y * C
+    keys = ka.shape[0]
+    small = rows // n
+    pairs = width // 128
+
+    def arr(shape, dtype=BF):
+        return jax.ShapeDtypeStruct(shape, dtype)
+
+    outs = [arr(s.shape, F32) for s in shards] + [
+        arr((16, width), F32), arr((n, small, width)), arr((rows, width)),
+    ]
+    vm = pltpu.VMEM
+    acts = vm((rows, width), BF)
+    acts32 = vm((rows, width), F32)
+    scratch = [
+        vm(wq.shape, BF), vm(wp.shape, BF), acts, acts, acts, vm(ka.shape, BF), vm(va.shape, BF), acts,
+        vm(lse.shape, F32), acts32, acts, vm(vec.shape, F32), vm((width, rows), BF), acts32, acts32, acts, acts,
+        vm(wq.shape, BF), vm(wp.shape, BF), vm(wu.shape, BF), vm(wd.shape, BF),
+        vm((2, width, 256), BF), vm((2, 256, width), BF), vm((2, rows, 256), BF), vm((2, rows, 256), BF),
+        vm((keys, 128), F32), vm((keys, 128), F32),
+        acts32, acts, acts, acts, vm((rows, 3 * width), BF),
+        vm((6, 16, width), F32), vm((5, 16, width), F32), vm((ff // 256, 1, 256), F32),
+        pltpu.SemaphoreType.DMA((12,)), pltpu.SemaphoreType.DMA((4, 2)), pltpu.SemaphoreType.DMA((11, 8)),
+        pltpu.SemaphoreType.DMA((8,)), pltpu.SemaphoreType.DMA((2, 5)),
+    ]
+    for _, R, _, _, cn, zlist, _ in reduce_shapes(width, ff):
+        k = len(zlist)
+        scratch += [vm((2 * k, 2, R, cn), BF), vm((2 * k, R, cn), BF), vm((k, R, cn), BF), vm((Z, R, cn), BF)]
+    anyspec = pl.BlockSpec(memory_space=pl.ANY)
+    smem = pl.BlockSpec(memory_space=pltpu.SMEM)
+    vmem = pl.BlockSpec(memory_space=pltpu.VMEM)
+    return pl.pallas_call(
+        backward_kernel,
+        out_shape=outs,
+        in_specs=[smem, smem] + [anyspec] * len(saved),
+        out_specs=[vmem] * 5 + [anyspec] * 2,
+        scratch_shapes=scratch,
+        compiler_params=pltpu.CompilerParams(
+            collective_id=1, has_side_effects=True, vmem_limit_bytes=67043328
+        ),
+        name="backward",
+    )(lengths, dealing, *saved)
+
+
+def slice_plan(
+    x_source, cotangent, lengths, dealing, qkv_weight, proj_weight, up_weight, down_weight,
+    first_gain, first_shift, proj_bias, second_gain, second_shift, up_bias, down_bias,
+):
+    slots = dealing.shape[0]
+    width = x_source.shape[2]
+    n = Z * Y * C
+    d = lax.axis_index("dp")
+    owners = jnp.sum(
+        jnp.where(dealing[None, :] == jnp.arange(slots)[:, None], jnp.arange(slots)[None, :], 0), axis=1
+    )
+    xg = x_source[owners]
+    shards = [w.astype(BF).T for w in (qkv_weight, proj_weight, up_weight, down_weight)]
+    seven = jnp.stack([first_gain, first_shift, proj_bias, second_gain, second_shift, down_bias]).astype(BF)
+    own = seven.shape[1]
+    place = jnp.arange(width) // own
+    table = jnp.where(place == d, jnp.tile(seven, (1, n)), jnp.zeros((), BF))
+    long = up_bias.astype(BF)
+    wide = jnp.where(jnp.arange(long.shape[0] * n) // long.shape[0] == d, jnp.tile(long, n), jnp.zeros((), BF))
+    sv = jnp.concatenate([table, wide.reshape(-1, width), jnp.zeros((16 - 6 - wide.shape[0] // width, width), BF)])
+    saved = forward(lengths, dealing, xg, cotangent[0], *shards, sv)
+    gq, gp, gu, gd, sums, ret, out = backward(lengths, dealing, saved, shards)
+    input_grad = ret[dealing]
+    picked = lax.dynamic_slice_in_dim(sums[:6].reshape(6, n, own), d, 1, axis=1)[:, 0]
+    long_sum = lax.dynamic_slice_in_dim(sums[BU:BU + wide.shape[0] // width].reshape(-1), d * long.shape[0], long.shape[0])
+    return (
+        out[None], input_grad, gq.T, gp.T, gu.T, gd.T,
+        picked[G1], picked[C1], picked[BP], picked[G2], picked[C2], long_sum, picked[BD],
+    )
 
 
 def layer_norm(values, scaling, offset):
@@ -138,7 +1269,7 @@
     return jnp.einsum("sqd,sqe->de", left, right, preferred_element_type=jnp.float32)
 
 
-def local(
+def general(
     x_source,
     cotangent,
     lengths,
@@ -403,4 +1534,6 @@
         P("dp"),
         P("dp"),
     )
+    planned = tuple(mesh.shape.items()) == (("dp", Z * Y * C), ("cp", X))
+    local = slice_plan if planned else general
     return jax.shard_map(local, mesh=mesh, in_specs=in_specs, out_specs=out_specs, check_vma=False)

time: 751 us -> 273 us (0.36)
  waiting for transfers between devices: 320 us -> 0 us
  Pallas kernels: 0 us -> 247 us
  blocking collectives: 164 us -> 0 us
  matrix products: 132 us -> 0 us
  other arithmetic: 53.6 us -> 11.3 us
  local copies, waits for them, and re-layouts: 44 us -> 13.1 us
  between operations: 17.6 us -> 0.75 us
  starting transfers between devices: 11.2 us -> 0 us
    pallas_call x0 -> x2, Pallas kernels: none -> 247 us  [the longest x1 124 us: backward(): pl.pallas_call(backward_kernel, out_shape=outs, in_specs=[smem, smem] + [...]
    reduce_scatter x7 -> x0, waiting for transfers between devices: 182 us -> none  [the longest x1 72 us: local(): lax.psum_scatter(grad_up.astype(jnp.bfloat16), 'dp', scatter_dimension=1,...]
    dot_general x18 -> x0, matrix products: 132 us -> none  [the longest x4 22.8 us: mat_back(): jnp.einsum('sqe,de->sqd', left, right, preferred_element_type=jnp.float32)]
    unnamed x2 -> x0, blocking collectives: 128 us -> none
    all_gather x5 -> x0, waiting for transfers between devices: 113 us -> none  [the longest x1 47.1 us: fetch_weights(): lax.all_gather(down_part, 'dp', axis=1, tiled=True)]
    all_gather x4 -> x0, blocking collectives: 30.8 us -> none  [the longest x1 9.79 us: fetch_weights(): lax.all_gather(up_weight.astype(jnp.bfloat16), 'cp', axis=0, tiled=True)]
    unnamed x18 -> x0, waiting for transfers between devices: 24.3 us -> none
    convert_element_type x27 -> x1, other arithmetic: 22.3 us -> 0.68 us  [slice_plan(): long = up_bias.astype(BF)]
  transfers between devices with their start and end apart: 17 -> 0, of which waited for: 12 -> 0; matrix products, arithmetic and copies ran while one was open for 25% -> 0% of each run, Pallas kernels for 0% -> 0%
where the time goes in v1:
time: 273 us; the launch traced here: 272 us
  Pallas kernels  247 us (90%)
  local copies, waits for them, and re-layouts  13.1 us (5%)
  other arithmetic  11.3 us (4%)
    pallas_call x1, Pallas kernels, backward(): pl.pallas_call(backward_kernel, out_shape=outs, in_specs=[smem, smem] + [...  124 us
    pallas_call x1, Pallas kernels, forward(): pl.pallas_call(forward_kernel, out_shape=outs, in_specs=[smem, smem] + [a...  123 us
    transpose x4, other arithmetic, slice_plan(): w.astype(BF)  6.37 us

profile of v1, /device:TPU:0, one launch (start us, length us, event | category | flops | bytes accessed | tf_op | source)
XLA Modules:
  0.0 272.1 jit_solution(10625181008701705533)
XLA Ops:
  0.6 0.7 convert_bitcast_fusion.4
  1.3 0.7 convert_bitcast_fusion.6
  2.0 0.7 convert_bitcast_fusion.8
  2.7 0.1 tile.21
  2.9 0.7 convert_element_type.24
  3.5 0.1 tile.23
  3.7 0.6 pad_maximum_fusion.sv
  4.3 0.8 select_reduce_fusion
  5.1 2.6 gather_fusion
  7.7 1.6 convert_bitcast_fusion.sd
  9.3 1.6 convert_bitcast_fusion.1.su
  11.0 1.6 convert_bitcast_fusion.2.sq
  12.6 1.5 convert_bitcast_fusion.3.sp
  14.1 123.0 %forward.1 = (bf16[2304,768]{1,0:T(8,128)(2,1)}, bf16[768,768]{1,0:T(8,128)(2,1)}, bf16[3072,768]{1,0:T(8,128)(2,1)}, bf16[768,3072]{1,0:T(8,128)(2,1)}, bf16[51...) custom-call(s32[16]{0:T(128)} %refs_0_.1, ...), custom_call_target="tpu_custom_call" | custom-call | tf_op jit(solution)/shard_map/forward/pallas_call | solution.py:549
  137.1 124.0 %backward.1 = (f32[144,384]{1,0:T(8,128)}, f32[48,384]{1,0:T(8,128)}, f32[192,384]{1,0:T(8,128)}, f32[48,1536]{1,0:T(8,128)}, f32[16,768]{1,0:T(8,128)}, /*index...) custom-call(s32[16]{0:T(128)} %refs_0_.1, s32[16]{0:T(128)} %refs_1_.1, bf16[2304,768]{1,0:T(8,128)(2,1)} %get-tuple-element.37.refs_2_, ...), custom_call_target="tpu_custom_call" | custom-call | tf_op jit(solution)/shard_map/backward/pallas_call | solution.py:1105
  261.0 0.0 copy-start.2
  261.1 0.0 copy-start.3
  261.1 0.0 copy-start.1
  261.1 0.7 compare_select_fusion
  261.8 2.6 gather_fusion.1
  264.4 0.7 slice.30
  265.2 0.1 reshape.123
  265.3 0.6 fusion.7
  265.8 0.8 slice.36
  266.6 0.6 dynamic_slice.7
  267.3 2.1 copy.33
  269.3 0.0 copy-done.2
  269.3 0.7 copy.34
  270.0 0.0 copy-done.3
  270.0 0.6 copy.35
  270.7 0.7 copy.36
  271.4 0.7 copy.37
  (14 shorter events, 0.2 us)
Async XLA Ops:
  261.0 8.3 %copy-start.2 = (f32[144,384]{1,0:T(8,128)S(1)}, f32[144,384]{1,0:T(8,128)}, u32[]{:S(2)}) copy-start(f32[144,384]{1,0:T(8,128)} %get-tuple-element.56) | copy-start | bytes 663556
  261.1 9.0 %copy-start.3 = (f32[48,384]{1,0:T(8,128)S(1)}, f32[48,384]{1,0:T(8,128)}, u32[]{:S(2)}) copy-start(f32[48,384]{1,0:T(8,128)} %get-tuple-element.57) | copy-start | bytes 221188
  261.1 9.6 %copy-start.1 = (f32[192,384]{1,0:T(8,128)S(1)}, f32[192,384]{1,0:T(8,128)}, u32[]{:S(2)}) copy-start(f32[192,384]{1,0:T(8,128)} %get-tuple-element.58) | copy-start | bytes 884740
  261.1 10.3 %copy-start = (f32[48,1536]{1,0:T(8,128)S(1)}, f32[48,1536]{1,0:T(8,128)}, u32[]{:S(2)}) copy-start(f32[48,1536]{1,0:T(8,128)} %get-tuple-element.59) | copy-start | bytes 884740

commit v2 on v1

--- a/solution.py
+++ b/solution.py
@@ -43,6 +43,10 @@
     )
 
 
+def lcopy(src, dst, sem):
+    return pltpu.make_async_copy(src, dst, sem)
+
+
 def wait_bytes(ref, sem):
     pltpu.make_async_copy(ref, ref, sem).wait()
 
@@ -63,7 +67,11 @@
         return carry
 
     lax.fori_loop(0, everyone, greet, 0)
-    pl.semaphore_wait(barrier, everyone - 1)
+
+    def entered():
+        pl.semaphore_wait(barrier, everyone - 1)
+
+    return entered
 
 
 def dot_nn(a, b):
@@ -94,8 +102,8 @@
 
 
 class Piece:
-    def __init__(self, full, shard, R, r0, rn, step, c0, cn):
-        self.full, self.shard = full, shard
+    def __init__(self, full, R, r0, rn, step, c0, cn):
+        self.full = full
         self.R, self.r0, self.rn, self.step, self.c0, self.cn = R, r0, rn, step, c0, cn
 
     def at(self, z, y, c, x):
@@ -104,19 +112,17 @@
             pl.ds(mult(d * self.R + self.r0, 16), self.rn), pl.ds(mult(x * self.step + self.c0, 128), self.cn)
         ]
 
-    def own(self):
-        return self.shard.at[pl.ds(self.r0, self.rn), pl.ds(self.c0, self.cn)]
-
 
 class Gather:
-    LOC, ZS, ZR, S2, R2, S3, R3, S4, R4 = range(9)
-
-    def __init__(self, piece, sems, k, dummy, where):
+    ZS, ZR, S2, R2, S3, R3, S4, R4 = range(8)
+
+    def __init__(self, piece, sems, k, dummy, where, turned):
         self.p, self.sems, self.k, self.dummy = piece, sems, k, dummy
         z, y, c, x, _ = where
         self.z, self.y, self.c, self.x = z, y, c, x
-        self.y2, self.x2 = (y + 1 - c) % 2, (x + c) % 2
-        self.y3, self.x3 = (y + c) % 2, (x + 1 - c) % 2
+        self.o = o = 1 if turned else c
+        self.y2, self.x2 = (y + 1 - o) % 2, (x + o) % 2
+        self.y3, self.x3 = (y + o) % 2, (x + 1 - o) % 2
 
     def sem(self, which):
         return self.sems.at[self.k, which]
@@ -127,14 +133,13 @@
 
     def start(self):
         p, z, y, c, x = self.p, self.z, self.y, self.c, self.x
-        pltpu.make_async_copy(p.own(), p.at(z, y, c, x), self.sem(self.LOC)).start()
+        own = p.at(z, y, c, x)
         for dz in range(1, Z):
             z2 = (z + dz) % Z
-            rcopy(p.own(), p.at(z, y, c, x), self.sem(self.ZS), self.sem(self.ZR), dev(z2, y, c, x)).start()
+            rcopy(own, own, self.sem(self.ZS), self.sem(self.ZR), dev(z2, y, c, x)).start()
 
     def tick2(self):
         p, z, y, c, x = self.p, self.z, self.y, self.c, self.x
-        self.wait(1, self.LOC)
         self.wait(Z - 1, self.ZR)
         for zz in range(Z):
             q = p.at(zz, y, c, x)
@@ -157,8 +162,8 @@
         self.wait(2 * Z, self.R3)
         for zz in range(Z):
             for which in range(2):
-                yy = which * (1 - c) + (1 - y) * c
-                xx = (1 - x) * (1 - c) + which * c
+                yy = which * (1 - self.o) + (1 - y) * self.o
+                xx = (1 - x) * (1 - self.o) + which * self.o
                 q = p.at(zz, yy, c, xx)
                 rcopy(q, q, self.sem(self.S4), self.sem(self.R4), dev(z, y, 1 - c, x)).start()
 
@@ -173,27 +178,26 @@
 
 
 class Vectors:
-    LOC, ZS, ZR, S2, R2, S4, R4 = range(7)
-
-    def __init__(self, full, shard, sems, where):
-        self.full, self.shard, self.sems, self.where = full, shard, sems, where
+    ZS, ZR, S2, R2, S4, R4 = range(6)
+
+    def __init__(self, full, sems, where):
+        self.full, self.sems, self.where = full, sems, where
 
     def at(self, z, y, c):
         return self.full.at[(z * Y + y) * C + c]
 
     def start(self):
         z, y, c, x, _ = self.where
-        pltpu.make_async_copy(self.shard, self.at(z, y, c), self.sems.at[self.LOC]).start()
+        own = self.at(z, y, c)
         for dz in range(1, Z):
             z2 = (z + dz) % Z
-            rcopy(self.shard, self.at(z, y, c), self.sems.at[self.ZS], self.sems.at[self.ZR], dev(z2, y, c, x)).start()
+            rcopy(own, own, self.sems.at[self.ZS], self.sems.at[self.ZR], dev(z2, y, c, x)).start()
 
     def wait(self, count, which):
         wait_bytes(self.full.at[pl.ds(0, count)], self.sems.at[which])
 
     def tick2(self):
         z, y, c, x, _ = self.where
-        self.wait(1, self.LOC)
         self.wait(Z - 1, self.ZR)
         for zz in range(Z):
             q = self.at(zz, y, c)
@@ -219,27 +223,35 @@
 G1, C1, BP, G2, C2, BD, BU = range(7)
 
 
-def gather_chunks(wq, wp, wu, wd, sq, sp, su, sd):
-    rq, rp, ru, rd = sq.shape[0], sp.shape[0], su.shape[0], sd.shape[0]
-    half, wide = sq.shape[1], sd.shape[1]
+def gather_chunks(wq, wp, wu, wd):
+    rq, rp, ru, rd = (w.shape[0] // (Z * Y * C) for w in (wq, wp, wu, wd))
+    half, wide = wq.shape[1] // X, wd.shape[1] // X
     out = []
     for k in range(3):
-        out.append(Piece(wq, sq, rq, k * (rq // 3), rq // 3, half, 0, half))
-    out.append(Piece(wp, sp, rp, 0, rp, half, 0, half))
+        out.append(Piece(wq, rq, k * (rq // 3), rq // 3, half, 0, half))
+    out.append(Piece(wp, rp, 0, rp, half, 0, half))
     for k in range(4):
-        out.append(Piece(wu, su, ru, k * (ru // 4), ru // 4, half, 0, half))
+        out.append(Piece(wu, ru, k * (ru // 4), ru // 4, half, 0, half))
     for k in range(4):
-        out.append(Piece(wd, sd, rd, 0, rd, wide, k * (wide // 4), wide // 4))
+        out.append(Piece(wd, rd, 0, rd, wide, k * (wide // 4), wide // 4))
     return out
 
 
+def one_hot(count, width, first):
+    at_row = lax.broadcasted_iota(jnp.int32, (count, width), 0)
+    at_col = lax.broadcasted_iota(jnp.int32, (count, width), 1)
+    return (at_col == at_row + first).astype(BF)
+
+
 N_GATHER = 12
+TURNED = (7, 9, 11)
+COT_STEPS = (5, 7)
 
 
 def forward_kernel(
-    len_ref, deal_ref, xg, cot, sq, sp, su, sd, sv,
+    len_ref, deal_ref, cot, x_in, sq, sp, su, sd, v_g1, v_c1, v_bp, v_g2, v_c2, v_bd, v_bu,
     wq_o, wp_o, wu_o, wd_o, xr_o, gw_o, qs_o, ka_o, va_o, at_o, lse_o, r_o, a2_o, hd_o, gp_o, vec_o, out_o,
-    wq, wp, wu, wd, xr, a1, qs, ka, va, at, lse, r, a2, hd, gp, vg, vec, bu3, sc0, sc1, outw,
+    wq, wp, wu, wd, xr, a1, qs, ka, va, at, lse, r, a2, hd, gp, vg, vec, bu3, sc0, sc1, outw, xg, acc,
     gsem, vsem, msem, osem,
 ):
     where = coords()
@@ -247,27 +259,69 @@
     width = xr.shape[1]
     rows = xr.shape[0]
     qrows = rows // 2
-    small = xg.shape[1]
+    small = x_in.shape[1]
     pairs = width // 128
     tile = 256
 
-    enter(Z * Y * C * X)
-
-    vectors = Vectors(vg, sv, vsem, where)
+    entered = enter(Z * Y * C * X)
+
+    n = Z * Y * C
+    for shard, full in ((sq, wq), (sp, wp), (su, wu), (sd, wd)):
+        own, long = shard.shape
+        full[pl.ds(mult(d * own, 16), own), pl.ds(mult(x * long, 128), long)] = shard[...].astype(BF)
+    vg[d] = jnp.zeros(vg.shape[1:], BF)
+    own = v_g1.shape[1]
+    seven = jnp.concatenate([v[...] for v in (v_g1, v_c1, v_bp, v_g2, v_c2, v_bd)], axis=0).astype(BF)
+    placed = dot_nn(seven, one_hot(own, width, d * own))
+    long = v_bu.shape[1]
+    per_row = width // long
+    placed_long = dot_nn(v_bu[...].astype(BF), one_hot(long, width, (d % per_row) * long))
+    rows_long = [jnp.where(d // per_row == k, placed_long, 0.0) for k in range(n // per_row)]
+    rest = jnp.zeros((16 - 6 - n // per_row, width), F32)
+    vg[d] = jnp.concatenate([placed] + rows_long + [rest], axis=0).astype(BF)
+    slots = x_in.shape[0]
+    for t in range(slots):
+        owner = jnp.int32(0)
+        for s in range(slots):
+            owner = jnp.where(deal_ref[s] == t, s, owner)
+        xg[t] = x_in[owner]
+
+    entered()
+
+    vectors = Vectors(vg, vsem, where)
     vectors.start()
+    chunks = [
+        Gather(p, gsem, k, wu, where, k in TURNED) for k, p in enumerate(gather_chunks(wq, wp, wu, wd))
+    ]
+
+    def send_cot(b):
+        core_b = (x + b) % 2
+        src_b = cot.at[pl.ds(b * qrows, qrows)]
+        dst_b = gw_o.at[pl.ds(mult(x * qrows, qrows), qrows)]
+        same = jnp.logical_and(core_b == c, c == x)
+
+        @pl.when(same)
+        def _():
+            lcopy(src_b, dst_b, msem.at[3]).start()
+
+        @pl.when(jnp.logical_not(same))
+        def _():
+            rcopy(src_b, dst_b, msem.at[2], msem.at[3], dev(z, y, core_b, c)).start()
+
     per_quarter = qrows // small
     place = mult(x * qrows + (d % per_quarter) * small, 16)
     core_to = (x + d // per_quarter) % 2
     dst = xr.at[pl.ds(place, small)]
 
-    def deal_out(t, carry):
+    def deal_out(k, carry):
+        t = (d + k + x * (slots // 2)) % slots
         td = (t // 2) * 2 + core_to
         tx = t % 2
         mine = jnp.logical_and(td == d, tx == x)
 
         @pl.when(mine)
         def _():
-            pltpu.make_async_copy(xg.at[t], dst, msem.at[1]).start()
+            lcopy(xg.at[t], dst, msem.at[1]).start()
 
         @pl.when(jnp.logical_not(mine))
         def _():
@@ -275,28 +329,27 @@
 
         return carry
 
-    lax.fori_loop(0, xg.shape[0], deal_out, 0)
-    chunks = [
-        Gather(p, gsem, k, wu, where) for k, p in enumerate(gather_chunks(wq, wp, wu, wd, sq, sp, su, sd))
-    ]
-    for ch in chunks:
+    ahead = 2
+    for ch in chunks[:ahead]:
         ch.start()
 
-    vectors.tick2()
-    vectors.tick3()
-
-    order = []
-    for s in range(len(chunks) + 2):
+    def step(s):
+        if s + ahead < len(chunks):
+            chunks[s + ahead].start()
+        if s < 4:
+            lax.fori_loop(s * slots // 4, (s + 1) * slots // 4, deal_out, 0)
+        if s in COT_STEPS:
+            send_cot(COT_STEPS.index(s))
         for back, name in ((0, "tick2"), (1, "tick3"), (2, "tick4")):
             if 0 <= s - back < len(chunks):
-                order.append((s - back, name))
-    pending = [getattr(chunks[k], name) for k, name in order]
-
-    def run(n):
-        for _ in range(n):
-            if pending:
-                pending.pop(0)()
-
+                getattr(chunks[s - back], name)()
+
+    step(0)
+    vectors.tick2()
+    step(1)
+    vectors.tick3()
+    step(2)
+    step(3)
     vectors.tick4()
 
     def add_table(k, acc):
@@ -318,26 +371,11 @@
 
     lax.fori_loop(0, rows // lrows, first_norm, 0)
 
-    run(13)
+    step(4)
     for k in range(3):
         chunks[k].tick5()
     keep = [pltpu.make_async_copy(wq, wq_o, osem.at[0])]
     keep[-1].start()
-
-    def cot_copy(b):
-        return (x + b) % 2, cot.at[pl.ds(b * qrows, qrows)], gw_o.at[pl.ds(mult(x * qrows, qrows), qrows)]
-
-    for b in range(2):
-        core_b, src_b, dst_b = cot_copy(b)
-        same = jnp.logical_and(core_b == c, c == x)
-
-        @pl.when(same)
-        def _(src_b=src_b, dst_b=dst_b):
-            pltpu.make_async_copy(src_b, dst_b, msem.at[3]).start()
-
-        @pl.when(jnp.logical_not(same))
-        def _(src_b=src_b, dst_b=dst_b, core_b=core_b):
-            rcopy(src_b, dst_b, msem.at[2], msem.at[3], dev(z, y, core_b, c)).start()
 
     quarters = (c, 3 - c)
 
@@ -362,7 +400,7 @@
             to = ka if part == 1 else va
             for i in range(2):
                 rcopy(to.at[q_at(i)], to.at[q_at(i)], msem.at[4 + 2 * (part - 1)], msem.at[5 + 2 * (part - 1)], dev(z, y, 1 - c, x)).start()
-        run(1)
+    step(5)
     wait_bytes(ka.at[pl.ds(0, rows)], msem.at[5])
     wait_bytes(va.at[pl.ds(0, rows)], msem.at[7])
     for src, out, s in ((qs, qs_o, 1), (ka, ka_o, 2), (va, va_o, 3), (xr, xr_o, 4), (vec, vec_o, 5)):
@@ -422,7 +460,7 @@
     per = 2
     for k in range(0, pairs, per):
         lax.fori_loop(k, k + per, pair_body, 0)
-        run(5)
+        step(6 + k // per)
 
     chunks[3].tick5()
     for src, out, s in ((wp, wp_o, 6), (at, at_o, 7), (lse, lse_o, 8)):
@@ -444,7 +482,7 @@
         return carry
 
     lax.fori_loop(0, rows // lrows, second_norm, 0)
-    run(2)
+    step(9)
     for k in range(4, 8):
         chunks[k].tick5()
     for src, out, s in ((wu, wu_o, 9), (r, r_o, 10), (a2, a2_o, 11)):
@@ -465,28 +503,38 @@
     blocks = hd.shape[1] // tile
     for k in range(0, blocks, 4):
         lax.fori_loop(k, k + 4, up, 0)
-        run(2)
+        step(10 + k // 4)
     for src, out, s in ((hd, hd_o, 12), (gp, gp_o, 13)):
         keep.append(pltpu.make_async_copy(src, out, osem.at[s]))
         keep[-1].start()
-    run(len(pending))
-    for k in range(8, len(chunks)):
-        chunks[k].tick5()
-    keep.append(pltpu.make_async_copy(wd, wd_o, osem.at[14]))
-    keep[-1].start()
     my_len = live_length(len_ref, deal_ref, (z * Y + y) * C + x)
     rowpos = lax.broadcasted_iota(jnp.int32, (qrows, 1), 0)
-
-    def down(n, carry):
-        lanes = pl.ds(mult(n * tile, tile), tile)
-        res = dot_nt(hd[...], wd[pl.ds(mult(n * tile, tile), tile), :])
-        res = r[:, lanes] + res + vec[BD:BD + 1, lanes]
-        for i in range(2):
-            live = quarters[i] * qrows + rowpos < my_len
-            outw[i * qrows:(i + 1) * qrows, lanes] = jnp.where(live, res[i * qrows:(i + 1) * qrows], 0.0).astype(BF)
-        return carry
-
-    lax.fori_loop(0, steps, down, 0)
+    parts = len(chunks) - 8
+    wide = wd.shape[1] // X
+    for k in range(parts):
+        if k == 1:
+            step(13)
+        chunks[8 + k].tick5()
+        cuts = [slice(h * wide + k * (wide // parts), h * wide + (k + 1) * (wide // parts)) for h in range(X)]
+        for h, cut in enumerate(cuts):
+            keep.append(pltpu.make_async_copy(wd.at[:, cut], wd_o.at[:, cut], osem.at[16 + X * k + h]))
+            keep[-1].start()
+
+        def down(n, carry, k=k, cuts=cuts):
+            lanes = pl.ds(mult(n * tile, tile), tile)
+            res = dot_nt(hd[:, cuts[0]], wd[lanes, cuts[0]])
+            for cut in cuts[1:]:
+                res = res + dot_nt(hd[:, cut], wd[lanes, cut])
+            res = res + (r[:, lanes] + vec[BD:BD + 1, lanes] if k == 0 else acc[:, lanes])
+            if k < parts - 1:
+                acc[:, lanes] = res
+            else:
+                for i in range(2):
+                    live = quarters[i] * qrows + rowpos < my_len
+                    outw[i * qrows:(i + 1) * qrows, lanes] = jnp.where(live, res[i * qrows:(i + 1) * qrows], 0.0).astype(BF)
+            return carry
+
+        lax.fori_loop(0, steps, down, 0)
     keep.append(pltpu.make_async_copy(outw, out_o, osem.at[15]))
     keep[-1].start()
 
@@ -517,10 +565,10 @@
         cp.wait()
 
 
-def forward(lengths, dealing, xg, cot, sq, sp, su, sd, sv):
-    width = xg.shape[2]
+def forward(lengths, dealing, cot, x_source, shards, vectors):
+    slots, small, width = x_source.shape
     rows = cot.shape[0]
-    ff = su.shape[0] * Z * Y * C
+    ff = shards[2].shape[0] * Z * Y * C
     keys = rows * 2
     pairs = width // 128
 
@@ -540,36 +588,45 @@
         vm((keys, width), BF), vm((rows, width), BF), vm((pairs, 8, rows // 2), F32), vm((rows, width), F32),
         vm((rows, width), BF), vm((rows, ff), BF), vm((rows, ff), BF), vm((Z * Y * C, 16, width), BF),
         vm((16, width), F32), vm((ff // 256, 1, 256), F32), vm((keys, rows // 2), F32), vm((keys, rows // 2), F32),
-        vm((rows, width), BF),
-        pltpu.SemaphoreType.DMA((N_GATHER, 9)), pltpu.SemaphoreType.DMA((7,)), pltpu.SemaphoreType.DMA((8,)),
-        pltpu.SemaphoreType.DMA((16,)),
+        vm((rows, width), BF), vm(x_source.shape, BF), vm((rows, width), F32),
+        pltpu.SemaphoreType.DMA((N_GATHER, 8)), pltpu.SemaphoreType.DMA((6,)), pltpu.SemaphoreType.DMA((8,)),
+        pltpu.SemaphoreType.DMA((24,)),
     ]
     anyspec = pl.BlockSpec(memory_space=pl.ANY)
     smem = pl.BlockSpec(memory_space=pltpu.SMEM)
+    vmem = pl.BlockSpec(memory_space=pltpu.VMEM)
     return pl.pallas_call(
         forward_kernel,
         out_shape=outs,
-        in_specs=[smem, smem] + [anyspec] * 7,
+        in_specs=[smem, smem, anyspec] + [vmem] * 12,
         out_specs=[anyspec] * len(outs),
         scratch_shapes=scratch,
         compiler_params=pltpu.CompilerParams(
             collective_id=0, has_side_effects=True, vmem_limit_bytes=60 * 1024 * 1024
         ),
         name="forward",
-    )(lengths, dealing, xg, cot, sq, sp, su, sd, sv)
+    )(lengths, dealing, cot, x_source, *shards, *vectors)
+
+
+def when(cond):
+    if isinstance(cond, bool):
+        return (lambda f: f()) if cond else (lambda f: None)
+    return pl.when(cond)
 
 
 class Reduce:
-    S1, R1, S2, R2, S3, R3, S4, R4 = range(8)
-
-    def __init__(self, grad, R, step, c0, C, zlist, bufs, out, out_c0, sems, k, where):
+    S1, R1, S2, R2, S3, R3, S4, R4, S5, R5 = range(10)
+
+    def __init__(self, grad, R, step, c0, C, zlist, bufs, out, out_c0, sems, k, where, turned):
         self.grad, self.R, self.step, self.c0, self.cn, self.zlist = grad, R, step, c0, C, zlist
-        self.r1, self.r2, self.r3, self.r4 = bufs
+        self.r1, self.r2, self.r3, self.r4, self.r5 = bufs
         self.out, self.out_c0, self.sems, self.k = out, out_c0, sems, k
         self.z, self.y, self.c, self.x, _ = where
-        c, y, x = self.c, self.y, self.x
-        self.y2, self.x2 = (y + c) % 2, (x + 1 - c) % 2
-        self.y3, self.x3 = (y + 1 - c) % 2, (x + c) % 2
+        y, x = self.y, self.x
+        self.o = o = 1 if turned else self.c
+        self.y2, self.x2 = (y + o) % 2, (x + 1 - o) % 2
+        self.y3, self.x3 = (y + 1 - o) % 2, (x + o) % 2
+        self.every = len(zlist) == Z
 
     def sem(self, which):
         return self.sems.at[self.k, which]
@@ -587,7 +644,7 @@
         self.grad[rows, cols] = (self.grad[rows, cols].astype(F32) + got.astype(F32)).astype(BF)
 
     def zidx(self, zi):
-        return self.zlist[0] if len(self.zlist) == 1 else zi
+        return zi if self.every else self.zlist[0]
 
     def start(self):
         z, y, c, x = self.z, self.y, self.c, self.x
@@ -601,7 +658,7 @@
                     ).start()
 
     def tick2(self):
-        z, y, c, x = self.z, self.y, self.c, self.x
+        z, y, c, x, o = self.z, self.y, self.c, self.x, self.o
         wait_bytes(self.r1, self.sem(self.R1))
 
         def body(e, carry):
@@ -614,18 +671,18 @@
         to = dev(z, self.y2, c, self.x2)
         for zi, zz in enumerate(self.zlist):
             for w in range(2):
-                yy = w * (1 - c) + (1 - y) * c
-                xx = (1 - x) * (1 - c) + w * c
+                yy = w * (1 - o) + (1 - y) * o
+                xx = (1 - x) * (1 - o) + w * o
                 rcopy(self.at(zz, yy, c, xx), self.r2.at[zi * 2 + w], self.sem(self.S2), self.sem(self.R2), to).start()
 
     def tick3(self):
-        z, y, c, x = self.z, self.y, self.c, self.x
+        z, y, c, x, o = self.z, self.y, self.c, self.x, self.o
         wait_bytes(self.r2, self.sem(self.R2))
 
         def body(e, carry):
             w = e % 2
-            yy = w * (1 - c) + y * c
-            xx = x * (1 - c) + w * c
+            yy = w * (1 - o) + y * o
+            xx = x * (1 - o) + w * o
             self.add(self.rows(self.zidx(e // 2), yy, c), self.cols(xx), self.r2[e])
             return carry
 
@@ -634,6 +691,9 @@
         for zi, zz in enumerate(self.zlist):
             rcopy(self.at(zz, self.y3, c, self.x3), self.r3.at[zi], self.sem(self.S3), self.sem(self.R3), to).start()
 
+    def first_hop(self, k):
+        return [(k ^ 1, k, 0), ((3 - k) ^ 1, 3 - k, 1)]
+
     def tick4(self):
         z, y, c, x = self.z, self.y, self.c, self.x
         wait_bytes(self.r3, self.sem(self.R3))
@@ -643,38 +703,79 @@
             return carry
 
         lax.fori_loop(0, len(self.zlist), body, 0)
-        for zz in self.zlist:
-            @pl.when(z != zz)
-            def _(zz=zz):
+        if self.every:
+            mate = z + 1 - 2 * (z % 2)
+            for slot, zz in enumerate((mate, 3 - mate)):
                 rcopy(
-                    self.at(zz, y, c, x), self.r4.at[z], self.sem(self.S4), self.sem(self.R4), dev(zz, y, c, x)
+                    self.at(zz, y, c, x), self.r4.at[slot], self.sem(self.S4), self.sem(self.R4), dev(mate, y, c, x)
                 ).start()
+        else:
+            k = self.zlist[0]
+            for sender, taker, slot in self.first_hop(k):
+                @pl.when(z == sender)
+                def _(taker=taker, slot=slot):
+                    rcopy(
+                        self.at(k, y, c, x), self.r4.at[slot], self.sem(self.S4), self.sem(self.R4),
+                        dev(taker, y, c, x),
+                    ).start()
 
     def tick5(self):
         z, y, c, x = self.z, self.y, self.c, self.x
-
-        def last():
-            wait_bytes(self.r4.at[pl.ds(0, Z - 1)], self.sem(self.R4))
-            total = self.grad[self.rows(z, y, c), self.cols(x)].astype(F32)
-            for dz in range(1, Z):
-                total = total + self.r4[(z + dz) % Z].astype(F32)
-            self.out[:, self.out_c0:self.out_c0 + self.cn] = total
-
-        if len(self.zlist) == Z:
-            last()
+        k = self.zlist[0]
+
+        def take(zz, slot):
+            self.add(self.rows(zz, y, c), self.cols(x), self.r4[slot])
+
+        def pass_on(zz):
+            rcopy(self.at(zz, y, c, x), self.r5, self.sem(self.S5), self.sem(self.R5), dev(zz, y, c, x)).start()
+
+        if self.every:
+            wait_bytes(self.r4, self.sem(self.R4))
+            take(3 - z, 1)
+            pass_on(3 - z)
+            take(z, 0)
         else:
-            pl.when(z == self.zlist[0])(last)
+            @pl.when(z == 3 - k)
+            def _():
+                wait_bytes(self.r4.at[1], self.sem(self.R4))
+                take(k, 1)
+                pass_on(k)
+
+            @pl.when(z == k)
+            def _():
+                wait_bytes(self.r4.at[0], self.sem(self.R4))
+                take(k, 0)
+
+    def tick6(self):
+        z, y, c, x = self.z, self.y, self.c, self.x
+
+        @when(True if self.every else z == self.zlist[0])
+        def _():
+            wait_bytes(self.r5, self.sem(self.R5))
+            own = self.grad[self.rows(z, y, c), self.cols(x)].astype(F32)
+            self.out[:, self.out_c0:self.out_c0 + self.cn] = own + self.r5[...].astype(F32)
 
     def drain(self):
+        z = self.z
         wait_bytes(self.r1, self.sem(self.S1))
         wait_bytes(self.r2, self.sem(self.S2))
         wait_bytes(self.r3, self.sem(self.S3))
-        if len(self.zlist) == Z:
-            wait_bytes(self.r4.at[pl.ds(0, Z - 1)], self.sem(self.S4))
+        if self.every:
+            wait_bytes(self.r4, self.sem(self.S4))
+            wait_bytes(self.r5, self.sem(self.S5))
         else:
-            @pl.when(self.z != self.zlist[0])
+            k = self.zlist[0]
+            for sender, _, slot in self.first_hop(k):
+                @pl.when(z == sender)
+                def _():
+                    wait_bytes(self.r4.at[0], self.sem(self.S4))
+
+            @pl.when(z == 3 - k)
             def _():
-                wait_bytes(self.r4.at[0], self.sem(self.S4))
+                wait_bytes(self.r5, self.sem(self.S5))
+
+
+TURNED_BACK = (3, 6)
 
 
 def reduce_shapes(width, ff):
@@ -695,7 +796,7 @@
         "lse_i", "r_i", "a2_i", "hd_i", "gp_i", "vec_i", "out_i", "og_q", "og_p", "og_u", "og_d", "osum", "ret",
         "out_n", "wq", "wp", "xr", "g", "qs", "ka", "va", "at", "lse", "r", "a2", "vec", "gt", "d2", "dr", "drl",
         "do", "gq", "gp_", "gu", "gd", "wd_t", "wu_t", "hd_t", "gp_t", "dka", "dva", "own_v", "sv", "rk", "rv", "dm",
-        "vs", "vr", "bub", "lsem", "tsem", "rsem", "msem", "vsem",
+        "vs", "vr", "bub", "ret_v", "lsem", "tsem", "rsem", "msem", "vsem",
     )
     env = dict(zip(names, refs[: len(names)]))
     env.update(a1=env["a2"], own_k=env["d2"], sk=env["drl"], dx=env["do"])
@@ -716,7 +817,7 @@
     def at_quarter(k):
         return pl.ds(mult(k * qrows, qrows), qrows)
 
-    enter(Z * Y * C * X)
+    entered = enter(Z * Y * C * X)
 
     loads = {}
     for k, (src, dst) in enumerate(
@@ -749,6 +850,8 @@
     for name in ("r", "vec", "wp", "at", "qs", "ka", "va", "lse", "xr", "wq"):
         loads[name].start()
 
+    entered()
+
     for i in range(2):
         same = jnp.logical_and(x == c, x == i)
         src = e.out_i.at[pl.ds(i * qrows, qrows)]
@@ -756,7 +859,7 @@
 
         @pl.when(same)
         def _(src=src, dst=dst):
-            pltpu.make_async_copy(src, dst, e.msem.at[1]).start()
+            lcopy(src, dst, e.msem.at[1]).start()
 
         @pl.when(jnp.logical_not(same))
         def _(src=src, dst=dst, i=i):
@@ -766,7 +869,7 @@
     chunks = []
     for k, (name, R, step, c0, cn, zlist, oc) in enumerate(reduce_shapes(width, ff)):
         grad, out = grads[name]
-        chunks.append(Reduce(grad, R, step, c0, cn, zlist, bufs[4 * k:4 * k + 4], out, oc, e.rsem, k, where))
+        chunks.append(Reduce(grad, R, step, c0, cn, zlist, bufs[5 * k:5 * k + 5], out, oc, e.rsem, k, where, k in TURNED_BACK))
     dA, dB, u0, u1, u2, u3, pj, q0, q1, q2, q3 = chunks
 
     my_len = live_length(e.len_ref, e.deal_ref, (z * Y + y) * C + x)
@@ -786,8 +889,8 @@
 
     ff_tiles = ff // tile
     plan = {
-        2: [u0.start], 3: [u0.tick2], 5: [u2.start, dA.start, u0.tick3], 7: [u0.tick4, u2.tick2],
-        8: [u1.start, dA.tick2], 9: [u2.tick3], 10: [dA.tick3], 11: [u3.start, dB.start, u2.tick4],
+        2: [u0.start], 4: [u0.tick2], 5: [u2.start, dA.start], 7: [u2.tick2], 8: [u1.start, u0.tick3],
+        9: [dA.tick2], 10: [u1.tick2, u2.tick3], 11: [u3.start, dB.start, u0.tick4],
     }
 
     def ffn(idx, carry):
@@ -837,8 +940,6 @@
         )
 
     sum_g2, sum_c2, sum_bp = lax.fori_loop(0, rows // lrows, norm_two, (blank, blank, blank))
-    u1.tick2()
-    dA.tick4()
 
     loads["wp"].wait()
     loads["at"].wait()
@@ -851,8 +952,8 @@
 
     lax.fori_loop(0, steps, proj_back, 0)
     pj.start()
-    u1.tick3()
     u3.tick2()
+    u0.tick5()
 
     for name in ("qs", "ka", "va", "lse"):
         loads[name].wait()
@@ -863,6 +964,11 @@
     def split(v):
         zero = jnp.zeros_like(v)
         return jnp.where(lane < HEAD_DIM, v, zero), jnp.where(lane >= HEAD_DIM, v, zero)
+
+    between = {
+        (0, 0): [dB.tick2, pj.tick2, dA.tick3], (1, 1): [u1.tick3], (2, 0): [u2.tick4], (2, 1): [u3.tick3],
+        (3, 0): [u2.tick5], (4, 0): [dB.tick3, u1.tick4], (5, 0): [u1.tick5], (5, 1): [pj.tick3],
+    }
 
     def pair_body(p, carry):
         lanes = pl.ds(mult(p * 128, 128), 128)
@@ -898,22 +1004,29 @@
             none = jnp.zeros((HEAD_DIM, qrows), F32)
             dq = lax.fori_loop(0, quarter + 1, keys, (none, none))
             e.dm[own, lanes] = (jnp.concatenate(dq, axis=0).T * HEAD_DIM ** -0.5).astype(BF)
+            for (at_p, at_i), acts in between.items():
+                if at_i == i:
+                    @pl.when(p == at_p)
+                    def _(acts=acts):
+                        for act in acts:
+                            act()
         for i in range(2):
             own = slice(i * qrows, (i + 1) * qrows)
             e.own_k[own, lanes] = e.dka[at_quarter(quarters[i]), :]
             e.own_v[own, lanes] = e.dva[at_quarter(quarters[i]), :]
             e.sk[own, lanes] = e.dka[at_quarter(theirs[i]), :].astype(BF)
             e.sv[own, lanes] = e.dva[at_quarter(theirs[i]), :].astype(BF)
+        for k in range(pairs // 2):
+            @pl.when(p == 2 * k + 1)
+            def _(k=k):
+                cut = slice(2 * k * 128, (2 * k + 2) * 128)
+                for src, dst, s in ((e.sk, e.rk, 2), (e.sv, e.rv, 4)):
+                    rcopy(
+                        src.at[:, cut], dst.at[:, cut], e.msem.at[s], e.msem.at[s + 1], dev(z, y, 1 - c, x)
+                    ).start()
         return carry
 
-    between = [[dB.tick2, u1.tick4, u3.tick3, pj.tick2], [dB.tick3, u3.tick4, pj.tick3], [dB.tick4, pj.tick4]]
-    for k in range(3):
-        lax.fori_loop(2 * k, 2 * k + 2, pair_body, 0)
-        for act in between[k]:
-            act()
-        cut = slice(2 * k * 128, (2 * k + 2) * 128)
-        for src, dst, s in ((e.sk, e.rk, 2), (e.sv, e.rv, 4)):
-            rcopy(src.at[:, cut], dst.at[:, cut], e.msem.at[s], e.msem.at[s + 1], dev(z, y, 1 - c, x)).start()
+    lax.fori_loop(0, pairs, pair_body, 0)
 
     loads["xr"].wait()
 
@@ -932,6 +1045,7 @@
 
     lax.fori_loop(0, 3, qkv_grad, 0)
     q0.start()
+    dA.tick4()
     wait_bytes(e.rk, e.msem.at[3])
     wait_bytes(e.rv, e.msem.at[5])
     for part, (mine, got) in enumerate(((e.own_k, e.rk), (e.own_v, e.rv))):
@@ -943,17 +1057,7 @@
             return carry
 
         lax.fori_loop(0, rows // lrows, merge, 0)
-    lax.fori_loop(3, 5, qkv_grad, 0)
-    q1.start()
-    q0.tick2()
-    lax.fori_loop(5, 7, qkv_grad, 0)
-    q2.start()
-    q1.tick2()
-    lax.fori_loop(7, 9, qkv_grad, 0)
-    q3.start()
-    q0.tick3()
-    q2.tick2()
-
+    u3.tick4()
     loads["wq"].wait()
 
     def input_back(n, carry):
@@ -962,8 +1066,8 @@
         return carry
 
     lax.fori_loop(0, steps, input_back, 0)
-    q1.tick3()
-    q3.tick2()
+    q0.tick2()
+    pj.tick4()
 
     def norm_one_back(k, sums):
         at_rows = pl.ds(mult(k * lrows, lrows), lrows)
@@ -976,6 +1080,8 @@
         return sums[0] + jnp.sum(da * n1, axis=0, keepdims=True), sums[1] + jnp.sum(da, axis=0, keepdims=True)
 
     sum_g1, sum_c1 = lax.fori_loop(0, rows // lrows, norm_one_back, (blank, blank))
+    dB.tick4()
+    dA.tick5()
 
     e.vs[0] = jnp.zeros_like(e.vs[0])
     for row, value in ((G1, sum_g1), (C1, sum_c1), (BP, sum_bp), (G2, sum_g2), (C2, sum_c2), (BD, total_bd)):
@@ -1000,44 +1106,81 @@
     small = e.ret.shape[1]
     per_quarter = qrows // small
     slot = (z * Y + y) * C + x
-    for i in range(2):
-        def give_back(b, carry, i=i):
-            td = ((i + c) % 2) * per_quarter + b
-            src = e.dx.at[pl.ds(mult(i * qrows + b * small, small), small)]
-            mine = jnp.logical_and(td == d, x == i)
-
-            @pl.when(mine)
-            def _():
-                pltpu.make_async_copy(src, e.ret.at[slot], e.msem.at[7]).start()
-
-            @pl.when(jnp.logical_not(mine))
-            def _():
-                rcopy(src, e.ret.at[slot], e.msem.at[6], e.msem.at[7], {"dp": td, "cp": i}).start()
-
-            return carry
-
-        lax.fori_loop(0, per_quarter, give_back, 0)
-
-    q2.tick3()
+
+    def give_back(k, carry):
+        i = (k + x) % 2
+        e8 = (k // 2 + d) % per_quarter
+        td = ((i + c) % 2) * per_quarter + e8
+        src = e.dx.at[pl.ds(mult(i * qrows + e8 * small, small), small)]
+        mine = jnp.logical_and(td == d, x == i)
+
+        @pl.when(mine)
+        def _():
+            lcopy(src, e.ret_v.at[slot], e.msem.at[7]).start()
+
+        @pl.when(jnp.logical_not(mine))
+        def _():
+            rcopy(src, e.ret_v.at[slot], e.msem.at[6], e.msem.at[7], {"dp": td, "cp": i}).start()
+
+        return carry
+
+    share = per_quarter // 2
+    lax.fori_loop(0, share, give_back, 0)
+    lax.fori_loop(3, 5, qkv_grad, 0)
+    q1.start()
+    lax.fori_loop(share, 2 * share, give_back, 0)
+    lax.fori_loop(5, 7, qkv_grad, 0)
+    q2.start()
+    lax.fori_loop(2 * share, 3 * share, give_back, 0)
+    u3.tick5()
+    lax.fori_loop(7, 9, qkv_grad, 0)
+    q3.start()
+    lax.fori_loop(3 * share, 4 * share, give_back, 0)
+    q0.tick3()
+    q1.tick2()
+    pj.tick5()
     land(0)
     hop(1)
-    q0.tick4()
-    q3.tick3()
+    for ch in (u0, u2, u1):
+        ch.tick6()
+    q2.tick2()
+    q3.tick2()
     land(1)
     hop(2)
-    q1.tick4()
-    q2.tick4()
-    for ch in (u0, u1, u2, u3, dA, dB, pj):
-        ch.tick5()
+    dB.tick5()
+    dA.tick6()
+    q0.tick4()
+    q1.tick3()
     land(2)
     hop(3)
-    q3.tick4()
+    q2.tick3()
+    q3.tick3()
+    q1.tick4()
     land(3)
     hop(4)
+    q2.tick4()
+    q3.tick4()
+    u3.tick6()
+    q0.tick5()
+    pj.tick6()
+    q1.tick5()
+    land(4)
+    own = width // (Z * Y * C)
+    e.osum[0:6, :] = pltpu.roll(e.vs[5, 0:6, :], (width - d * own) % width, 1)[:, :tile]
+    long = ff // (Z * Y * C)
+    per_row = width // long
+    e.osum[6:7, :] = pltpu.roll(
+        e.vs[5, pl.ds(BU + d // per_row, 1), :], (width - (d % per_row) * long) % width, 1
+    )[:, :tile]
+    e.osum[7:8, :] = jnp.zeros((1, tile), F32)
+    q2.tick5()
+    q3.tick5()
+    dB.tick6()
+    wait_bytes(e.dx, e.msem.at[7])
+    for s in range(e.ret.shape[0]):
+        e.ret[s] = e.ret_v[jnp.clip(e.deal_ref[s], 0, e.ret.shape[0] - 1)]
     for ch in (q0, q1, q2, q3):
-        ch.tick5()
-    land(4)
-    e.osum[...] = e.vs[5]
+        ch.tick6()
 
     for ch in chunks:
         ch.drain()
@@ -1053,8 +1196,6 @@
     @pl.when((x + c) % 2 != d // per_quarter)
     def _():
         wait_bytes(e.dx, e.msem.at[6])
-
-    wait_bytes(e.dx, e.msem.at[7])
 
     @pl.when(c == x)
     def _():
@@ -1080,7 +1221,7 @@
         return jax.ShapeDtypeStruct(shape, dtype)
 
     outs = [arr(s.shape, F32) for s in shards] + [
-        arr((16, width), F32), arr((n, small, width)), arr((rows, width)),
+        arr((8, 256), F32), arr((n, small, width)), arr((rows, width)),
     ]
     vm = pltpu.VMEM
     acts = vm((rows, width), BF)
@@ -1092,13 +1233,13 @@
         vm((2, width, 256), BF), vm((2, 256, width), BF), vm((2, rows, 256), BF), vm((2, rows, 256), BF),
         vm((keys, 128), F32), vm((keys, 128), F32),
         acts32, acts, acts, acts, vm((rows, 3 * width), BF),
-        vm((6, 16, width), F32), vm((5, 16, width), F32), vm((ff // 256, 1, 256), F32),
-        pltpu.SemaphoreType.DMA((12,)), pltpu.SemaphoreType.DMA((4, 2)), pltpu.SemaphoreType.DMA((11, 8)),
+        vm((6, 16, width), F32), vm((5, 16, width), F32), vm((ff // 256, 1, 256), F32), vm((n, small, width), BF),
+        pltpu.SemaphoreType.DMA((12,)), pltpu.SemaphoreType.DMA((4, 2)), pltpu.SemaphoreType.DMA((11, 10)),
         pltpu.SemaphoreType.DMA((8,)), pltpu.SemaphoreType.DMA((2, 5)),
     ]
     for _, R, _, _, cn, zlist, _ in reduce_shapes(width, ff):
         k = len(zlist)
-        scratch += [vm((2 * k, 2, R, cn), BF), vm((2 * k, R, cn), BF), vm((k, R, cn), BF), vm((Z, R, cn), BF)]
+        scratch += [vm((2 * k, 2, R, cn), BF), vm((2 * k, R, cn), BF), vm((k, R, cn), BF), vm((2, R, cn), BF), vm((R, cn), BF)]
     anyspec = pl.BlockSpec(memory_space=pl.ANY)
     smem = pl.BlockSpec(memory_space=pltpu.SMEM)
     vmem = pl.BlockSpec(memory_space=pltpu.VMEM)
@@ -1106,7 +1247,7 @@
         backward_kernel,
         out_shape=outs,
         in_specs=[smem, smem] + [anyspec] * len(saved),
-        out_specs=[vmem] * 5 + [anyspec] * 2,
+        out_specs=[vmem] * 6 + [anyspec],
         scratch_shapes=scratch,
         compiler_params=pltpu.CompilerParams(
             collective_id=1, has_side_effects=True, vmem_limit_bytes=67043328
@@ -1119,30 +1260,16 @@
     x_source, cotangent, lengths, dealing, qkv_weight, proj_weight, up_weight, down_weight,
     first_gain, first_shift, proj_bias, second_gain, second_shift, up_bias, down_bias,
 ):
-    slots = dealing.shape[0]
-    width = x_source.shape[2]
-    n = Z * Y * C
-    d = lax.axis_index("dp")
-    owners = jnp.sum(
-        jnp.where(dealing[None, :] == jnp.arange(slots)[:, None], jnp.arange(slots)[None, :], 0), axis=1
-    )
-    xg = x_source[owners]
-    shards = [w.astype(BF).T for w in (qkv_weight, proj_weight, up_weight, down_weight)]
-    seven = jnp.stack([first_gain, first_shift, proj_bias, second_gain, second_shift, down_bias]).astype(BF)
-    own = seven.shape[1]
-    place = jnp.arange(width) // own
-    table = jnp.where(place == d, jnp.tile(seven, (1, n)), jnp.zeros((), BF))
-    long = up_bias.astype(BF)
-    wide = jnp.where(jnp.arange(long.shape[0] * n) // long.shape[0] == d, jnp.tile(long, n), jnp.zeros((), BF))
-    sv = jnp.concatenate([table, wide.reshape(-1, width), jnp.zeros((16 - 6 - wide.shape[0] // width, width), BF)])
-    saved = forward(lengths, dealing, xg, cotangent[0], *shards, sv)
-    gq, gp, gu, gd, sums, ret, out = backward(lengths, dealing, saved, shards)
-    input_grad = ret[dealing]
-    picked = lax.dynamic_slice_in_dim(sums[:6].reshape(6, n, own), d, 1, axis=1)[:, 0]
-    long_sum = lax.dynamic_slice_in_dim(sums[BU:BU + wide.shape[0] // width].reshape(-1), d * long.shape[0], long.shape[0])
+    shards = [w.T for w in (qkv_weight, proj_weight, up_weight, down_weight)]
+    vectors = [
+        v[None] for v in (first_gain, first_shift, proj_bias, second_gain, second_shift, down_bias, up_bias)
+    ]
+    saved = forward(lengths, dealing, cotangent[0], x_source, shards, vectors)
+    gq, gp, gu, gd, sums, input_grad, out = backward(lengths, dealing, saved, shards)
+    own, long = first_gain.shape[0], up_bias.shape[0]
     return (
         out[None], input_grad, gq.T, gp.T, gu.T, gd.T,
-        picked[G1], picked[C1], picked[BP], picked[G2], picked[C2], long_sum, picked[BD],
+        sums[G1, :own], sums[C1, :own], sums[BP, :own], sums[G2, :own], sums[C2, :own], sums[6, :long], sums[BD, :own],
     )
 
 

time: 273 us -> 234 us (0.86)
  Pallas kernels: 247 us -> 221 us
  other arithmetic: 11.3 us -> 0 us
  local copies, waits for them, and re-layouts: 13.1 us -> 9.65 us
    pallas_call x1, Pallas kernels: 123 us -> 110 us  [forward(): pl.pallas_call(forward_kernel, out_shape=outs, in_specs=[smem, smem, anys...]
    pallas_call x1, Pallas kernels: 124 us -> 111 us  [backward(): pl.pallas_call(backward_kernel, out_shape=outs, in_specs=[smem, smem] + [...]
    transpose x4 -> x0, other arithmetic: 6.37 us -> none  [slice_plan(): w.astype(BF)]
    gather x2 -> x0, local copies, waits for them, and re-layouts: 5.22 us -> none  [the longest x1 2.61 us: slice_plan(): xg = x_source[owners]]
    unnamed x13 -> x14, local copies, waits for them, and re-layouts: 4.82 us -> 6.89 us
where the time goes in v2:
time: 234 us; the launch traced here: 231 us
  Pallas kernels  221 us (94%)
  local copies, waits for them, and re-layouts  9.65 us (4%)
    pallas_call x1, Pallas kernels, backward(): pl.pallas_call(backward_kernel, out_shape=outs, in_specs=[smem, smem] + [...  111 us
    pallas_call x1, Pallas kernels, forward(): pl.pallas_call(forward_kernel, out_shape=outs, in_specs=[smem, smem, anys...  110 us
    unnamed x14, local copies, waits for them, and re-layouts  6.89 us

profile of v2, /device:TPU:0, one launch (start us, length us, event | category | flops | bytes accessed | tf_op | source)
XLA Modules:
  0.0 231.1 jit_solution(14826375816972145123)
XLA Ops:
  0.6 109.9 %forward.1 = (bf16[2304,768]{1,0:T(8,128)(2,1)}, bf16[768,768]{1,0:T(8,128)(2,1)}, bf16[3072,768]{1,0:T(8,128)(2,1)}, bf16[768,3072]{1,0:T(8,128)(2,1)}, bf16[51...) custom-call(s32[16]{0:T(128)} %refs_0_.1, ...), custom_call_target="tpu_custom_call" | custom-call | tf_op jit(solution)/shard_map/forward/pallas_call | solution.py:598
  110.5 110.9 %backward.1 = (f32[144,384]{1,0:T(8,128)}, f32[48,384]{1,0:T(8,128)}, f32[192,384]{1,0:T(8,128)}, f32[48,1536]{1,0:T(8,128)}, f32[8,256]{1,0:T(8,128)}, /*index=...) custom-call(s32[16]{0:T(128)} %refs_0_.1, s32[16]{0:T(128)} %refs_1_.1, bf16[2304,768]{1,0:T(8,128)(2,1)} %get-tuple-element.37.refs_2_, ...), custom_call_target="tpu_custom_call" | custom-call | tf_op jit(solution)/shard_map/backward/pallas_call | solution.py:1246
  221.4 0.0 copy-start.2
  221.4 0.0 copy-start.3
  221.4 0.0 copy-start.1
  221.5 0.0 copy-start
  221.5 1.3 slice.26
  222.8 1.4 slice_bitcast_fusion
  224.2 2.1 copy.34
  226.3 2.1 copy.35
  228.4 0.0 copy-done.2
  228.4 0.7 copy.36
  229.0 0.0 copy-done.3
  229.0 0.6 copy.37
  229.7 0.0 copy-done.1
  229.7 0.7 copy.38
  230.4 0.0 copy-done
  230.4 0.7 copy.39
Async XLA Ops:
  221.4 6.9 %copy-start.2 = (f32[144,384]{1,0:T(8,128)S(1)}, f32[144,384]{1,0:T(8,128)}, u32[]{:S(2)}) copy-start(f32[144,384]{1,0:T(8,128)} %get-tuple-element.56) | copy-start | bytes 663556
  221.4 7.6 %copy-start.3 = (f32[48,384]{1,0:T(8,128)S(1)}, f32[48,384]{1,0:T(8,128)}, u32[]{:S(2)}) copy-start(f32[48,384]{1,0:T(8,128)} %get-tuple-element.57) | copy-start | bytes 221188
  221.4 8.2 %copy-start.1 = (f32[192,384]{1,0:T(8,128)S(1)}, f32[192,384]{1,0:T(8,128)}, u32[]{:S(2)}) copy-start(f32[192,384]{1,0:T(8,128)} %get-tuple-element.58) | copy-start | bytes 884740
  221.5 8.9 %copy-start = (f32[48,1536]{1,0:T(8,128)S(1)}, f32[48,1536]{1,0:T(8,128)}, u32[]{:S(2)}) copy-start(f32[48,1536]{1,0:T(8,128)} %get-tuple-element.59) | copy-start | bytes 884740

commit v3 on v2

--- a/solution.py
+++ b/solution.py
@@ -114,110 +114,122 @@
 
 
 class Gather:
-    ZS, ZR, S2, R2, S3, R3, S4, R4 = range(8)
-
-    def __init__(self, piece, sems, k, dummy, where, turned):
-        self.p, self.sems, self.k, self.dummy = piece, sems, k, dummy
+    FAR, MATE, A, B, CORE = range(5)
+
+    def __init__(self, piece, sems, k, dummy, where, kind, turned):
+        self.p, self.sems, self.k, self.dummy, self.kind = piece, sems, k, dummy, kind
         z, y, c, x, _ = where
         self.z, self.y, self.c, self.x = z, y, c, x
-        self.o = o = 1 if turned else c
-        self.y2, self.x2 = (y + 1 - o) % 2, (x + o) % 2
-        self.y3, self.x3 = (y + o) % 2, (x + 1 - o) % 2
-
-    def sem(self, which):
-        return self.sems.at[self.k, which]
-
-    def wait(self, count, which):
+        o = 1 if turned else c
+        self.far, self.mate = 3 - z, z + 1 - 2 * (z % 2)
+        self.ya, self.xa = (y + 1 - o) % 2, (x + o) % 2
+        self.yb, self.xb = (y + o) % 2, (x + 1 - o) % 2
+        self.to = {
+            self.FAR: dev(self.far, y, c, x), self.MATE: dev(self.mate, y, c, x), self.A: dev(z, self.ya, c, self.xa),
+            self.B: dev(z, self.yb, c, self.xb), self.CORE: dev(z, y, 1 - c, x),
+        }
+        self.counts = {self.FAR: 1, self.MATE: 2, self.A: 4} if kind == 1 else {self.FAR: 2, self.MATE: 4, self.A: 1}
+        self.counts.update({self.B: 8, self.CORE: 16})
+
+    def send(self, pieces, *ways):
+        for way in ways:
+            for z, y, x in pieces:
+                q = self.p.at(z, y, self.c, x)
+                rcopy(q, q, self.sems.at[self.k, 0, way], self.sems.at[self.k, 1, way], self.to[way]).start()
+
+    def wait(self, way, side=1):
         p = self.p
-        wait_bytes(self.dummy.at[pl.ds(0, count * p.rn), pl.ds(0, p.cn)], self.sem(which))
+        wait_bytes(self.dummy.at[pl.ds(0, self.counts[way] * p.rn), pl.ds(0, p.cn)], self.sems.at[self.k, side, way])
 
     def start(self):
-        p, z, y, c, x = self.p, self.z, self.y, self.c, self.x
-        own = p.at(z, y, c, x)
-        for dz in range(1, Z):
-            z2 = (z + dz) % Z
-            rcopy(own, own, self.sem(self.ZS), self.sem(self.ZR), dev(z2, y, c, x)).start()
+        own = [(self.z, self.y, self.x)]
+        if self.kind == 1:
+            self.send(own, self.FAR, self.MATE, self.A, self.B, self.CORE)
+        else:
+            self.send(own, self.A, self.FAR, self.MATE, self.B, self.CORE)
+
+    def tick1(self):
+        if self.kind == 1:
+            self.wait(self.FAR)
+            self.send([(self.far, self.y, self.x)], self.MATE, self.A, self.B, self.CORE)
+        else:
+            self.wait(self.A)
+            self.send([(self.z, self.ya, self.xa)], self.FAR, self.MATE, self.B, self.CORE)
 
     def tick2(self):
-        p, z, y, c, x = self.p, self.z, self.y, self.c, self.x
-        self.wait(Z - 1, self.ZR)
-        for zz in range(Z):
-            q = p.at(zz, y, c, x)
-            rcopy(q, q, self.sem(self.S2), self.sem(self.R2), dev(z, self.y2, c, self.x2)).start()
-        for zz in range(Z):
-            q = p.at(zz, y, c, x)
-            rcopy(q, q, self.sem(self.S3), self.sem(self.R3), dev(z, self.y3, c, self.x3)).start()
-            rcopy(q, q, self.sem(self.S4), self.sem(self.R4), dev(z, y, 1 - c, x)).start()
+        if self.kind == 1:
+            self.wait(self.MATE)
+            self.send([(self.mate, self.y, self.x), (3 - self.mate, self.y, self.x)], self.A, self.B, self.CORE)
+        else:
+            self.wait(self.FAR)
+            self.send([(self.far, self.y, self.x), (self.far, self.ya, self.xa)], self.MATE, self.B, self.CORE)
 
     def tick3(self):
-        p, z, y, c, x = self.p, self.z, self.y, self.c, self.x
-        self.wait(Z, self.R2)
-        for zz in range(Z):
-            q = p.at(zz, self.y2, c, self.x2)
-            rcopy(q, q, self.sem(self.S3), self.sem(self.R3), dev(z, self.y3, c, self.x3)).start()
-            rcopy(q, q, self.sem(self.S4), self.sem(self.R4), dev(z, y, 1 - c, x)).start()
+        if self.kind == 1:
+            self.wait(self.A)
+            self.send([(k, self.ya, self.xa) for k in range(Z)], self.B, self.CORE)
+        else:
+            self.wait(self.MATE)
+            self.send(
+                [(k, y, x) for k in (self.mate, 3 - self.mate) for y, x in ((self.y, self.x), (self.ya, self.xa))],
+                self.B, self.CORE,
+            )
 
     def tick4(self):
-        p, z, y, c, x = self.p, self.z, self.y, self.c, self.x
-        self.wait(2 * Z, self.R3)
-        for zz in range(Z):
-            for which in range(2):
-                yy = which * (1 - self.o) + (1 - y) * self.o
-                xx = (1 - x) * (1 - self.o) + which * self.o
-                q = p.at(zz, yy, c, xx)
-                rcopy(q, q, self.sem(self.S4), self.sem(self.R4), dev(z, y, 1 - c, x)).start()
+        self.wait(self.B)
+        self.send(
+            [(k, y, x) for k in range(Z) for y, x in ((self.yb, self.xb), (1 - self.y, 1 - self.x))], self.CORE
+        )
 
     def tick5(self):
-        self.wait(4 * Z, self.R4)
+        self.wait(self.CORE)
 
     def drain(self):
-        self.wait(Z - 1, self.ZS)
-        self.wait(Z, self.S2)
-        self.wait(2 * Z, self.S3)
-        self.wait(4 * Z, self.S4)
+        for way in range(5):
+            self.wait(way, 0)
 
 
 class Vectors:
-    ZS, ZR, S2, R2, S4, R4 = range(6)
+    FAR, MATE, A, CORE = range(4)
 
     def __init__(self, full, sems, where):
-        self.full, self.sems, self.where = full, sems, where
-
-    def at(self, z, y, c):
-        return self.full.at[(z * Y + y) * C + c]
+        self.full, self.sems = full, sems
+        z, y, c, x, _ = where
+        self.z, self.y, self.c = z, y, c
+        self.far, self.mate = 3 - z, z + 1 - 2 * (z % 2)
+        self.to = (dev(self.far, y, c, x), dev(self.mate, y, c, x), dev(z, 1 - y, c, x), dev(z, y, 1 - c, x))
+        self.counts = (1, 2, 4, 8)
+
+    def send(self, pieces, *ways):
+        for way in ways:
+            for z, y in pieces:
+                q = self.full.at[(z * Y + y) * C + self.c]
+                rcopy(q, q, self.sems.at[0, way], self.sems.at[1, way], self.to[way]).start()
+
+    def wait(self, way, side=1):
+        wait_bytes(self.full.at[pl.ds(0, self.counts[way])], self.sems.at[side, way])
 
     def start(self):
-        z, y, c, x, _ = self.where
-        own = self.at(z, y, c)
-        for dz in range(1, Z):
-            z2 = (z + dz) % Z
-            rcopy(own, own, self.sems.at[self.ZS], self.sems.at[self.ZR], dev(z2, y, c, x)).start()
-
-    def wait(self, count, which):
-        wait_bytes(self.full.at[pl.ds(0, count)], self.sems.at[which])
+        self.send([(self.z, self.y)], self.FAR, self.MATE, self.A, self.CORE)
+
+    def tick1(self):
+        self.wait(self.FAR)
+        self.send([(self.far, self.y)], self.MATE, self.A, self.CORE)
 
     def tick2(self):
-        z, y, c, x, _ = self.where
-        self.wait(Z - 1, self.ZR)
-        for zz in range(Z):
-            q = self.at(zz, y, c)
-            rcopy(q, q, self.sems.at[self.S2], self.sems.at[self.R2], dev(z, 1 - y, c, x)).start()
-            rcopy(q, q, self.sems.at[self.S4], self.sems.at[self.R4], dev(z, y, 1 - c, x)).start()
+        self.wait(self.MATE)
+        self.send([(self.mate, self.y), (3 - self.mate, self.y)], self.A, self.CORE)
 
     def tick3(self):
-        z, y, c, x, _ = self.where
-        self.wait(Z, self.R2)
-        for zz in range(Z):
-            q = self.at(zz, 1 - y, c)
-            rcopy(q, q, self.sems.at[self.S4], self.sems.at[self.R4], dev(z, y, 1 - c, x)).start()
+        self.wait(self.A)
+        self.send([(k, 1 - self.y) for k in range(Z)], self.CORE)
 
     def tick4(self):
-        self.wait(2 * Z, self.R4)
+        self.wait(self.CORE)
 
     def drain(self):
-        self.wait(Z - 1, self.ZS)
-        self.wait(Z, self.S2)
-        self.wait(2 * Z, self.S4)
+        for way in range(4):
+            self.wait(way, 0)
 
 
 G1, C1, BP, G2, C2, BD, BU = range(7)
@@ -244,8 +256,11 @@
 
 
 N_GATHER = 12
-TURNED = (7, 9, 11)
-COT_STEPS = (5, 7)
+TICKS = ("tick1", "tick2", "tick3", "tick4")
+KINDS = (1, 1, 1, 1, 2, 2, 1, 2, 2, 1, 2, 2)
+TURNED = (7,)
+COT_STEPS = (6, 8)
+LAGS = ((0, 1, 2, 3),) * 4 + ((0, 1, 2, 4),) * 8
 
 
 def forward_kernel(
@@ -291,7 +306,7 @@
     vectors = Vectors(vg, vsem, where)
     vectors.start()
     chunks = [
-        Gather(p, gsem, k, wu, where, k in TURNED) for k, p in enumerate(gather_chunks(wq, wp, wu, wd))
+        Gather(p, gsem, k, wu, where, KINDS[k], k in TURNED) for k, p in enumerate(gather_chunks(wq, wp, wu, wd))
     ]
 
     def send_cot(b):
@@ -340,15 +355,17 @@
             lax.fori_loop(s * slots // 4, (s + 1) * slots // 4, deal_out, 0)
         if s in COT_STEPS:
             send_cot(COT_STEPS.index(s))
-        for back, name in ((0, "tick2"), (1, "tick3"), (2, "tick4")):
-            if 0 <= s - back < len(chunks):
-                getattr(chunks[s - back], name)()
+        for n in range(4):
+            for k in range(len(chunks)):
+                if k + LAGS[k][n] == s:
+                    getattr(chunks[k], TICKS[n])()
 
     step(0)
+    vectors.tick1()
+    step(1)
     vectors.tick2()
-    step(1)
+    step(2)
     vectors.tick3()
-    step(2)
     step(3)
     vectors.tick4()
 
@@ -372,6 +389,7 @@
     lax.fori_loop(0, rows // lrows, first_norm, 0)
 
     step(4)
+    step(5)
     for k in range(3):
         chunks[k].tick5()
     keep = [pltpu.make_async_copy(wq, wq_o, osem.at[0])]
@@ -400,7 +418,7 @@
             to = ka if part == 1 else va
             for i in range(2):
                 rcopy(to.at[q_at(i)], to.at[q_at(i)], msem.at[4 + 2 * (part - 1)], msem.at[5 + 2 * (part - 1)], dev(z, y, 1 - c, x)).start()
-    step(5)
+    step(6)
     wait_bytes(ka.at[pl.ds(0, rows)], msem.at[5])
     wait_bytes(va.at[pl.ds(0, rows)], msem.at[7])
     for src, out, s in ((qs, qs_o, 1), (ka, ka_o, 2), (va, va_o, 3), (xr, xr_o, 4), (vec, vec_o, 5)):
@@ -460,7 +478,7 @@
     per = 2
     for k in range(0, pairs, per):
         lax.fori_loop(k, k + per, pair_body, 0)
-        step(6 + k // per)
+        step(7 + k // per)
 
     chunks[3].tick5()
     for src, out, s in ((wp, wp_o, 6), (at, at_o, 7), (lse, lse_o, 8)):
@@ -482,7 +500,8 @@
         return carry
 
     lax.fori_loop(0, rows // lrows, second_norm, 0)
-    step(9)
+    step(10)
+    step(11)
     for k in range(4, 8):
         chunks[k].tick5()
     for src, out, s in ((wu, wu_o, 9), (r, r_o, 10), (a2, a2_o, 11)):
@@ -503,7 +522,7 @@
     blocks = hd.shape[1] // tile
     for k in range(0, blocks, 4):
         lax.fori_loop(k, k + 4, up, 0)
-        step(10 + k // 4)
+        step(12 + k // 4)
     for src, out, s in ((hd, hd_o, 12), (gp, gp_o, 13)):
         keep.append(pltpu.make_async_copy(src, out, osem.at[s]))
         keep[-1].start()
@@ -513,7 +532,7 @@
     wide = wd.shape[1] // X
     for k in range(parts):
         if k == 1:
-            step(13)
+            step(15)
         chunks[8 + k].tick5()
         cuts = [slice(h * wide + k * (wide // parts), h * wide + (k + 1) * (wide // parts)) for h in range(X)]
         for h, cut in enumerate(cuts):
@@ -589,7 +608,7 @@
         vm((rows, width), BF), vm((rows, ff), BF), vm((rows, ff), BF), vm((Z * Y * C, 16, width), BF),
         vm((16, width), F32), vm((ff // 256, 1, 256), F32), vm((keys, rows // 2), F32), vm((keys, rows // 2), F32),
         vm((rows, width), BF), vm(x_source.shape, BF), vm((rows, width), F32),
-        pltpu.SemaphoreType.DMA((N_GATHER, 8)), pltpu.SemaphoreType.DMA((6,)), pltpu.SemaphoreType.DMA((8,)),
+        pltpu.SemaphoreType.DMA((N_GATHER, 2, 5)), pltpu.SemaphoreType.DMA((2, 4)), pltpu.SemaphoreType.DMA((8,)),
         pltpu.SemaphoreType.DMA((24,)),
     ]
     anyspec = pl.BlockSpec(memory_space=pl.ANY)

time: 234 us -> 218 us (0.932)
  Pallas kernels: 221 us -> 207 us
    pallas_call x1, Pallas kernels: 110 us -> 94.7 us  [forward(): pl.pallas_call(forward_kernel, out_shape=outs, in_specs=[smem, smem, anys...]
where the time goes in v3:
time: 218 us; the launch traced here: 217 us
  Pallas kernels  207 us (95%)
  local copies, waits for them, and re-layouts  9.65 us (4%)
    pallas_call x1, Pallas kernels, backward(): pl.pallas_call(backward_kernel, out_shape=outs, in_specs=[smem, smem] + [...  112 us
    pallas_call x1, Pallas kernels, forward(): pl.pallas_call(forward_kernel, out_shape=outs, in_specs=[smem, smem, anys...  94.7 us
    unnamed x14, local copies, waits for them, and re-layouts  6.89 us

profile of v3, /device:TPU:0, one launch (start us, length us, event | category | flops | bytes accessed | tf_op | source)
XLA Modules:
  0.0 217.2 jit_solution(9246759490922612969)
XLA Ops:
  0.6 94.7 %forward.1 = (bf16[2304,768]{1,0:T(8,128)(2,1)}, bf16[768,768]{1,0:T(8,128)(2,1)}, bf16[3072,768]{1,0:T(8,128)(2,1)}, bf16[768,3072]{1,0:T(8,128)(2,1)}, bf16[51...) custom-call(s32[16]{0:T(128)} %refs_0_.1, ...), custom_call_target="tpu_custom_call" | custom-call | tf_op jit(solution)/shard_map/forward/pallas_call | solution.py:617
  95.4 112.1 %backward.1 = (f32[144,384]{1,0:T(8,128)}, f32[48,384]{1,0:T(8,128)}, f32[192,384]{1,0:T(8,128)}, f32[48,1536]{1,0:T(8,128)}, f32[8,256]{1,0:T(8,128)}, /*index=...) custom-call(s32[16]{0:T(128)} %refs_0_.1, s32[16]{0:T(128)} %refs_1_.1, bf16[2304,768]{1,0:T(8,128)(2,1)} %get-tuple-element.37.refs_2_, ...), custom_call_target="tpu_custom_call" | custom-call | tf_op jit(solution)/shard_map/backward/pallas_call | solution.py:1265
  207.5 0.0 copy-start.2
  207.5 0.0 copy-start.3
  207.5 0.0 copy-start.1
  207.6 0.0 copy-start
  207.6 1.3 slice.26
  208.9 1.4 slice_bitcast_fusion
  210.3 2.1 copy.34
  212.4 2.1 copy.35
  214.5 0.0 copy-done.2
  214.5 0.7 copy.36
  215.1 0.0 copy-done.3
  215.1 0.6 copy.37
  215.8 0.0 copy-done.1
  215.8 0.7 copy.38
  216.5 0.0 copy-done
  216.5 0.7 copy.39
Async XLA Ops:
  207.5 6.9 %copy-start.2 = (f32[144,384]{1,0:T(8,128)S(1)}, f32[144,384]{1,0:T(8,128)}, u32[]{:S(2)}) copy-start(f32[144,384]{1,0:T(8,128)} %get-tuple-element.56) | copy-start | bytes 663556
  207.5 7.6 %copy-start.3 = (f32[48,384]{1,0:T(8,128)S(1)}, f32[48,384]{1,0:T(8,128)}, u32[]{:S(2)}) copy-start(f32[48,384]{1,0:T(8,128)} %get-tuple-element.57) | copy-start | bytes 221188
  207.5 8.2 %copy-start.1 = (f32[192,384]{1,0:T(8,128)S(1)}, f32[192,384]{1,0:T(8,128)}, u32[]{:S(2)}) copy-start(f32[192,384]{1,0:T(8,128)} %get-tuple-element.58) | copy-start | bytes 884740
  207.6 8.9 %copy-start = (f32[48,1536]{1,0:T(8,128)S(1)}, f32[48,1536]{1,0:T(8,128)}, u32[]{:S(2)}) copy-start(f32[48,1536]{1,0:T(8,128)} %get-tuple-element.59) | copy-start | bytes 884740

commit v4 on v3

--- a/solution.py
+++ b/solution.py
@@ -438,19 +438,20 @@
             zero = jnp.zeros_like(qp)
             qh = (jnp.where(lane < HEAD_DIM, qp, zero), jnp.where(lane >= HEAD_DIM, qp, zero))
 
-            def scores(j, tops):
+            def scores(j, tops, diagonal=False):
                 at_keys = pl.ds(mult(j * qrows, qrows), qrows)
                 kj = ka[at_keys, lanes]
-                keep_it = jnp.logical_or(kpos <= qpos, j < quarter)
                 new = []
                 for h, sc in enumerate((sc0, sc1)):
-                    s = jnp.where(keep_it, dot_nt(kj, qh[h]), NEG_BIG)
+                    s = dot_nt(kj, qh[h])
+                    if diagonal:
+                        s = jnp.where(kpos <= qpos, s, NEG_BIG)
                     sc[at_keys, :] = s
                     new.append(jnp.maximum(tops[h], jnp.max(s.reshape(groups, 8, qrows), axis=0)))
                 return tuple(new)
 
             low = jnp.full((8, qrows), NEG_BIG, F32)
-            tops = lax.fori_loop(0, quarter + 1, scores, (low, low))
+            tops = scores(quarter, lax.fori_loop(0, quarter, scores, (low, low)), True)
             tops = tuple(jnp.max(t, axis=0, keepdims=True) for t in tops)
 
             def values(j, state):
@@ -636,7 +637,8 @@
 class Reduce:
     S1, R1, S2, R2, S3, R3, S4, R4, S5, R5 = range(10)
 
-    def __init__(self, grad, R, step, c0, C, zlist, bufs, out, out_c0, sems, k, where, turned):
+    def __init__(self, grad, R, step, c0, C, zlist, bufs, out, out_c0, sems, k, where, kind, turned):
+        self.kind = kind
         self.grad, self.R, self.step, self.c0, self.cn, self.zlist = grad, R, step, c0, C, zlist
         self.r1, self.r2, self.r3, self.r4, self.r5 = bufs
         self.out, self.out_c0, self.sems, self.k = out, out_c0, sems, k
@@ -706,15 +708,41 @@
             return carry
 
         lax.fori_loop(0, len(self.zlist) * 2, body, 0)
+        if self.kind == 2:
+            mate = z + 1 - 2 * (z % 2)
+            for slot, zz in enumerate((mate, 3 - mate)):
+                for w in range(2):
+                    rcopy(
+                        self.left(zz, w), self.r4.at[slot * 2 + w], self.sem(self.S4), self.sem(self.R4),
+                        dev(mate, y, c, x),
+                    ).start()
+            return
         to = dev(z, self.y3, c, self.x3)
         for zi, zz in enumerate(self.zlist):
             rcopy(self.at(zz, self.y3, c, self.x3), self.r3.at[zi], self.sem(self.S3), self.sem(self.R3), to).start()
 
+    def left_cut(self, zz, w):
+        o = self.o
+        return self.rows(zz, w * (1 - o) + self.y * o, self.c), self.cols(self.x * (1 - o) + w * o)
+
+    def left(self, zz, w):
+        return self.grad.at[self.left_cut(zz, w)]
+
     def first_hop(self, k):
         return [(k ^ 1, k, 0), ((3 - k) ^ 1, 3 - k, 1)]
 
     def tick4(self):
         z, y, c, x = self.z, self.y, self.c, self.x
+        if self.kind == 2:
+            wait_bytes(self.r4, self.sem(self.R4))
+            for w in range(2):
+                self.add(*self.left_cut(3 - z, w), self.r4[2 + w])
+                rcopy(
+                    self.left(3 - z, w), self.r5.at[w], self.sem(self.S5), self.sem(self.R5), dev(3 - z, y, c, x)
+                ).start()
+            for w in range(2):
+                self.add(*self.left_cut(z, w), self.r4[w])
+            return
         wait_bytes(self.r3, self.sem(self.R3))
 
         def body(zi, carry):
@@ -740,13 +768,22 @@
 
     def tick5(self):
         z, y, c, x = self.z, self.y, self.c, self.x
+        if self.kind == 2:
+            wait_bytes(self.r5, self.sem(self.R5))
+            for w in range(2):
+                self.add(*self.left_cut(z, w), self.r5[w])
+            rcopy(
+                self.at(z, self.y3, c, self.x3), self.r3.at[0], self.sem(self.S3), self.sem(self.R3),
+                dev(z, self.y3, c, self.x3),
+            ).start()
+            return
         k = self.zlist[0]
 
         def take(zz, slot):
             self.add(self.rows(zz, y, c), self.cols(x), self.r4[slot])
 
         def pass_on(zz):
-            rcopy(self.at(zz, y, c, x), self.r5, self.sem(self.S5), self.sem(self.R5), dev(zz, y, c, x)).start()
+            rcopy(self.at(zz, y, c, x), self.r5.at[0], self.sem(self.S5), self.sem(self.R5), dev(zz, y, c, x)).start()
 
         if self.every:
             wait_bytes(self.r4, self.sem(self.R4))
@@ -770,9 +807,10 @@
 
         @when(True if self.every else z == self.zlist[0])
         def _():
-            wait_bytes(self.r5, self.sem(self.R5))
+            last, sem = (self.r3, self.R3) if self.kind == 2 else (self.r5, self.R5)
+            wait_bytes(last, self.sem(sem))
             own = self.grad[self.rows(z, y, c), self.cols(x)].astype(F32)
-            self.out[:, self.out_c0:self.out_c0 + self.cn] = own + self.r5[...].astype(F32)
+            self.out[:, self.out_c0:self.out_c0 + self.cn] = own + last[0].astype(F32)
 
     def drain(self):
         z = self.z
@@ -794,7 +832,8 @@
                 wait_bytes(self.r5, self.sem(self.S5))
 
 
-TURNED_BACK = (3, 6)
+TURNED_BACK = ()
+KINDS_BACK = (2,) * 4 + (1,) * 9
 
 
 def reduce_shapes(width, ff):
@@ -802,11 +841,35 @@
     every = list(range(Z))
     half = width // X
     wide = ff // X
-    shapes = [("d", width // n, wide, k * (wide // 2), wide // 2, every, k * (wide // 2)) for k in range(2)]
+    shapes = [("d", width // n, wide, k * (wide // 4), wide // 4, every, k * (wide // 4)) for k in range(4)]
     shapes += [("u", ff // n, half, 0, half, [k], 0) for k in range(Z)]
     shapes += [("p", width // n, half, 0, half, every, 0)]
     shapes += [("q", 3 * width // n, half, 0, half, [k], 0) for k in range(Z)]
     return shapes
+
+
+PLAN = (
+    "f2", ("u0", 1), "f4", ("u0", 2), "f5", ("u2", 1), ("d0", 1), ("d1", 1), "f7", ("u2", 2), "f8", ("u1", 1), ("d0", 2),
+    "f9", ("d1", 2), "f10", ("u1", 2), ("u0", 3), "f11", ("u3", 1), ("d2", 1), ("d3", 1), "norm2", ("u2", 3),
+    "proj", ("pj", 1), ("u3", 2), ("d2", 2), ("d0", 3), ("d3", 2), "a00", ("pj", 2), ("d1", 3), "a10", ("u1", 3), ("d0", 4),
+    "a11", ("u0", 4), ("d1", 4), ("u2", 4), "a21", ("u3", 3), ("d0", 5), ("u0", 5), "a31", ("d2", 3), ("d1", 5), ("u2", 5),
+    "a40", ("d3", 3), "a50", ("pj", 3), ("d2", 4), ("u1", 4), "a51", ("u3", 4), "norm1", ("d3", 4), "qa", ("q0", 1),
+    ("pj", 4), "merge", ("d2", 5), "qb", ("q1", 1), ("u1", 5), ("q0", 2), "qc", ("q2", 1), ("u3", 5), "qd", ("q3", 1),
+    ("q1", 2), ("d3", 5), "da", ("q2", 2), ("q3", 2), ("q0", 3), ("pj", 5), "ln", ("x", 0), ("u0", 6), ("u2", 6), ("d0", 6),
+    ("d1", 6), ("x", 1), ("v", 0), ("q1", 3), ("d2", 6), ("u1", 6), ("u3", 6), ("x", 2), ("v", 1), ("q2", 3), ("d3", 6),
+    ("x", 3), ("q3", 3), ("q0", 4), ("v", 2), ("pj", 6), ("q1", 4), ("q0", 5), ("v", 3), ("q2", 4), ("q1", 5), ("q3", 4),
+    ("q2", 5), ("v", 4), ("q3", 5), ("q0", 6), ("q1", 6), ("q2", 6), ("q3", 6),
+)
+
+
+def part_actions(plan):
+    parts, now = {}, None
+    for item in plan:
+        if isinstance(item, str):
+            now = parts.setdefault(item, [])
+        else:
+            now.append(item)
+    return parts
 
 
 def backward_kernel(*refs):
@@ -815,7 +878,7 @@
         "lse_i", "r_i", "a2_i", "hd_i", "gp_i", "vec_i", "out_i", "og_q", "og_p", "og_u", "og_d", "osum", "ret",
         "out_n", "wq", "wp", "xr", "g", "qs", "ka", "va", "at", "lse", "r", "a2", "vec", "gt", "d2", "dr", "drl",
         "do", "gq", "gp_", "gu", "gd", "wd_t", "wu_t", "hd_t", "gp_t", "dka", "dva", "own_v", "sv", "rk", "rv", "dm",
-        "vs", "vr", "bub", "ret_v", "lsem", "tsem", "rsem", "msem", "vsem",
+        "vs", "vr", "bub", "lsem", "tsem", "rsem", "msem", "vsem",
     )
     env = dict(zip(names, refs[: len(names)]))
     env.update(a1=env["a2"], own_k=env["d2"], sk=env["drl"], dx=env["do"])
@@ -869,27 +932,27 @@
     for name in ("r", "vec", "wp", "at", "qs", "ka", "va", "lse", "xr", "wq"):
         loads[name].start()
 
-    entered()
-
-    for i in range(2):
-        same = jnp.logical_and(x == c, x == i)
-        src = e.out_i.at[pl.ds(i * qrows, qrows)]
-        dst = e.out_n.at[pl.ds(mult(((i + c) % 2) * qrows, qrows), qrows)]
-
-        @pl.when(same)
-        def _(src=src, dst=dst):
-            lcopy(src, dst, e.msem.at[1]).start()
-
-        @pl.when(jnp.logical_not(same))
-        def _(src=src, dst=dst, i=i):
-            rcopy(src, dst, e.msem.at[0], e.msem.at[1], dev(z, y, x, i)).start()
-
     grads = {"q": (e.gq, e.og_q), "p": (e.gp_, e.og_p), "u": (e.gu, e.og_u), "d": (e.gd, e.og_d)}
     chunks = []
     for k, (name, R, step, c0, cn, zlist, oc) in enumerate(reduce_shapes(width, ff)):
         grad, out = grads[name]
-        chunks.append(Reduce(grad, R, step, c0, cn, zlist, bufs[5 * k:5 * k + 5], out, oc, e.rsem, k, where, k in TURNED_BACK))
-    dA, dB, u0, u1, u2, u3, pj, q0, q1, q2, q3 = chunks
+        chunks.append(Reduce(grad, R, step, c0, cn, zlist, bufs[5 * k:5 * k + 5], out, oc, e.rsem, k, where, KINDS_BACK[k], k in TURNED_BACK))
+    names_of = ("d0", "d1", "d2", "d3", "u0", "u1", "u2", "u3", "pj", "q0", "q1", "q2", "q3")
+    by_name = dict(zip(names_of, chunks))
+    parts = part_actions(PLAN)
+
+    def after(part):
+        for name, k in parts.get(part, ()):
+            if name in by_name:
+                ch = by_name[name]
+                (ch.start, ch.tick2, ch.tick3, ch.tick4, ch.tick5, ch.tick6)[k - 1]()
+            elif name == "x":
+                give(k)
+            else:
+                land(k)
+                if k < 4:
+                    hop(k + 1)
+
 
     my_len = live_length(e.len_ref, e.deal_ref, (z * Y + y) * C + x)
     rowpos = lax.broadcasted_iota(jnp.int32, (lrows, 1), 0)
@@ -907,12 +970,7 @@
     loads["a2"].wait()
 
     ff_tiles = ff // tile
-    plan = {
-        2: [u0.start], 4: [u0.tick2], 5: [u2.start, dA.start], 7: [u2.tick2], 8: [u1.start, u0.tick3],
-        9: [dA.tick2], 10: [u1.tick2, u2.tick3], 11: [u3.start, dB.start, u0.tick4],
-    }
-
-    def ffn(idx, carry):
+    def ffn(idx, carry, acting=True):
         slot = idx % 2
         n = tile_of(idx)
         cut = pl.ds(mult(n * tile, tile), tile)
@@ -929,14 +987,35 @@
         e.gd[:, cut] = dot_nn(e.gt[...], e.hd_t[slot]).astype(BF)
         e.gu[cut, :] = dot_tn(du, e.a2[...]).astype(BF)
         e.d2[...] += dot_nn(du, e.wu_t[slot])
-        for at_idx, acts in plan.items():
-            @pl.when(idx == at_idx)
-            def _(acts=acts):
-                for act in acts:
-                    act()
+        for k in range(2, ff_tiles) if acting else ():
+            if f"f{k}" in parts:
+                @pl.when(idx == k)
+                def _(k=k):
+                    after(f"f{k}")
+
         return carry
 
-    lax.fori_loop(0, ff_tiles, ffn, 0)
+    def ffn_first(idx, carry):
+        return ffn(idx, carry, False)
+
+    lax.fori_loop(0, 2, ffn_first, 0)
+
+    entered()
+
+    for i in range(2):
+        same = jnp.logical_and(x == c, x == i)
+        src = e.out_i.at[pl.ds(i * qrows, qrows)]
+        dst = e.out_n.at[pl.ds(mult(((i + c) % 2) * qrows, qrows), qrows)]
+
+        @pl.when(same)
+        def _(src=src, dst=dst):
+            lcopy(src, dst, e.msem.at[1]).start()
+
+        @pl.when(jnp.logical_not(same))
+        def _(src=src, dst=dst, i=i):
+            rcopy(src, dst, e.msem.at[0], e.msem.at[1], dev(z, y, x, i)).start()
+
+    lax.fori_loop(2, ff_tiles, ffn, 0)
 
     loads["r"].wait()
     loads["vec"].wait()
@@ -960,6 +1039,8 @@
 
     sum_g2, sum_c2, sum_bp = lax.fori_loop(0, rows // lrows, norm_two, (blank, blank, blank))
 
+    after("norm2")
+
     loads["wp"].wait()
     loads["at"].wait()
 
@@ -970,9 +1051,7 @@
         return carry
 
     lax.fori_loop(0, steps, proj_back, 0)
-    pj.start()
-    u3.tick2()
-    u0.tick5()
+    after("proj")
 
     for name in ("qs", "ka", "va", "lse"):
         loads[name].wait()
@@ -983,11 +1062,6 @@
     def split(v):
         zero = jnp.zeros_like(v)
         return jnp.where(lane < HEAD_DIM, v, zero), jnp.where(lane >= HEAD_DIM, v, zero)
-
-    between = {
-        (0, 0): [dB.tick2, pj.tick2, dA.tick3], (1, 1): [u1.tick3], (2, 0): [u2.tick4], (2, 1): [u3.tick3],
-        (3, 0): [u2.tick5], (4, 0): [dB.tick3, u1.tick4], (5, 0): [u1.tick5], (5, 1): [pj.tick3],
-    }
 
     def pair_body(p, carry):
         lanes = pl.ds(mult(p * 128, 128), 128)
@@ -1003,14 +1077,15 @@
             delta = [jnp.sum(prod[h * HEAD_DIM:(h + 1) * HEAD_DIM], axis=0, keepdims=True) for h in range(2)]
             logs = [e.lse[p, i * 2 + h:i * 2 + h + 1, :] for h in range(2)]
 
-            def keys(j, dq):
+            def keys(j, dq, diagonal=False):
                 at_keys = pl.ds(mult(j * qrows, qrows), qrows)
                 kj, vj = e.ka[at_keys, lanes], e.va[at_keys, lanes]
                 kt = kj.T
-                keep_it = jnp.logical_or(kpos <= qpos, j < quarter)
                 probs, grads_s, new = [], [], []
                 for h in range(2):
-                    s = jnp.where(keep_it, dot_nt(kj, qh[h]), NEG_BIG)
+                    s = dot_nt(kj, qh[h])
+                    if diagonal:
+                        s = jnp.where(kpos <= qpos, s, NEG_BIG)
                     pt = jnp.exp(s - logs[h])
                     ds = (pt * (dot_nt(vj, doh[h]) - delta[h])).astype(BF)
                     probs.append(pt.astype(BF))
@@ -1021,14 +1096,15 @@
                 return tuple(new)
 
             none = jnp.zeros((HEAD_DIM, qrows), F32)
-            dq = lax.fori_loop(0, quarter + 1, keys, (none, none))
+            dq = lax.fori_loop(0, quarter, keys, (none, none))
+            dq = keys(quarter, dq, True)
             e.dm[own, lanes] = (jnp.concatenate(dq, axis=0).T * HEAD_DIM ** -0.5).astype(BF)
-            for (at_p, at_i), acts in between.items():
-                if at_i == i:
-                    @pl.when(p == at_p)
-                    def _(acts=acts):
-                        for act in acts:
-                            act()
+            for k in range(pairs):
+                if f"a{k}{i}" in parts:
+                    @pl.when(p == k)
+                    def _(k=k, i=i):
+                        after(f"a{k}{i}")
+
         for i in range(2):
             own = slice(i * qrows, (i + 1) * qrows)
             e.own_k[own, lanes] = e.dka[at_quarter(quarters[i]), :]
@@ -1056,6 +1132,7 @@
         return carry
 
     lax.fori_loop(0, rows // lrows, norm_one, 0)
+    after("norm1")
 
     def qkv_grad(n, carry):
         cut = pl.ds(mult(n * tile, tile), tile)
@@ -1063,8 +1140,7 @@
         return carry
 
     lax.fori_loop(0, 3, qkv_grad, 0)
-    q0.start()
-    dA.tick4()
+    after("qa")
     wait_bytes(e.rk, e.msem.at[3])
     wait_bytes(e.rv, e.msem.at[5])
     for part, (mine, got) in enumerate(((e.own_k, e.rk), (e.own_v, e.rv))):
@@ -1076,7 +1152,10 @@
             return carry
 
         lax.fori_loop(0, rows // lrows, merge, 0)
-    u3.tick4()
+    after("merge")
+    for name, first, stop in (("qb", 3, 5), ("qc", 5, 7), ("qd", 7, 9)):
+        lax.fori_loop(first, stop, qkv_grad, 0)
+        after(name)
     loads["wq"].wait()
 
     def input_back(n, carry):
@@ -1085,8 +1164,7 @@
         return carry
 
     lax.fori_loop(0, steps, input_back, 0)
-    q0.tick2()
-    pj.tick4()
+    after("da")
 
     def norm_one_back(k, sums):
         at_rows = pl.ds(mult(k * lrows, lrows), lrows)
@@ -1099,8 +1177,6 @@
         return sums[0] + jnp.sum(da * n1, axis=0, keepdims=True), sums[1] + jnp.sum(da, axis=0, keepdims=True)
 
     sum_g1, sum_c1 = lax.fori_loop(0, rows // lrows, norm_one_back, (blank, blank))
-    dB.tick4()
-    dA.tick5()
 
     e.vs[0] = jnp.zeros_like(e.vs[0])
     for row, value in ((G1, sum_g1), (C1, sum_c1), (BP, sum_bp), (G2, sum_g2), (C2, sum_c2), (BD, total_bd)):
@@ -1135,55 +1211,20 @@
 
         @pl.when(mine)
         def _():
-            lcopy(src, e.ret_v.at[slot], e.msem.at[7]).start()
+            lcopy(src, e.ret.at[slot], e.msem.at[7]).start()
 
         @pl.when(jnp.logical_not(mine))
         def _():
-            rcopy(src, e.ret_v.at[slot], e.msem.at[6], e.msem.at[7], {"dp": td, "cp": i}).start()
+            rcopy(src, e.ret.at[slot], e.msem.at[6], e.msem.at[7], {"dp": td, "cp": i}).start()
 
         return carry
 
     share = per_quarter // 2
-    lax.fori_loop(0, share, give_back, 0)
-    lax.fori_loop(3, 5, qkv_grad, 0)
-    q1.start()
-    lax.fori_loop(share, 2 * share, give_back, 0)
-    lax.fori_loop(5, 7, qkv_grad, 0)
-    q2.start()
-    lax.fori_loop(2 * share, 3 * share, give_back, 0)
-    u3.tick5()
-    lax.fori_loop(7, 9, qkv_grad, 0)
-    q3.start()
-    lax.fori_loop(3 * share, 4 * share, give_back, 0)
-    q0.tick3()
-    q1.tick2()
-    pj.tick5()
-    land(0)
-    hop(1)
-    for ch in (u0, u2, u1):
-        ch.tick6()
-    q2.tick2()
-    q3.tick2()
-    land(1)
-    hop(2)
-    dB.tick5()
-    dA.tick6()
-    q0.tick4()
-    q1.tick3()
-    land(2)
-    hop(3)
-    q2.tick3()
-    q3.tick3()
-    q1.tick4()
-    land(3)
-    hop(4)
-    q2.tick4()
-    q3.tick4()
-    u3.tick6()
-    q0.tick5()
-    pj.tick6()
-    q1.tick5()
-    land(4)
+
+    def give(k):
+        lax.fori_loop(k * share, (k + 1) * share, give_back, 0)
+
+    after("ln")
     own = width // (Z * Y * C)
     e.osum[0:6, :] = pltpu.roll(e.vs[5, 0:6, :], (width - d * own) % width, 1)[:, :tile]
     long = ff // (Z * Y * C)
@@ -1192,14 +1233,7 @@
         e.vs[5, pl.ds(BU + d // per_row, 1), :], (width - (d % per_row) * long) % width, 1
     )[:, :tile]
     e.osum[7:8, :] = jnp.zeros((1, tile), F32)
-    q2.tick5()
-    q3.tick5()
-    dB.tick6()
     wait_bytes(e.dx, e.msem.at[7])
-    for s in range(e.ret.shape[0]):
-        e.ret[s] = e.ret_v[jnp.clip(e.deal_ref[s], 0, e.ret.shape[0] - 1)]
-    for ch in (q0, q1, q2, q3):
-        ch.tick6()
 
     for ch in chunks:
         ch.drain()
@@ -1252,13 +1286,14 @@
         vm((2, width, 256), BF), vm((2, 256, width), BF), vm((2, rows, 256), BF), vm((2, rows, 256), BF),
         vm((keys, 128), F32), vm((keys, 128), F32),
         acts32, acts, acts, acts, vm((rows, 3 * width), BF),
-        vm((6, 16, width), F32), vm((5, 16, width), F32), vm((ff // 256, 1, 256), F32), vm((n, small, width), BF),
-        pltpu.SemaphoreType.DMA((12,)), pltpu.SemaphoreType.DMA((4, 2)), pltpu.SemaphoreType.DMA((11, 10)),
+        vm((6, 16, width), F32), vm((5, 16, width), F32), vm((ff // 256, 1, 256), F32),
+        pltpu.SemaphoreType.DMA((12,)), pltpu.SemaphoreType.DMA((4, 2)), pltpu.SemaphoreType.DMA((13, 10)),
         pltpu.SemaphoreType.DMA((8,)), pltpu.SemaphoreType.DMA((2, 5)),
     ]
-    for _, R, _, _, cn, zlist, _ in reduce_shapes(width, ff):
+    for kind, (_, R, _, _, cn, zlist, _) in zip(KINDS_BACK, reduce_shapes(width, ff)):
         k = len(zlist)
-        scratch += [vm((2 * k, 2, R, cn), BF), vm((2 * k, R, cn), BF), vm((k, R, cn), BF), vm((2, R, cn), BF), vm((R, cn), BF)]
+        last = (1, 4, 2) if kind == 2 else (k, 2, 1)
+        scratch += [vm((2 * k, 2, R, cn), BF)] + [vm((m, R, cn), BF) for m in (2 * k,) + last]
     anyspec = pl.BlockSpec(memory_space=pl.ANY)
     smem = pl.BlockSpec(memory_space=pltpu.SMEM)
     vmem = pl.BlockSpec(memory_space=pltpu.VMEM)
@@ -1266,13 +1301,38 @@
         backward_kernel,
         out_shape=outs,
         in_specs=[smem, smem] + [anyspec] * len(saved),
-        out_specs=[vmem] * 6 + [anyspec],
+        out_specs=[vmem] * 5 + [anyspec] * 2,
         scratch_shapes=scratch,
         compiler_params=pltpu.CompilerParams(
             collective_id=1, has_side_effects=True, vmem_limit_bytes=67043328
         ),
         name="backward",
     )(lengths, dealing, *saved)
+
+
+def finish_kernel(deal_ref, gq, gp, gu, gd, sums, ret, out, grad_o, out_o, gq_o, gp_o, gu_o, gd_o, *rows_o):
+    for s in range(ret.shape[0]):
+        grad_o[s] = ret[deal_ref[s]]
+    for src, dst in ((out, out_o), (gq, gq_o), (gp, gp_o), (gu, gu_o), (gd, gd_o)):
+        dst[...] = src[...]
+    for k, row in enumerate(rows_o):
+        row[...] = sums[k:k + 1, :row.shape[1]]
+
+
+def finish(dealing, grads, sums, ret, out, own, long):
+    def like(a):
+        return jax.ShapeDtypeStruct(a.shape, a.dtype)
+
+    outs = [like(ret), like(out)] + [like(g) for g in grads]
+    outs += [jax.ShapeDtypeStruct((1, own), F32)] * 6 + [jax.ShapeDtypeStruct((1, long), F32)]
+    vmem = pl.BlockSpec(memory_space=pltpu.VMEM)
+    return pl.pallas_call(
+        finish_kernel,
+        out_shape=outs,
+        in_specs=[pl.BlockSpec(memory_space=pltpu.SMEM)] + [vmem] * 7,
+        out_specs=[vmem] * len(outs),
+        name="finish",
+    )(dealing, *grads, sums, ret, out)
 
 
 def slice_plan(
@@ -1284,11 +1344,13 @@
         v[None] for v in (first_gain, first_shift, proj_bias, second_gain, second_shift, down_bias, up_bias)
     ]
     saved = forward(lengths, dealing, cotangent[0], x_source, shards, vectors)
-    gq, gp, gu, gd, sums, input_grad, out = backward(lengths, dealing, saved, shards)
-    own, long = first_gain.shape[0], up_bias.shape[0]
+    gq, gp, gu, gd, sums, ret, out = backward(lengths, dealing, saved, shards)
+    done = finish(dealing, (gq, gp, gu, gd), sums, ret, out, first_gain.shape[0], up_bias.shape[0])
+    input_grad, output, gq, gp, gu, gd = done[:6]
+    by_row = [v.reshape(-1) for v in done[6:]]
     return (
-        out[None], input_grad, gq.T, gp.T, gu.T, gd.T,
-        sums[G1, :own], sums[C1, :own], sums[BP, :own], sums[G2, :own], sums[C2, :own], sums[6, :long], sums[BD, :own],
+        output[None], input_grad, gq.T, gp.T, gu.T, gd.T,
+        by_row[G1], by_row[C1], by_row[BP], by_row[G2], by_row[C2], by_row[6], by_row[BD],
     )
 
 

time: 218 us -> 208 us (0.954)
  local copies, waits for them, and re-layouts: 9.65 us -> 0 us
    unnamed x14 -> x0, local copies, waits for them, and re-layouts: 6.89 us -> none
    pallas_call x1, Pallas kernels: 112 us -> 109 us  [backward(): pl.pallas_call(backward_kernel, out_shape=outs, in_specs=[smem, smem] + [...]
    pallas_call x0 -> x1, Pallas kernels: none -> 3.18 us  [finish(): pl.pallas_call(finish_kernel, out_shape=outs, in_specs=[pl.BlockSpec(memo...]
where the time goes in v4:
time: 208 us; the launch traced here: 207 us
  Pallas kernels  207 us (100%)
    pallas_call x1, Pallas kernels, backward(): pl.pallas_call(backward_kernel, out_shape=outs, in_specs=[smem, smem] + [...  109 us
    pallas_call x1, Pallas kernels, forward(): pl.pallas_call(forward_kernel, out_shape=outs, in_specs=[smem, smem, anys...  94.8 us

profile of v4, /device:TPU:0, one launch (start us, length us, event | category | flops | bytes accessed | tf_op | source)
XLA Modules:
  0.0 207.4 jit_solution(2986649822252898446)
XLA Ops:
  0.6 94.8 %forward.1 = (bf16[2304,768]{1,0:T(8,128)(2,1)}, bf16[768,768]{1,0:T(8,128)(2,1)}, bf16[3072,768]{1,0:T(8,128)(2,1)}, bf16[768,3072]{1,0:T(8,128)(2,1)}, bf16[51...) custom-call(s32[16]{0:T(128)} %refs_0_.1, ...), custom_call_target="tpu_custom_call" | custom-call | tf_op jit(solution)/shard_map/forward/pallas_call | solution.py:618
  95.5 108.6 %backward.1 = (f32[144,384]{1,0:T(8,128)}, f32[48,384]{1,0:T(8,128)}, f32[192,384]{1,0:T(8,128)}, f32[48,1536]{1,0:T(8,128)}, f32[8,256]{1,0:T(8,128)}, /*index=...) custom-call(s32[16]{0:T(128)} %refs_0_.1, s32[16]{0:T(128)} %deal_ref.3, bf16[2304,768]{1,0:T(8,128)(2,1)} %get-tuple-element.50.refs_2_, ...), custom_call_target="tpu_custom_call" | custom-call | tf_op jit(solution)/shard_map/backward/pallas_call | solution.py:1300
  204.1 3.2 %finish.1 = (bf16[16,32,768]{2,1,0:T(8,128)(2,1)}, bf16[512,768]{1,0:T(8,128)(2,1)}, f32[144,384]{1,0:T(8,128)}, f32[48,384]{1,0:T(8,128)}, f32[192,384]{1,0:T(8...) custom-call(s32[16]{0:T(128)} %deal_ref.3, ...), custom_call_target="tpu_custom_call" | custom-call | tf_op jit(solution)/shard_map/finish/pallas_call | solution.py:1329

commit v5 on v4

--- a/solution.py
+++ b/solution.py
@@ -259,15 +259,16 @@
 TICKS = ("tick1", "tick2", "tick3", "tick4")
 KINDS = (1, 1, 1, 1, 2, 2, 1, 2, 2, 1, 2, 2)
 TURNED = (7,)
-COT_STEPS = (6, 8)
+COT_STEPS = (6, 6, 6, 6, 8, 8, 8, 8)
 LAGS = ((0, 1, 2, 3),) * 4 + ((0, 1, 2, 4),) * 8
 
 
 def forward_kernel(
-    len_ref, deal_ref, cot, x_in, sq, sp, su, sd, v_g1, v_c1, v_bp, v_g2, v_c2, v_bd, v_bu,
+    len_ref, deal_ref, cot, x_any, sq_any, sp_any, su_any, sd_any, g1_any, c1_any, bp_any, g2_any, c2_any, bd_any, bu_any,
     wq_o, wp_o, wu_o, wd_o, xr_o, gw_o, qs_o, ka_o, va_o, at_o, lse_o, r_o, a2_o, hd_o, gp_o, vec_o, out_o,
     wq, wp, wu, wd, xr, a1, qs, ka, va, at, lse, r, a2, hd, gp, vg, vec, bu3, sc0, sc1, outw, xg, acc,
-    gsem, vsem, msem, osem,
+    x_in, sq, sp, su, sd, v_g1, v_c1, v_bp, v_g2, v_c2, v_bd, v_bu,
+    gsem, vsem, msem, osem, isem,
 ):
     where = coords()
     z, y, c, x, d = where
@@ -275,15 +276,23 @@
     rows = xr.shape[0]
     qrows = rows // 2
     small = x_in.shape[1]
+    sources = (sq_any, sp_any, su_any, sd_any, g1_any, c1_any, bp_any, g2_any, c2_any, bd_any, bu_any, x_any)
+    places = (sq, sp, su, sd, v_g1, v_c1, v_bp, v_g2, v_c2, v_bd, v_bu, x_in)
+    loads = [pltpu.make_async_copy(s, t, isem.at[k]) for k, (s, t) in enumerate(zip(sources, places))]
+    for load in loads:
+        load.start()
     pairs = width // 128
     tile = 256
 
     entered = enter(Z * Y * C * X)
 
     n = Z * Y * C
-    for shard, full in ((sq, wq), (sp, wp), (su, wu), (sd, wd)):
+    for load, shard, full in zip(loads, (sq, sp, su, sd), (wq, wp, wu, wd)):
+        load.wait()
         own, long = shard.shape
         full[pl.ds(mult(d * own, 16), own), pl.ds(mult(x * long, 128), long)] = shard[...].astype(BF)
+    for load in loads[4:]:
+        load.wait()
     vg[d] = jnp.zeros(vg.shape[1:], BF)
     own = v_g1.shape[1]
     seven = jnp.concatenate([v[...] for v in (v_g1, v_c1, v_bp, v_g2, v_c2, v_bd)], axis=0).astype(BF)
@@ -309,10 +318,12 @@
         Gather(p, gsem, k, wu, where, KINDS[k], k in TURNED) for k, p in enumerate(gather_chunks(wq, wp, wu, wd))
     ]
 
-    def send_cot(b):
+    def send_cot(k):
+        b, part = k // 4, k % 4
+        some = qrows // 4
         core_b = (x + b) % 2
-        src_b = cot.at[pl.ds(b * qrows, qrows)]
-        dst_b = gw_o.at[pl.ds(mult(x * qrows, qrows), qrows)]
+        src_b = cot.at[pl.ds(b * qrows + part * some, some)]
+        dst_b = gw_o.at[pl.ds(mult(x * qrows + part * some, some), some)]
         same = jnp.logical_and(core_b == c, c == x)
 
         @pl.when(same)
@@ -353,8 +364,9 @@
             chunks[s + ahead].start()
         if s < 4:
             lax.fori_loop(s * slots // 4, (s + 1) * slots // 4, deal_out, 0)
-        if s in COT_STEPS:
-            send_cot(COT_STEPS.index(s))
+        for k, at_step in enumerate(COT_STEPS):
+            if at_step == s:
+                send_cot(k)
         for n in range(4):
             for k in range(len(chunks)):
                 if k + LAGS[k][n] == s:
@@ -609,16 +621,16 @@
         vm((rows, width), BF), vm((rows, ff), BF), vm((rows, ff), BF), vm((Z * Y * C, 16, width), BF),
         vm((16, width), F32), vm((ff // 256, 1, 256), F32), vm((keys, rows // 2), F32), vm((keys, rows // 2), F32),
         vm((rows, width), BF), vm(x_source.shape, BF), vm((rows, width), F32),
+        vm(x_source.shape, BF), *[vm(a.shape, F32) for a in (*shards, *vectors)],
         pltpu.SemaphoreType.DMA((N_GATHER, 2, 5)), pltpu.SemaphoreType.DMA((2, 4)), pltpu.SemaphoreType.DMA((8,)),
-        pltpu.SemaphoreType.DMA((24,)),
+        pltpu.SemaphoreType.DMA((24,)), pltpu.SemaphoreType.DMA((12,)),
     ]
     anyspec = pl.BlockSpec(memory_space=pl.ANY)
     smem = pl.BlockSpec(memory_space=pltpu.SMEM)
-    vmem = pl.BlockSpec(memory_space=pltpu.VMEM)
     return pl.pallas_call(
         forward_kernel,
         out_shape=outs,
-        in_specs=[smem, smem, anyspec] + [vmem] * 12,
+        in_specs=[smem, smem] + [anyspec] * 13,
         out_specs=[anyspec] * len(outs),
         scratch_shapes=scratch,
         compiler_params=pltpu.CompilerParams(
@@ -849,16 +861,18 @@
 
 
 PLAN = (
-    "f2", ("u0", 1), "f4", ("u0", 2), "f5", ("u2", 1), ("d0", 1), ("d1", 1), "f7", ("u2", 2), "f8", ("u1", 1), ("d0", 2),
-    "f9", ("d1", 2), "f10", ("u1", 2), ("u0", 3), "f11", ("u3", 1), ("d2", 1), ("d3", 1), "norm2", ("u2", 3),
-    "proj", ("pj", 1), ("u3", 2), ("d2", 2), ("d0", 3), ("d3", 2), "a00", ("pj", 2), ("d1", 3), "a10", ("u1", 3), ("d0", 4),
-    "a11", ("u0", 4), ("d1", 4), ("u2", 4), "a21", ("u3", 3), ("d0", 5), ("u0", 5), "a31", ("d2", 3), ("d1", 5), ("u2", 5),
-    "a40", ("d3", 3), "a50", ("pj", 3), ("d2", 4), ("u1", 4), "a51", ("u3", 4), "norm1", ("d3", 4), "qa", ("q0", 1),
-    ("pj", 4), "merge", ("d2", 5), "qb", ("q1", 1), ("u1", 5), ("q0", 2), "qc", ("q2", 1), ("u3", 5), "qd", ("q3", 1),
-    ("q1", 2), ("d3", 5), "da", ("q2", 2), ("q3", 2), ("q0", 3), ("pj", 5), "ln", ("x", 0), ("u0", 6), ("u2", 6), ("d0", 6),
-    ("d1", 6), ("x", 1), ("v", 0), ("q1", 3), ("d2", 6), ("u1", 6), ("u3", 6), ("x", 2), ("v", 1), ("q2", 3), ("d3", 6),
-    ("x", 3), ("q3", 3), ("q0", 4), ("v", 2), ("pj", 6), ("q1", 4), ("q0", 5), ("v", 3), ("q2", 4), ("q1", 5), ("q3", 4),
-    ("q2", 5), ("v", 4), ("q3", 5), ("q0", 6), ("q1", 6), ("q2", 6), ("q3", 6),
+    "f2", ("u0", 1), "f4", ("u0", 2), "f5", ("u2", 1), ("d0", 1), ("d1", 1), "f7", ("u2", 2), "f8", ("u1", 1),
+    ("d0", 2), "f9", ("d1", 2), "f10", ("u1", 2), ("u0", 3), "f11", ("u3", 1), ("d2", 1), ("d3", 1), "norm2",
+    ("u2", 3), "proj", ("pj", 1), ("u3", 2), ("d2", 2), ("d0", 3), ("d3", 2), "a00", ("pj", 2), ("d1", 3), ("o", 0),
+    "a01", ("o", 1), "a10", ("u1", 3), ("d0", 4), ("o", 2), "a11", ("u0", 4), ("d1", 4), ("u2", 4), ("o", 3), "a20",
+    ("o", 4), "a21", ("u3", 3), ("d0", 5), ("u0", 5), ("o", 5), "a30", ("o", 6), "a31", ("d2", 3), ("d1", 5),
+    ("u2", 5), ("o", 7), "a40", ("d3", 3), "a50", ("pj", 3), ("d2", 4), ("u1", 4), "a51", ("u3", 4), "norm1",
+    ("d3", 4), "qa", ("q0", 1), ("pj", 4), "merge", ("d2", 5), "qb", ("q1", 1), ("u1", 5), ("q0", 2), "qc", ("q2", 1),
+    ("u3", 5), "qd", ("q3", 1), ("q1", 2), ("d3", 5), "da", ("q3", 2), ("q0", 3), ("pj", 5), "ln", ("u2", 6),
+    ("q2", 2), ("x", 0), ("u0", 6), ("d0", 6), ("d1", 6), ("x", 1), ("v", 0), ("q1", 3), ("d2", 6), ("u1", 6),
+    ("u3", 6), ("x", 2), ("v", 1), ("q2", 3), ("d3", 6), ("x", 3), ("q3", 3), ("q0", 4), ("v", 2), ("pj", 6),
+    ("q1", 4), ("q0", 5), ("v", 3), ("q2", 4), ("q1", 5), ("q3", 4), ("q2", 5), ("v", 4), ("q3", 5), ("q0", 6),
+    ("q1", 6), ("q2", 6), ("q3", 6),
 )
 
 
@@ -932,6 +946,21 @@
     for name in ("r", "vec", "wp", "at", "qs", "ka", "va", "lse", "xr", "wq"):
         loads[name].start()
 
+    def send_out(k):
+        i, part = k // 4, k % 4
+        some = qrows // 4
+        same = jnp.logical_and(x == c, x == i)
+        src = e.out_i.at[pl.ds(i * qrows + part * some, some)]
+        dst = e.out_n.at[pl.ds(mult(((i + c) % 2) * qrows + part * some, some), some)]
+
+        @pl.when(same)
+        def _():
+            lcopy(src, dst, e.msem.at[1]).start()
+
+        @pl.when(jnp.logical_not(same))
+        def _():
+            rcopy(src, dst, e.msem.at[0], e.msem.at[1], dev(z, y, x, i)).start()
+
     grads = {"q": (e.gq, e.og_q), "p": (e.gp_, e.og_p), "u": (e.gu, e.og_u), "d": (e.gd, e.og_d)}
     chunks = []
     for k, (name, R, step, c0, cn, zlist, oc) in enumerate(reduce_shapes(width, ff)):
@@ -948,6 +977,8 @@
                 (ch.start, ch.tick2, ch.tick3, ch.tick4, ch.tick5, ch.tick6)[k - 1]()
             elif name == "x":
                 give(k)
+            elif name == "o":
+                send_out(k)
             else:
                 land(k)
                 if k < 4:
@@ -1001,19 +1032,6 @@
     lax.fori_loop(0, 2, ffn_first, 0)
 
     entered()
-
-    for i in range(2):
-        same = jnp.logical_and(x == c, x == i)
-        src = e.out_i.at[pl.ds(i * qrows, qrows)]
-        dst = e.out_n.at[pl.ds(mult(((i + c) % 2) * qrows, qrows), qrows)]
-
-        @pl.when(same)
-        def _(src=src, dst=dst):
-            lcopy(src, dst, e.msem.at[1]).start()
-
-        @pl.when(jnp.logical_not(same))
-        def _(src=src, dst=dst, i=i):
-            rcopy(src, dst, e.msem.at[0], e.msem.at[1], dev(z, y, x, i)).start()
 
     lax.fori_loop(2, ff_tiles, ffn, 0)
 

time: 208 us -> 204 us (0.981)
  Pallas kernels: 207 us -> 203 us
    pallas_call x1, Pallas kernels: 109 us -> 106 us  [backward(): pl.pallas_call(backward_kernel, out_shape=outs, in_specs=[smem, smem] + [...]
where the time goes in v5:
time: 204 us
  Pallas kernels  203 us (100%)
    pallas_call x1, Pallas kernels, backward(): pl.pallas_call(backward_kernel, out_shape=outs, in_specs=[smem, smem] + [...  106 us
    pallas_call x1, Pallas kernels, forward(): pl.pallas_call(forward_kernel, out_shape=outs, in_specs=[smem, smem] + [a...  94 us

profile of v5, /device:TPU:0, one launch (start us, length us, event | category | flops | bytes accessed | tf_op | source)
XLA Modules:
  0.0 204.0 jit_solution(12749264271347858501)
XLA Ops:
  0.6 94.0 %forward.1 = (bf16[2304,768]{1,0:T(8,128)(2,1)}, bf16[768,768]{1,0:T(8,128)(2,1)}, bf16[3072,768]{1,0:T(8,128)(2,1)}, bf16[768,3072]{1,0:T(8,128)(2,1)}, bf16[51...) custom-call(s32[16]{0:T(128)} %refs_0_.1, ...), custom_call_target="tpu_custom_call" | custom-call | tf_op jit(solution)/shard_map/forward/pallas_call | solution.py:630
  94.7 106.0 %backward.1 = (f32[144,384]{1,0:T(8,128)}, f32[48,384]{1,0:T(8,128)}, f32[192,384]{1,0:T(8,128)}, f32[48,1536]{1,0:T(8,128)}, f32[8,256]{1,0:T(8,128)}, /*index=...) custom-call(s32[16]{0:T(128)} %refs_0_.1, s32[16]{0:T(128)} %deal_ref.3, bf16[2304,768]{1,0:T(8,128)(2,1)} %get-tuple-element.50.refs_2_, ...), custom_call_target="tpu_custom_call" | custom-call | tf_op jit(solution)/shard_map/backward/pallas_call | solution.py:1318
  200.7 3.2 %finish.1 = (bf16[16,32,768]{2,1,0:T(8,128)(2,1)}, bf16[512,768]{1,0:T(8,128)(2,1)}, f32[144,384]{1,0:T(8,128)}, f32[48,384]{1,0:T(8,128)}, f32[192,384]{1,0:T(8...) custom-call(s32[16]{0:T(128)} %deal_ref.3, ...), custom_call_target="tpu_custom_call" | custom-call | tf_op jit(solution)/shard_map/finish/pallas_call | solution.py:1347

commit v6 on v5

--- a/solution.py
+++ b/solution.py
@@ -860,26 +860,32 @@
     return shapes
 
 
+(
+    D0, D1, D2, D3, U0, U1, U2, U3, PJ, Q0, Q1, Q2, Q3, GIVE, OUT, HOP,
+) = range(16)
+(
+    F2, F3, F4, F5, F6, F7, F8, F9, F10, F11, NORM_TWO, PROJ, A00, A01, A10, A11, A20, A21, A30, A31, A40, A41, A50,
+    A51, NORM_ONE, QA, MERGE, QB, QC, QD, DA, LN,
+) = range(100, 132)
+
 PLAN = (
-    "f2", ("u0", 1), "f4", ("u0", 2), "f5", ("u2", 1), ("d0", 1), ("d1", 1), "f7", ("u2", 2), "f8", ("u1", 1),
-    ("d0", 2), "f9", ("d1", 2), "f10", ("u1", 2), ("u0", 3), "f11", ("u3", 1), ("d2", 1), ("d3", 1), "norm2",
-    ("u2", 3), "proj", ("pj", 1), ("u3", 2), ("d2", 2), ("d0", 3), ("d3", 2), "a00", ("pj", 2), ("d1", 3), ("o", 0),
-    "a01", ("o", 1), "a10", ("u1", 3), ("d0", 4), ("o", 2), "a11", ("u0", 4), ("d1", 4), ("u2", 4), ("o", 3), "a20",
-    ("o", 4), "a21", ("u3", 3), ("d0", 5), ("u0", 5), ("o", 5), "a30", ("o", 6), "a31", ("d2", 3), ("d1", 5),
-    ("u2", 5), ("o", 7), "a40", ("d3", 3), "a50", ("pj", 3), ("d2", 4), ("u1", 4), "a51", ("u3", 4), "norm1",
-    ("d3", 4), "qa", ("q0", 1), ("pj", 4), "merge", ("d2", 5), "qb", ("q1", 1), ("u1", 5), ("q0", 2), "qc", ("q2", 1),
-    ("u3", 5), "qd", ("q3", 1), ("q1", 2), ("d3", 5), "da", ("q3", 2), ("q0", 3), ("pj", 5), "ln", ("u2", 6),
-    ("q2", 2), ("x", 0), ("u0", 6), ("d0", 6), ("d1", 6), ("x", 1), ("v", 0), ("q1", 3), ("d2", 6), ("u1", 6),
-    ("u3", 6), ("x", 2), ("v", 1), ("q2", 3), ("d3", 6), ("x", 3), ("q3", 3), ("q0", 4), ("v", 2), ("pj", 6),
-    ("q1", 4), ("q0", 5), ("v", 3), ("q2", 4), ("q1", 5), ("q3", 4), ("q2", 5), ("v", 4), ("q3", 5), ("q0", 6),
-    ("q1", 6), ("q2", 6), ("q3", 6),
+    F2, (U0, 1), F4, (U0, 2), F5, (U2, 1), (D0, 1), (D1, 1), F7, (U2, 2), F8, (U1, 1), (D0, 2), F9, (D1, 2), F10,
+    (U1, 2), (U0, 3), F11, (U3, 1), (D2, 1), (D3, 1), NORM_TWO, (U2, 3), PROJ, (PJ, 1), (U3, 2), (D2, 2), (D0, 3),
+    (D3, 2), A00, (PJ, 2), (D1, 3), (OUT, 0), A01, (OUT, 1), A10, (U1, 3), (D0, 4), (OUT, 2), A11, (U0, 4), (D1, 4),
+    (U2, 4), (OUT, 3), A20, (OUT, 4), A21, (U3, 3), (D0, 5), (U0, 5), (OUT, 5), A30, (OUT, 6), A31, (D2, 3), (D1, 5),
+    (U2, 5), (OUT, 7), A40, (D3, 3), A50, (PJ, 3), (D2, 4), (U1, 4), A51, (U3, 4), NORM_ONE, (D3, 4), QA, (Q0, 1),
+    (PJ, 4), MERGE, (D2, 5), QB, (Q1, 1), (U1, 5), (Q0, 2), QC, (Q2, 1), (U3, 5), QD, (Q3, 1), (Q1, 2), (D3, 5), DA,
+    (Q3, 2), (Q0, 3), (PJ, 5), LN, (U2, 6), (Q2, 2), (GIVE, 0), (U0, 6), (D0, 6), (D1, 6), (GIVE, 1), (HOP, 0),
+    (Q1, 3), (D2, 6), (U1, 6), (U3, 6), (GIVE, 2), (HOP, 1), (Q2, 3), (D3, 6), (GIVE, 3), (Q3, 3), (Q0, 4), (HOP, 2),
+    (PJ, 6), (Q1, 4), (Q0, 5), (HOP, 3), (Q2, 4), (Q1, 5), (Q3, 4), (Q2, 5), (HOP, 4), (Q3, 5), (Q0, 6), (Q1, 6),
+    (Q2, 6), (Q3, 6),
 )
 
 
 def part_actions(plan):
     parts, now = {}, None
     for item in plan:
-        if isinstance(item, str):
+        if isinstance(item, int):
             now = parts.setdefault(item, [])
         else:
             now.append(item)
@@ -966,18 +972,16 @@
     for k, (name, R, step, c0, cn, zlist, oc) in enumerate(reduce_shapes(width, ff)):
         grad, out = grads[name]
         chunks.append(Reduce(grad, R, step, c0, cn, zlist, bufs[5 * k:5 * k + 5], out, oc, e.rsem, k, where, KINDS_BACK[k], k in TURNED_BACK))
-    names_of = ("d0", "d1", "d2", "d3", "u0", "u1", "u2", "u3", "pj", "q0", "q1", "q2", "q3")
-    by_name = dict(zip(names_of, chunks))
     parts = part_actions(PLAN)
 
     def after(part):
         for name, k in parts.get(part, ()):
-            if name in by_name:
-                ch = by_name[name]
+            if name < len(chunks):
+                ch = chunks[name]
                 (ch.start, ch.tick2, ch.tick3, ch.tick4, ch.tick5, ch.tick6)[k - 1]()
-            elif name == "x":
+            elif name == GIVE:
                 give(k)
-            elif name == "o":
+            elif name == OUT:
                 send_out(k)
             else:
                 land(k)
@@ -1019,10 +1023,10 @@
         e.gu[cut, :] = dot_tn(du, e.a2[...]).astype(BF)
         e.d2[...] += dot_nn(du, e.wu_t[slot])
         for k in range(2, ff_tiles) if acting else ():
-            if f"f{k}" in parts:
+            if F2 + k - 2 in parts:
                 @pl.when(idx == k)
                 def _(k=k):
-                    after(f"f{k}")
+                    after(F2 + k - 2)
 
         return carry
 
@@ -1057,7 +1061,7 @@
 
     sum_g2, sum_c2, sum_bp = lax.fori_loop(0, rows // lrows, norm_two, (blank, blank, blank))
 
-    after("norm2")
+    after(NORM_TWO)
 
     loads["wp"].wait()
     loads["at"].wait()
@@ -1069,7 +1073,7 @@
         return carry
 
     lax.fori_loop(0, steps, proj_back, 0)
-    after("proj")
+    after(PROJ)
 
     for name in ("qs", "ka", "va", "lse"):
         loads[name].wait()
@@ -1118,10 +1122,10 @@
             dq = keys(quarter, dq, True)
             e.dm[own, lanes] = (jnp.concatenate(dq, axis=0).T * HEAD_DIM ** -0.5).astype(BF)
             for k in range(pairs):
-                if f"a{k}{i}" in parts:
+                if A00 + 2 * k + i in parts:
                     @pl.when(p == k)
                     def _(k=k, i=i):
-                        after(f"a{k}{i}")
+                        after(A00 + 2 * k + i)
 
         for i in range(2):
             own = slice(i * qrows, (i + 1) * qrows)
@@ -1150,7 +1154,7 @@
         return carry
 
     lax.fori_loop(0, rows // lrows, norm_one, 0)
-    after("norm1")
+    after(NORM_ONE)
 
     def qkv_grad(n, carry):
         cut = pl.ds(mult(n * tile, tile), tile)
@@ -1158,7 +1162,7 @@
         return carry
 
     lax.fori_loop(0, 3, qkv_grad, 0)
-    after("qa")
+    after(QA)
     wait_bytes(e.rk, e.msem.at[3])
     wait_bytes(e.rv, e.msem.at[5])
     for part, (mine, got) in enumerate(((e.own_k, e.rk), (e.own_v, e.rv))):
@@ -1170,8 +1174,8 @@
             return carry
 
         lax.fori_loop(0, rows // lrows, merge, 0)
-    after("merge")
-    for name, first, stop in (("qb", 3, 5), ("qc", 5, 7), ("qd", 7, 9)):
+    after(MERGE)
+    for name, first, stop in ((QB, 3, 5), (QC, 5, 7), (QD, 7, 9)):
         lax.fori_loop(first, stop, qkv_grad, 0)
         after(name)
     loads["wq"].wait()
@@ -1182,7 +1186,7 @@
         return carry
 
     lax.fori_loop(0, steps, input_back, 0)
-    after("da")
+    after(DA)
 
     def norm_one_back(k, sums):
         at_rows = pl.ds(mult(k * lrows, lrows), lrows)
@@ -1242,7 +1246,7 @@
     def give(k):
         lax.fori_loop(k * share, (k + 1) * share, give_back, 0)
 
-    after("ln")
+    after(LN)
     own = width // (Z * Y * C)
     e.osum[0:6, :] = pltpu.roll(e.vs[5, 0:6, :], (width - d * own) % width, 1)[:, :tile]
     long = ff // (Z * Y * C)

time: 204 us -> 204 us (level)
  no operation moved by 1% of the time
where the time goes in v6:
time: 204 us
  Pallas kernels  203 us (100%)
    pallas_call x1, Pallas kernels, backward(): pl.pallas_call(backward_kernel, out_shape=outs, in_specs=[smem, smem] + [...  106 us
    pallas_call x1, Pallas kernels, forward(): pl.pallas_call(forward_kernel, out_shape=outs, in_specs=[smem, smem] + [a...  94 us

profile of v6, /device:TPU:0, one launch (start us, length us, event | category | flops | bytes accessed | tf_op | source)
XLA Modules:
  0.0 204.0 jit_solution(12749264271347858501)
XLA Ops:
  0.6 94.0 %forward.1 = (bf16[2304,768]{1,0:T(8,128)(2,1)}, bf16[768,768]{1,0:T(8,128)(2,1)}, bf16[3072,768]{1,0:T(8,128)(2,1)}, bf16[768,3072]{1,0:T(8,128)(2,1)}, bf16[51...) custom-call(s32[16]{0:T(128)} %refs_0_.1, ...), custom_call_target="tpu_custom_call" | custom-call | tf_op jit(solution)/shard_map/forward/pallas_call | solution.py:630
  94.7 106.0 %backward.1 = (f32[144,384]{1,0:T(8,128)}, f32[48,384]{1,0:T(8,128)}, f32[192,384]{1,0:T(8,128)}, f32[48,1536]{1,0:T(8,128)}, f32[8,256]{1,0:T(8,128)}, /*index=...) custom-call(s32[16]{0:T(128)} %refs_0_.1, s32[16]{0:T(128)} %deal_ref.3, bf16[2304,768]{1,0:T(8,128)(2,1)} %get-tuple-element.50.refs_2_, ...), custom_call_target="tpu_custom_call" | custom-call | tf_op jit(solution)/shard_map/backward/pallas_call | solution.py:1322
  200.7 3.2 %finish.1 = (bf16[16,32,768]{2,1,0:T(8,128)(2,1)}, bf16[512,768]{1,0:T(8,128)(2,1)}, f32[144,384]{1,0:T(8,128)}, f32[48,384]{1,0:T(8,128)}, f32[192,384]{1,0:T(8...) custom-call(s32[16]{0:T(128)} %deal_ref.3, ...), custom_call_target="tpu_custom_call" | custom-call | tf_op jit(solution)/shard_map/finish/pallas_call | solution.py:1351

commit v7 on v6

--- a/solution.py
+++ b/solution.py
@@ -845,7 +845,7 @@
 
 
 TURNED_BACK = ()
-KINDS_BACK = (2,) * 4 + (1,) * 9
+KINDS_BACK = (2, 2, 2, 1) + (1,) * 9
 
 
 def reduce_shapes(width, ff):

time: 204 us -> 204 us (level); the launches traced: 204 us -> 201 us
  Pallas kernels: 203 us -> 200 us
    pallas_call x1, Pallas kernels: 106 us -> 103 us  [backward(): pl.pallas_call(backward_kernel, out_shape=outs, in_specs=[smem, smem] + [...]
where the time goes in v7:
time: 204 us; the launch traced here: 201 us
  Pallas kernels  200 us (98%)
    pallas_call x1, Pallas kernels, backward(): pl.pallas_call(backward_kernel, out_shape=outs, in_specs=[smem, smem] + [...  103 us
    pallas_call x1, Pallas kernels, forward(): pl.pallas_call(forward_kernel, out_shape=outs, in_specs=[smem, smem] + [a...  94 us

profile of v7, /device:TPU:0, one launch (start us, length us, event | category | flops | bytes accessed | tf_op | source)
XLA Modules:
  0.0 200.7 jit_solution(1424046981905893159)
XLA Ops:
  0.6 94.0 %forward.1 = (bf16[2304,768]{1,0:T(8,128)(2,1)}, bf16[768,768]{1,0:T(8,128)(2,1)}, bf16[3072,768]{1,0:T(8,128)(2,1)}, bf16[768,3072]{1,0:T(8,128)(2,1)}, bf16[51...) custom-call(s32[16]{0:T(128)} %refs_0_.1, ...), custom_call_target="tpu_custom_call" | custom-call | tf_op jit(solution)/shard_map/forward/pallas_call | solution.py:630
  94.7 102.7 %backward.1 = (f32[144,384]{1,0:T(8,128)}, f32[48,384]{1,0:T(8,128)}, f32[192,384]{1,0:T(8,128)}, f32[48,1536]{1,0:T(8,128)}, f32[8,256]{1,0:T(8,128)}, /*index=...) custom-call(s32[16]{0:T(128)} %refs_0_.1, s32[16]{0:T(128)} %deal_ref.3, bf16[2304,768]{1,0:T(8,128)(2,1)} %get-tuple-element.50.refs_2_, ...), custom_call_target="tpu_custom_call" | custom-call | tf_op jit(solution)/shard_map/backward/pallas_call | solution.py:1322
  197.4 3.2 %finish.1 = (bf16[16,32,768]{2,1,0:T(8,128)(2,1)}, bf16[512,768]{1,0:T(8,128)(2,1)}, f32[144,384]{1,0:T(8,128)}, f32[48,384]{1,0:T(8,128)}, f32[192,384]{1,0:T(8...) custom-call(s32[16]{0:T(128)} %deal_ref.3, ...), custom_call_target="tpu_custom_call" | custom-call | tf_op jit(solution)/shard_map/finish/pallas_call | solution.py:1351
